TPU v7x, 16 devices: a whole 2x2x2 slice. The times are simulated.
16 devices in a mesh: tp: 2 (over z), ep: 8 (over y, x, core).
Axes of the slice: x: 2, y: 2, z: 2, core: 2. Of those that a mesh axis runs over, the one named last changes fastest.
Arguments:
- tokens: bfloat16 [6144, 1280], P(('ep', 'tp'))
- grad_y: bfloat16 [6144, 1280], P(('ep', 'tp'))
- expert_ids: int32 [6144, 6], P(('ep', 'tp'))
- gate_vals: float32 [6144, 6], P(('ep', 'tp'))
- slot_ids: int32 [6144, 6], P(('ep', 'tp'))
- shared_w1: bfloat16 [1280, 1792], P(None, 'tp')
- shared_w3: bfloat16 [1280, 1792], P(None, 'tp')
- shared_w2: bfloat16 [1792, 1280], P('tp')
- expert_w1: bfloat16 [64, 1280, 896], P('ep')
- expert_w3: bfloat16 [64, 1280, 896], P('ep')
- expert_w2: bfloat16 [64, 896, 1280], P('ep')
Outputs:
- output 1: bfloat16 [6144, 1280], P(('ep', 'tp'))
- output 2: bfloat16 [6144, 1280], P(('ep', 'tp'))
- output 3: bfloat16 [1280, 1792], P(None, 'tp')
- output 4: bfloat16 [1280, 1792], P(None, 'tp')
- output 5: bfloat16 [1792, 1280], P('tp')
- output 6: bfloat16 [64, 1280, 896], P('ep', 'tp')
- output 7: bfloat16 [64, 1280, 896], P('ep', 'tp')
- output 8: bfloat16 [64, 896, 1280], P('ep', 'tp')
All inputs are finite; a program needn't handle non-finite values.
Results may differ from a plain program's by a relative error of at most 0.00108.
Values are sent between devices in bfloat16 or wider.
A program may use at most 1 GiB of HBM per device.

v0:
```python
import jax
import jax.numpy as jnp
from jax import lax
from jax.sharding import PartitionSpec as P


def gate_fn(proj_one, proj_three):
    return jax.nn.silu(proj_one) * proj_three


def dispatch_tables(expert_ids, slot_ids, buffer_rows, capacity):
    copy_count = expert_ids.shape[0] * expert_ids.shape[1]
    flat_pos = jnp.where(slot_ids >= 0, expert_ids * capacity + slot_ids, buffer_rows).reshape(-1)
    copy_of_row = jnp.full((buffer_rows,), copy_count, jnp.int32).at[flat_pos].set(
        jnp.arange(copy_count, dtype=jnp.int32), mode="drop")
    return flat_pos, copy_of_row


def solution(mesh):
    ep_size = mesh.shape["ep"]
    row_spec = P(("ep", "tp"), None)
    expert_spec = P("ep", None, None)
    expert_grad_spec = P("ep", "tp", None)

    def device_fn(tokens, grad_y, expert_ids, gate_vals, slot_ids,
                  shared_w1, shared_w3, shared_w2, expert_w1, expert_w3, expert_w2):
        rows_dev, model_dim = tokens.shape
        top_k = expert_ids.shape[1]
        experts = expert_w1.shape[0] * ep_size
        capacity = (2 * rows_dev * top_k + experts - 1) // experts
        buffer_rows = experts * capacity
        flat_pos, copy_of_row = dispatch_tables(expert_ids, slot_ids, buffer_rows, capacity)
        token_of_row = copy_of_row // top_k
        row_gate = jnp.take(gate_vals.reshape(-1), copy_of_row, axis=0, mode="fill", fill_value=0)

        tokens_all = lax.all_gather(tokens, "tp", axis=0, tiled=True)
        shared_one = jnp.dot(tokens_all, shared_w1, preferred_element_type=jnp.float32)
        shared_three = jnp.dot(tokens_all, shared_w3, preferred_element_type=jnp.float32)
        shared_gate, shared_vjp = jax.vjp(gate_fn, shared_one, shared_three)
        shared_hidden = shared_gate.astype(jnp.bfloat16)
        shared_part = jnp.dot(shared_hidden, shared_w2, preferred_element_type=jnp.float32)
        shared_out = lax.psum_scatter(shared_part, "tp", scatter_dimension=0, tiled=True)

        send_x = jnp.take(tokens, token_of_row, axis=0, mode="fill", fill_value=0)
        recv_x = lax.all_to_all(send_x.reshape(experts, capacity, model_dim), "ep", 0, 1, tiled=True)
        routed_one = jnp.einsum("lrd,ldf->lrf", recv_x, expert_w1, preferred_element_type=jnp.float32)
        routed_three = jnp.einsum("lrd,ldf->lrf", recv_x, expert_w3, preferred_element_type=jnp.float32)
        routed_gate, routed_vjp = jax.vjp(gate_fn, routed_one, routed_three)
        routed_hidden = routed_gate.astype(jnp.bfloat16)
        routed_out = jnp.einsum("lrf,lfd->lrd", routed_hidden, expert_w2,
                                preferred_element_type=jnp.float32).astype(jnp.bfloat16)
        back_out = lax.all_to_all(routed_out, "ep", 1, 0, tiled=True).reshape(buffer_rows, model_dim)
        copy_out = jnp.take(back_out, flat_pos, axis=0, mode="fill", fill_value=0).reshape(rows_dev, top_k, model_dim)
        routed_sum = jnp.sum(gate_vals[:, :, None] * copy_out.astype(jnp.float32), axis=1)
        out_y = (tokens.astype(jnp.float32) + shared_out + routed_sum).astype(jnp.bfloat16)

        send_dy = (row_gate[:, None] * jnp.take(grad_y, token_of_row, axis=0, mode="fill", fill_value=0)
                   .astype(jnp.float32)).astype(jnp.bfloat16)
        recv_dy = lax.all_to_all(send_dy.reshape(experts, capacity, model_dim), "ep", 0, 1, tiled=True)
        routed_dh = jnp.einsum("lrd,lfd->lrf", recv_dy, expert_w2, preferred_element_type=jnp.float32).astype(jnp.bfloat16)
        routed_da_one, routed_da_three = routed_vjp(routed_dh.astype(jnp.float32))
        routed_da_one = routed_da_one.astype(jnp.bfloat16)
        routed_da_three = routed_da_three.astype(jnp.bfloat16)
        routed_dx = (jnp.einsum("lrf,ldf->lrd", routed_da_one, expert_w1, preferred_element_type=jnp.float32)
                     + jnp.einsum("lrf,ldf->lrd", routed_da_three, expert_w3, preferred_element_type=jnp.float32))
        routed_dx = routed_dx.astype(jnp.bfloat16)
        part_one = jnp.einsum("lrd,lrf->ldf", recv_x, routed_da_one, preferred_element_type=jnp.float32)
        part_three = jnp.einsum("lrd,lrf->ldf", recv_x, routed_da_three, preferred_element_type=jnp.float32)
        part_two = jnp.einsum("lrf,lrd->lfd", routed_hidden, recv_dy, preferred_element_type=jnp.float32)
        back_dx = lax.all_to_all(routed_dx, "ep", 1, 0, tiled=True).reshape(buffer_rows, model_dim)
        copy_dx = jnp.take(back_dx, flat_pos, axis=0, mode="fill", fill_value=0).reshape(rows_dev, top_k, model_dim)
        routed_dx_sum = jnp.sum(copy_dx.astype(jnp.float32), axis=1)
        expert_grad_one = lax.psum_scatter(part_one, "tp", scatter_dimension=1, tiled=True).astype(jnp.bfloat16)
        expert_grad_three = lax.psum_scatter(part_three, "tp", scatter_dimension=1, tiled=True).astype(jnp.bfloat16)
        expert_grad_two = lax.psum_scatter(part_two, "tp", scatter_dimension=1, tiled=True).astype(jnp.bfloat16)

        grad_y_all = lax.all_gather(grad_y, "tp", axis=0, tiled=True)
        shared_dh = jnp.einsum("td,fd->tf", grad_y_all, shared_w2, preferred_element_type=jnp.float32).astype(jnp.bfloat16)
        shared_da_one, shared_da_three = shared_vjp(shared_dh.astype(jnp.float32))
        shared_da_one = shared_da_one.astype(jnp.bfloat16)
        shared_da_three = shared_da_three.astype(jnp.bfloat16)
        shared_dx_part = (jnp.einsum("tf,df->td", shared_da_one, shared_w1, preferred_element_type=jnp.float32)
                          + jnp.einsum("tf,df->td", shared_da_three, shared_w3, preferred_element_type=jnp.float32))
        shared_dx = lax.psum_scatter(shared_dx_part, "tp", scatter_dimension=0, tiled=True)
        shared_grad_one = lax.psum(jnp.einsum("td,tf->df", tokens_all, shared_da_one,
                                              preferred_element_type=jnp.float32), "ep").astype(jnp.bfloat16)
        shared_grad_three = lax.psum(jnp.einsum("td,tf->df", tokens_all, shared_da_three,
                                                preferred_element_type=jnp.float32), "ep").astype(jnp.bfloat16)
        shared_grad_two = lax.psum(jnp.einsum("tf,td->fd", shared_hidden, grad_y_all,
                                              preferred_element_type=jnp.float32), "ep").astype(jnp.bfloat16)
        grad_tokens = (grad_y.astype(jnp.float32) + shared_dx + routed_dx_sum).astype(jnp.bfloat16)
        return (out_y, grad_tokens, shared_grad_one, shared_grad_three, shared_grad_two,
                expert_grad_one, expert_grad_three, expert_grad_two)

    return jax.shard_map(
        device_fn, mesh=mesh,
        in_specs=(row_spec, row_spec, row_spec, row_spec, row_spec,
                  P(None, "tp"), P(None, "tp"), P("tp", None), expert_spec, expert_spec, expert_spec),
        out_specs=(row_spec, row_spec, P(None, "tp"), P(None, "tp"), P("tp", None),
                   expert_grad_spec, expert_grad_spec, expert_grad_spec),
        check_vma=False)
```

profile of v0, /device:TPU:0, one launch (start us, length us, event | category | flops | bytes accessed | tf_op | source)
XLA Modules:
  0.0 1692.8 jit_solution(2295565497172403811)
XLA Ops:
  8.4 9.0 scatter_custom_fusion
  19.2 24.1 %gather_fusion = f32[4608]{0:T(1024)S(1)} fusion(f32[2304]{0:T(1024)S(1)} %reshape.94, s32[5120]{0:T(1024)S(1)} %pad_clamp_fusion), kind=kCustom, calls=%fused_computation.4 | custom fusion | bytes 55296 | tf_op jit(solution)/shard_map/jit(_take)/gather | solution.py:34
  43.3 15.7 gather_fusion.3
  59.0 11.3 multiply_convert_fusion
  70.3 5.6 all-to-all-start.2
  77.4 15.7 gather_fusion.1
  93.0 10.8 broadcast_select_fusion
  103.8 7.0 all-gather.3.cloned.1.call-done
  110.8 6.0 fusion.19
  116.8 90.4 %all-to-all-done.2 = bf16[64,72,1280]{2,1,0:T(8,128)(2,1)} async-done(((bf16[64,72,1280]{2,1,0:T(8,128)(2,1)}), bf16[64,72,1280]{2,1,0:T(8,128)(2,1)}, u32[]{:S(2)}, u32[]{:S(2)}) %all-to-all-start.2) | async-done | bytes 11796512 | tf_op jit(solution)/shard_map/all_to_all | solution.py:59
  207.2 5.3 all-to-all-start
  213.1 4.6 convolution_convert_fusion.2
  217.8 4.3 fusion.8
  225.2 4.6 convolution_add_fusion
  229.9 5.4 fusion.20
  235.6 10.0 copy.41
  245.6 97.4 %all-to-all-done = bf16[64,72,1280]{2,1,0:T(8,128)(2,1)} async-done(((bf16[64,72,1280]{2,1,0:T(8,128)(2,1)}), bf16[64,72,1280]{2,1,0:T(8,128)(2,1)}, u32[]{:S(2)}, u32[]{:S(2)}) %all-to-all-start) | async-done | bytes 11796512 | tf_op jit(solution)/shard_map/all_to_all | solution.py:45
  343.0 10.0 copy.37
  353.0 21.6 %convolution_convert_fusion.1 = bf16[8,576,896]{2,1,0:T(8,128)(2,1)} fusion(bf16[8,576,1280]{2,1,0:T(8,128)(2,1)} %bitcast.62, bf16[8,896,1280]{2,1,0:T(8,128)(2,1)} %param.25), kind=kOutput, calls=%fused_computation.21 | convolution fusion | flops 10573774848 | bytes 38404096 | tf_op jit(solution)/shard_map/lrd,lfd->lrf/dot_general | solution.py:60
  374.6 23.8 %fusion.21 = f32[8,576,896]{2,1,0:T(8,128)} fusion(bf16[8,576,1280]{2,1,0:T(8,128)(2,1)} %bitcast.58, bf16[8,1280,896]{2,1,0:T(8,128)(2,1)} %param.24), kind=kOutput, calls=%fused_computation.61 | convolution fusion | flops 10569646080 | bytes 46661632 | tf_op jit(solution)/shard_map/lrd,ldf->lrf/dot_general | solution.py:47
  398.4 34.7 %fusion.3 = (bf16[8,576,896]{2,1,0:T(8,128)(2,1)}, bf16[8,576,896]{2,1,0:T(8,128)(2,1)}, f32[8,576,896]{2,1,0:T(8,128)}) fusion(f32[8,576,896]{2,1,0:T(8,128)} %fusion.21, bf16[8,576,896]{2,1,0:T(8,128)(2,1)} %convolution_convert_fusion.1, bf16[8,576,1280]{2,1,0:T(8,128)(2,1)} %bitcast.59, bf16[8,1280,896]{2,1,0:T(8,128)(2,1)} %param.23), kind=kOutput, calls=%fused_computation.14 | convolution fusion | flops 10631577600 | bytes 87949312 | tf_op jit(solution)/shard_map/lrd,ldf->lrf/dot_general | solution.py:46
  433.0 34.2 %fusion.16 = f32[8,1280,896]{2,1,0:T(8,128)} fusion(bf16[8,576,1280]{2,1,0:T(8,128)(2,1)} %bitcast.60, bf16[8,576,896]{2,1,0:T(8,128)(2,1)} %convolution_convert_fusion.1, f32[8,576,896]{2,1,0:T(8,128)} %get-tuple-element.45), kind=kOutput, calls=%fused_computation.58 | convolution fusion | flops 10598547456 | bytes 73269248 | tf_op jit(solution)/shard_map/lrd,lrf->ldf/dot_general | solution.py:68
  467.3 24.4 %fusion.26 = f32[8,896,1280]{2,1,0:T(8,128)} fusion(bf16[8,576,896]{2,1,0:T(8,128)(2,1)} %get-tuple-element.40, bf16[8,576,1280]{2,1,0:T(8,128)(2,1)} %bitcast.63), kind=kOutput, calls=%fused_computation.66 | convolution fusion | flops 10569646080 | bytes 56754176 | tf_op jit(solution)/shard_map/lrf,lrd->lfd/dot_general | solution.py:69
  491.8 27.7 %fusion.25 = f32[8,1280,896]{2,1,0:T(8,128)} fusion(bf16[8,576,1280]{2,1,0:T(8,128)(2,1)} %bitcast.61, bf16[8,576,896]{2,1,0:T(8,128)(2,1)} %get-tuple-element.39), kind=kOutput, calls=%fused_computation.65 | convolution fusion | flops 10569646080 | bytes 56754176 | tf_op jit(solution)/shard_map/lrd,lrf->ldf/dot_general | solution.py:67
  519.5 25.2 %fusion.23 = f32[8,576,1280]{2,1,0:T(8,128)} fusion(bf16[8,576,896]{2,1,0:T(8,128)(2,1)} %get-tuple-element.39, bf16[8,1280,896]{2,1,0:T(8,128)(2,1)} %param.23), kind=kOutput, calls=%fused_computation.63 | convolution fusion | flops 10569646080 | bytes 50200576 | tf_op jit(solution)/shard_map/lrf,ldf->lrd/dot_general | solution.py:64
  544.7 28.1 %add_convert_fusion = bf16[8,576,1280]{2,1,0:T(8,128)(2,1)} fusion(f32[8,576,1280]{2,1,0:T(8,128)} %fusion.23, bf16[8,1280,896]{2,1,0:T(8,128)(2,1)} %param.24, bf16[8,576,896]{2,1,0:T(8,128)(2,1)} %convolution_convert_fusion.1, f32[8,576,896]{2,1,0:T(8,128)} %get-tuple-element.45), kind=kOutput, calls=%fused_computation.7 | convolution fusion | flops 10610343936 | bytes 78512128 | tf_op jit(solution)/shard_map/lrf,ldf->lrd/dot_general | solution.py:65
  572.8 26.2 %copy.42 = bf16[8,576,1280]{2,0,1:T(8,128)(2,1)} copy(bf16[8,576,1280]{2,1,0:T(8,128)(2,1)} %add_convert_fusion) | data formatting | bytes 23592960 | tf_op jit(solution)/shard_map/convert_element_type | solution.py:66
  599.1 5.4 all-to-all-start.3
  604.5 22.6 %convolution_convert_fusion = bf16[8,576,1280]{2,1,0:T(8,128)(2,1)} fusion(bf16[8,576,896]{2,1,0:T(8,128)(2,1)} %get-tuple-element.40, bf16[8,896,1280]{2,1,0:T(8,128)(2,1)} %param.25), kind=kOutput, calls=%fused_computation.19 | convolution fusion | flops 10575544320 | bytes 38404096 | tf_op jit(solution)/shard_map/lrf,lfd->lrd/dot_general | solution.py:50
  627.1 26.2 %copy.38 = bf16[8,576,1280]{2,0,1:T(8,128)(2,1)} copy(bf16[8,576,1280]{2,1,0:T(8,128)(2,1)} %convolution_convert_fusion) | data formatting | bytes 23592960 | tf_op jit(solution)/shard_map/convert_element_type | solution.py:51
  653.3 81.7 %all-to-all-done.3 = bf16[8,576,1280]{2,0,1:T(8,128)(2,1)} async-done(((bf16[8,576,1280]{2,0,1:T(8,128)(2,1)}), bf16[8,576,1280]{2,0,1:T(8,128)(2,1)}, u32[]{:S(2)}, u32[]{:S(2)}) %all-to-all-start.3) | async-done | bytes 11796512 | tf_op jit(solution)/shard_map/all_to_all | solution.py:70
  735.0 5.5 all-to-all-start.1
  740.7 6.6 convolution_bitcast_fusion
  755.6 376.5 %all-reduce.2 = (bf16[1280,896]{0,1:T(8,128)(2,1)}, bf16[1280,896]{0,1:T(8,128)(2,1)S(1)}, bf16[896,1280]{1,0:T(8,128)(2,1)}) all-reduce(f32[1280,896]{0,1:T(8,128)} %convolution_bitcast_fusion.1, f32[1280,896]{0,1:T(8,128)} %convolution_bitcast_fusion, f32[896,1280]{1,0:T(8,128)} %fusion.24), channel_id=1, replica_groups=mesh['tp'=2,'ep'=8] {'ep'}, use_global_device_ids=true, to_apply=%region_5.8 | all-reduce | flops 3440640 | bytes 20643840 | tf_op jit(solution)/shard_map/psum | solution.py:85
  1132.1 4.3 copy.44
  1139.6 11.9 copy.43
  1151.5 11.9 copy.39
  1163.5 18.7 %gather_fusion.4 = bf16[2304,1280]{1,0:T(8,128)(2,1)} fusion(bf16[4608,1280]{1,0:T(8,128)(2,1)} %bitcast.54, s32[3072]{0:T(1024)S(1)} %pad_clamp_fusion.2), kind=kCustom, calls=%fused_computation.3.clone | custom fusion | bytes 11805696 | tf_op jit(solution)/shard_map/jit(_take)/gather | solution.py:71
  1182.1 18.7 %gather_fusion.2 = bf16[2304,1280]{1,0:T(8,128)(2,1)} fusion(bf16[4608,1280]{1,0:T(8,128)(2,1)} %bitcast.55, s32[3072]{0:T(1024)S(1)} %pad_clamp_fusion.2), kind=kCustom, calls=%fused_computation.1.clone | custom fusion | bytes 11805696 | tf_op jit(solution)/shard_map/jit(_take)/gather | solution.py:53
  1200.8 12.0 select_convert_fusion
  1212.8 13.5 reshape.98
  1226.3 13.8 reshape.97
  1240.1 11.5 reduce_sum.19
  1255.0 10.1 multiply_reduce_fusion
  1268.4 11.2 convert_element_type.110
  1279.6 11.2 convert_element_type.111
  1290.8 383.4 %reduce-scatter.10.cloned.1.call-done = f32[8,640,896]{2,1,0:T(8,128)} async-done(((f32[8,1280,896]{2,1,0:T(8,128)}), f32[8,640,896]{2,1,0:T(8,128)}) %reduce-scatter.10.cloned.1.call-update) | async-done | bytes 18350096 | tf_op jit(solution)/shard_map/reduce_scatter | solution.py:73
  1674.3 11.2 convert_element_type.109
  (84 shorter events, 27.0 us)
Async XLA Ops:
  7.2 210.6 %copy-start = (bf16[1280,896]{1,0:T(8,128)(2,1)S(1)}, bf16[1280,896]{1,0:T(8,128)(2,1)}, u32[]{:S(2)}) copy-start(bf16[1280,896]{1,0:T(8,128)(2,1)} %param.20) | copy-start | bytes 6881284
  8.2 9.3 copy-start.8
  18.4 0.7 copy-start.6
  19.2 24.1 %copy-start.2 = (bf16[384,1280]{1,0:T(8,128)(2,1)S(1)}, bf16[384,1280]{1,0:T(8,128)(2,1)}, u32[]{:S(2)}) copy-start(bf16[384,1280]{1,0:T(8,128)(2,1)} %param.16) | copy-start | bytes 2949124
  70.3 7.1 copy-start.4
  70.3 136.9 %all-to-all-start.2 = ((bf16[64,72,1280]{2,1,0:T(8,128)(2,1)}), bf16[64,72,1280]{2,1,0:T(8,128)(2,1)}, u32[]{:S(2)}, u32[]{:S(2)}) async-start(bf16[64,72,1280]{2,1,0:T(8,128)(2,1)} %bitcast.57), calls=%async_computation.4 | async-start | bytes 23592960 | tf_op jit(solution)/shard_map/all_to_all | solution.py:59
  75.9 34.9 %all-gather.3.cloned.1.call-start = ((), (), s32[]{:S(2)}) async-start(), calls=%async_computation.9 | async-start | bytes 2949120 | tf_op jit(solution)/shard_map/all_gather | solution.py:36
  76.6 136.5 %all-gather.5.cloned.1.call-start = ((), (), s32[]{:S(2)}) async-start(), calls=%async_computation.11 | async-start | bytes 2949120 | tf_op jit(solution)/shard_map/all_gather | solution.py:77
  207.2 135.9 %all-to-all-start = ((bf16[64,72,1280]{2,1,0:T(8,128)(2,1)}), bf16[64,72,1280]{2,1,0:T(8,128)(2,1)}, u32[]{:S(2)}, u32[]{:S(2)}) async-start(bf16[64,72,1280]{2,1,0:T(8,128)(2,1)} %bitcast.56), calls=%async_computation.1 | async-start | bytes 23592960 | tf_op jit(solution)/shard_map/all_to_all | solution.py:45
  212.5 1039.1 %reduce-scatter.8.cloned.1.call-start = ((), (), s32[]{:S(2)}) async-start(), calls=%async_computation.12 | async-start | bytes 5898240 | tf_op jit(solution)/shard_map/reduce_scatter | solution.py:84
  213.1 4.6 copy-start.12
  213.1 4.6 copy-start.15
  217.8 6.6 copy-start.20
  222.1 2.3 copy-start.17
  222.1 2.3 copy-start.19
  222.1 3.1 copy-start.10
  225.2 4.7 copy-start.11
  229.8 1035.2 %reduce-scatter.6.cloned.1.call-start = ((), (), s32[]{:S(2)}) async-start(), calls=%async_computation.10 | async-start | bytes 5898240 | tf_op jit(solution)/shard_map/reduce_scatter | solution.py:42
  235.3 1033.1 %reduce-scatter.12.cloned.1.call-start = ((), (), s32[]{:S(2)}) async-start(), calls=%async_computation.14 | async-start | bytes 55050240 | tf_op jit(solution)/shard_map/reduce_scatter | solution.py:74
  467.3 812.3 %reduce-scatter.14.cloned.1.call-start = ((), (), s32[]{:S(2)}) async-start(), calls=%async_computation.15 | async-start | bytes 55050240 | tf_op jit(solution)/shard_map/reduce_scatter | solution.py:75
  491.8 1182.5 %reduce-scatter.10.cloned.1.call-start = ((), (), s32[]{:S(2)}) async-start(), calls=%async_computation.13 | async-start | bytes 55050240 | tf_op jit(solution)/shard_map/reduce_scatter | solution.py:73
  599.1 136.0 %all-to-all-start.3 = ((bf16[8,576,1280]{2,0,1:T(8,128)(2,1)}), bf16[8,576,1280]{2,0,1:T(8,128)(2,1)}, u32[]{:S(2)}, u32[]{:S(2)}) async-start(bf16[8,576,1280]{2,0,1:T(8,128)(2,1)} %copy.42), calls=%async_computation.5 | async-start | bytes 23592960 | tf_op jit(solution)/shard_map/all_to_all | solution.py:70
  653.3 87.2 %copy-start.9 = (s32[384,6]{1,0:T(8,128)S(1)}, s32[384,6]{1,0:T(8,128)}, u32[]{:S(2)}) copy-start(s32[384,6]{1,0:T(8,128)} %copy-done.8) | copy-start | bytes 27652
  653.3 87.4 %copy-start.13 = (bf16[768,1280]{1,0:T(8,128)(2,1)S(1)}, bf16[768,1280]{1,0:T(8,128)(2,1)}, u32[]{:S(2)}) copy-start(bf16[768,1280]{1,0:T(8,128)(2,1)} %all-gather.3.cloned.1.call-done) | copy-start | bytes 5898244
  735.0 416.5 %all-to-all-start.1 = ((bf16[8,576,1280]{2,0,1:T(8,128)(2,1)}), bf16[8,576,1280]{2,0,1:T(8,128)(2,1)}, u32[]{:S(2)}, u32[]{:S(2)}) async-start(bf16[8,576,1280]{2,0,1:T(8,128)(2,1)} %copy.38), calls=%async_computation.2 | async-start | bytes 23592960 | tf_op jit(solution)/shard_map/all_to_all | solution.py:52
  740.7 6.6 copy-start.18
  747.3 4.2 copy-start.14
  747.3 4.2 copy-start.16
  1240.1 11.5 copy-start.3
  1240.1 14.9 copy-start.7
  1255.0 10.1 copy-start.5
  1279.6 405.8 %copy-start.1 = (bf16[1280,896]{1,0:T(8,128)(2,1)S(1)}, bf16[1280,896]{1,0:T(8,128)(2,1)}, u32[]{:S(2)}) copy-start(bf16[1280,896]{1,0:T(8,128)(2,1)} %param.20) | copy-start | bytes 6881284
Sparse Core Ops, SparseCore 0:
  78.2 32.5 all-gather.2
  112.3 29.5 all-gather.4
  229.9 52.3 reduce-scatter.7
  284.4 50.0 reduce-scatter.5
  467.4 400.7 reduce-scatter.11
  870.4 400.7 reduce-scatter.13
  1273.5 400.7 reduce-scatter.9
where the time goes:
time: 1700 us; the launch traced here: 1690 us
  waiting for transfers between devices  661 us (39%)
  blocking collectives  376 us (22%)
  matrix products  284 us (17%)
  local copies, waits for them, and re-layouts  236 us (14%)
  other arithmetic  96.9 us (6%)
  starting transfers between devices  22.8 us (1%)
    reduce_scatter x1, waiting for transfers between devices, device_fn(): lax.psum_scatter(part_one, 'tp', scatter_dimension=1, tiled=True)  383 us
    psum x1, blocking collectives, device_fn(): lax.psum(jnp.einsum('td,tf->df', tokens_all, shared_da_one, preferred_ele...  376 us
    all_to_all x1, waiting for transfers between devices, device_fn(): lax.all_to_all(send_x.reshape(experts, capacity, model_dim), 'ep', 0, 1,...  97.4 us
    all_to_all x1, waiting for transfers between devices, device_fn(): lax.all_to_all(send_dy.reshape(experts, capacity, model_dim), 'ep', 0, 1,...  90.4 us
    all_to_all x1, waiting for transfers between devices, device_fn(): lax.all_to_all(routed_dx, 'ep', 1, 0, tiled=True)  81.7 us
    dot_general x1, matrix products, device_fn(): jnp.einsum('lrd,ldf->lrf', recv_x, expert_w1, preferred_element_type=jnp....  34.7 us
    dot_general x1, matrix products, device_fn(): jnp.einsum('lrd,lrf->ldf', recv_x, routed_da_three, preferred_element_typ...  34.2 us
  transfers between devices with their start and end apart: 11, of which 5 were waited for; matrix products, arithmetic and copies ran while one was open for 32% of the time, Pallas kernels for 0%

commit v1 on v0

v1 whole, which is shorter than its diff:
```python
import functools

import jax
import jax.numpy as jnp
from jax import lax
from jax.experimental import pallas as pl
from jax.experimental.pallas import tpu as pltpu
from jax.sharding import PartitionSpec as P

F32 = jnp.float32
BF16 = jnp.bfloat16
SLICE = 128
VMEM_LIMIT = 64_000_000
NT = (((1,), (1,)), ((), ()))
TN = (((0,), (0,)), ((), ()))


def dot(a, b):
    return jnp.dot(a, b, preferred_element_type=F32)


def dot_nt(a, b):
    return lax.dot_general(a, b, NT, preferred_element_type=F32)


def dot_tn(a, b):
    return lax.dot_general(a, b, TN, preferred_element_type=F32)


def swiglu_parts(one, three, grad_hidden):
    sig = jax.nn.sigmoid(one)
    silu = one * sig
    dh = grad_hidden.astype(BF16).astype(F32)
    hidden = (silu * three).astype(BF16)
    da_one = (dh * three * (sig + silu * (1.0 - sig))).astype(BF16)
    da_three = (dh * silu).astype(BF16)
    return hidden, da_one, da_three


def params(axes):
    return pltpu.CompilerParams(dimension_semantics=("arbitrary",) * axes, vmem_limit_bytes=VMEM_LIMIT)


def dispatch_kernel(local, cap, top_k, ids, x_ref, dy_ref, meta_ref, xd_ref, qd_ref):
    tokens = x_ref.shape[-2]
    rows = local * cap
    meta = meta_ref[0, 0]
    base = (ids[1] * rows).astype(F32)
    row_ids = lax.broadcasted_iota(jnp.int32, (rows, tokens), 0).astype(F32) + base
    gates = jnp.zeros((rows, tokens), F32)
    for j in range(top_k):
        gates = jnp.where(meta[j][None, :] == row_ids, meta[top_k + j][None, :], gates)
    select = jnp.where(gates != 0.0, 1.0, 0.0).astype(BF16)
    row_gate = jnp.sum(gates, axis=1, keepdims=True)
    got_x = dot(select, x_ref[0, 0])
    for l in range(local):
        xd_ref[0, l] = got_x[l * cap:(l + 1) * cap].astype(BF16)
    got_dy = dot(select, dy_ref[0, 0]) * row_gate
    for l in range(local):
        qd_ref[0, l] = got_dy[l * cap:(l + 1) * cap].astype(BF16)


def dispatch(ids, x_all, dy_all, meta_all, local, cap, top_k, layers, first):
    groups, tps, tokens, dim = x_all.shape
    row_map = lambda y, s, ids: (s, (ids[0] + y + first) % tps, 0, 0)
    out = jax.ShapeDtypeStruct((layers, local, groups * cap, dim), BF16)
    out_spec = pl.BlockSpec((1, local, cap, dim), lambda y, s, ids: (y, 0, s, 0))
    return pl.pallas_call(
        functools.partial(dispatch_kernel, local, cap, top_k),
        grid_spec=pltpu.PrefetchScalarGridSpec(
            num_scalar_prefetch=1, grid=(layers, groups),
            in_specs=[pl.BlockSpec((1, 1, tokens, dim), row_map), pl.BlockSpec((1, 1, tokens, dim), row_map),
                      pl.BlockSpec((1, 1, 2 * top_k, tokens), row_map)],
            out_specs=[out_spec, out_spec]),
        out_shape=[out, out], compiler_params=params(2), name=f"dispatch{first}",
        cost_estimate=pl.CostEstimate(flops=layers * groups * local * cap * tokens * dim * 4,
                                      bytes_accessed=layers * groups * (tokens + local * cap) * dim * 4,
                                      transcendentals=0),
    )(ids, x_all, dy_all, meta_all)


def own_kernel(cap, x_ref, q_ref, w1_ref, w3_ref, w2_ref, o_ref, dr_ref, h_ref, da1_ref, da3_ref):
    rows = x_ref.shape[-2]
    groups = rows // cap
    half = rows // 2
    per = groups // 2
    for part in range(2):
        span = slice(part * half, (part + 1) * half)
        x = x_ref[0, 0, span]
        hidden, da_one, da_three = swiglu_parts(dot(x, w1_ref[0]), dot(x, w3_ref[0]),
                                                dot_nt(q_ref[0, 0, span], w2_ref[0]))
        h_ref[0, span] = hidden
        da1_ref[0, span] = da_one
        da3_ref[0, span] = da_three
        out = dot(hidden, w2_ref[0])
        grad = dot_nt(da_one, w1_ref[0]) + dot_nt(da_three, w3_ref[0])
        for s in range(per):
            o_ref[part * per + s] = out[s * cap:(s + 1) * cap].astype(BF16)
            dr_ref[part * per + s] = grad[s * cap:(s + 1) * cap].astype(BF16)


def own_experts(xd, qd, w1, w3, w2, cap):
    _, local, rows, dim = xd.shape
    ff = w1.shape[-1]
    groups = rows // cap
    row_spec = pl.BlockSpec((1, 1, rows, dim), lambda l: (0, l, 0, 0))
    back = jax.ShapeDtypeStruct((groups, local * cap, dim), BF16)
    back_spec = pl.BlockSpec((groups, cap, dim), lambda l: (0, l, 0))
    hid = jax.ShapeDtypeStruct((local, rows, ff), BF16)
    hid_spec = pl.BlockSpec((1, rows, ff), lambda l: (l, 0, 0))
    wide = pl.BlockSpec((1, dim, ff), lambda l: (l, 0, 0))
    tall = pl.BlockSpec((1, ff, dim), lambda l: (l, 0, 0))
    return pl.pallas_call(
        functools.partial(own_kernel, cap), grid=(local,),
        in_specs=[row_spec, row_spec, wide, wide, tall],
        out_specs=[back_spec, back_spec, hid_spec, hid_spec, hid_spec],
        out_shape=[back, back, hid, hid, hid], compiler_params=params(1), name="own",
        cost_estimate=pl.CostEstimate(flops=12 * local * rows * dim * ff,
                                      bytes_accessed=local * (8 * rows * dim + 6 * rows * ff + 6 * dim * ff),
                                      transcendentals=local * rows * ff),
    )(xd, qd, w1, w3, w2)


def grads_kernel(parts, ids, x_ref, q_ref, xp_ref, qp_ref, h_ref, da1_ref, da3_ref, w1_ref, w3_ref, w2_ref,
                 g1_ref, g3_ref, g2_ref, hid, da_one, da_three, tall):
    rows = x_ref.shape[-2]
    half = rows // 2
    hid[:rows] = h_ref[0]
    da_one[:rows] = da1_ref[0]
    da_three[:rows] = da3_ref[0]
    for part in range(2):
        span = slice(part * half, (part + 1) * half)
        dest = slice(rows + part * half, rows + (part + 1) * half)
        x = xp_ref[0, 0, span]
        hidden, one, three = swiglu_parts(dot(x, w1_ref[0]), dot(x, w3_ref[0]),
                                          dot_nt(qp_ref[0, 0, span], w2_ref[0]))
        hid[dest] = hidden
        da_one[dest] = one
        da_three[dest] = three
    part = ids[0]
    width = g1_ref.shape[1]
    columns = pl.ds(pl.multiple_of(part * width, 128), width)
    own_x = x_ref[0, 0, :, columns]
    far_x = xp_ref[0, 0, :, columns]
    g1_ref[0] = (dot_tn(own_x, da_one[:rows]) + dot_tn(far_x, da_one[rows:])).astype(BF16)
    g3_ref[0] = (dot_tn(own_x, da_three[:rows]) + dot_tn(far_x, da_three[rows:])).astype(BF16)
    height = g2_ref.shape[1]
    ff = hid.shape[1]
    reach = tall.shape[0]
    chunk = pl.ds(pl.multiple_of(part * (ff - reach), 128), reach)
    tall[...] = dot_tn(hid[:rows, chunk], q_ref[0, 0]) + dot_tn(hid[rows:, chunk], qp_ref[0, 0])
    skip = pl.multiple_of(part * (height - (ff - reach)), 8)
    g2_ref[0] = tall[pl.ds(skip, height)].astype(BF16)


def expert_grads(ids, xd, qd, xp, qp, h, da1, da3, w1, w3, w2, parts):
    _, local, rows, dim = xd.shape
    ff = w1.shape[-1]
    row_spec = pl.BlockSpec((1, 1, rows, dim), lambda l, ids: (0, l, 0, 0))
    hid_spec = pl.BlockSpec((1, rows, ff), lambda l, ids: (l, 0, 0))
    wide = pl.BlockSpec((1, dim, ff), lambda l, ids: (l, 0, 0))
    tall = pl.BlockSpec((1, ff, dim), lambda l, ids: (l, 0, 0))
    g1 = jax.ShapeDtypeStruct((local, dim // parts, ff), BF16)
    g2 = jax.ShapeDtypeStruct((local, ff // parts, dim), BF16)
    g1_spec = pl.BlockSpec((1, dim // parts, ff), lambda l, ids: (l, 0, 0))
    g2_spec = pl.BlockSpec((1, ff // parts, dim), lambda l, ids: (l, 0, 0))
    reach = -(-(ff // parts) // 128) * 128
    return pl.pallas_call(
        functools.partial(grads_kernel, parts),
        grid_spec=pltpu.PrefetchScalarGridSpec(
            num_scalar_prefetch=1, grid=(local,),
            in_specs=[row_spec, row_spec, row_spec, row_spec, hid_spec, hid_spec, hid_spec, wide, wide, tall],
            out_specs=[g1_spec, g1_spec, g2_spec],
            scratch_shapes=[pltpu.VMEM((2 * rows, ff), BF16)] * 3 + [pltpu.VMEM((reach, dim), F32)]),
        out_shape=[g1, g1, g2], compiler_params=params(1), name="grads",
        cost_estimate=pl.CostEstimate(flops=12 * local * rows * dim * ff,
                                      bytes_accessed=local * (8 * rows * dim + 6 * rows * ff + 9 * dim * ff),
                                      transcendentals=local * rows * ff),
    )(ids, xd, qd, xp, qp, h, da1, da3, w1, w3, w2)


def shared_kernel(ids, x_ref, dy_ref, wa_ref, w2_ref, h_ref, da_ref, ga_ref, g2_ref, acc_a, acc_2):
    layer, source = pl.program_id(0), pl.program_id(1)

    @pl.when((layer == 0) & (source == 0))
    def _():
        acc_a[...] = jnp.zeros_like(acc_a)
        acc_2[...] = jnp.zeros_like(acc_2)

    x, dy = x_ref[0, 0], dy_ref[0, 0]
    proj = dot(x, wa_ref[...])
    dh = dot_nt(dy, w2_ref[...])
    for half in range(2):
        one = proj[:, 2 * half * SLICE:(2 * half + 1) * SLICE]
        three = proj[:, (2 * half + 1) * SLICE:(2 * half + 2) * SLICE]
        hidden, da_one, da_three = swiglu_parts(one, three, dh[:, half * SLICE:(half + 1) * SLICE])
        h_ref[0, :, half * SLICE:(half + 1) * SLICE] = hidden
        da_ref[0, :, 2 * half * SLICE:(2 * half + 1) * SLICE] = da_one
        da_ref[0, :, (2 * half + 1) * SLICE:(2 * half + 2) * SLICE] = da_three
    acc_a[...] += dot_tn(x, da_ref[0, :, :2 * SLICE])
    acc_2[...] += dot_tn(h_ref[0, :, :SLICE], dy)

    @pl.when((layer == pl.num_programs(0) - 1) & (source == pl.num_programs(1) - 1))
    def _():
        ga_ref[...] = acc_a[...].astype(BF16)
        g2_ref[...] = acc_2[...].astype(BF16)


def shared_expert(ids, x_all, dy_all, wa, w2):
    groups, tps, tokens, dim = x_all.shape
    row_map = lambda y, s, ids: (s, (ids[0] + y) % tps, 0, 0)
    own_map = lambda y, s, ids: (jnp.where(y == 0, s, groups), 0, 0)
    fixed = lambda y, s, ids: (0, 0)
    return pl.pallas_call(
        shared_kernel,
        grid_spec=pltpu.PrefetchScalarGridSpec(
            num_scalar_prefetch=1, grid=(tps, groups),
            in_specs=[pl.BlockSpec((1, 1, tokens, dim), row_map), pl.BlockSpec((1, 1, tokens, dim), row_map),
                      pl.BlockSpec(wa.shape, fixed), pl.BlockSpec(w2.shape, fixed)],
            out_specs=[pl.BlockSpec((1, tokens, 2 * SLICE), own_map), pl.BlockSpec((1, tokens, 4 * SLICE), own_map),
                       pl.BlockSpec((dim, 2 * SLICE), fixed), pl.BlockSpec((SLICE, dim), fixed)],
            scratch_shapes=[pltpu.VMEM((dim, 2 * SLICE), F32), pltpu.VMEM((SLICE, dim), F32)]),
        out_shape=[jax.ShapeDtypeStruct((groups + 1, tokens, 2 * SLICE), BF16),
                   jax.ShapeDtypeStruct((groups + 1, tokens, 4 * SLICE), BF16),
                   jax.ShapeDtypeStruct((dim, 2 * SLICE), BF16), jax.ShapeDtypeStruct((SLICE, dim), BF16)],
        compiler_params=params(2), name="shared",
        cost_estimate=pl.CostEstimate(flops=18 * groups * tps * tokens * dim * SLICE,
                                      bytes_accessed=4 * groups * tps * tokens * dim, transcendentals=0),
    )(ids, x_all, dy_all, wa, w2)


def combine_kernel(local, cap, top_k, ids, meta_ref, o_ref, dr_ref, h_ref, da_ref, wa_ref, w2_ref, y_ref, dx_ref):
    tokens = h_ref.shape[-2]
    rows = local * cap
    meta = meta_ref[0]
    base = (ids[1] * rows).astype(F32)
    row_ids = lax.broadcasted_iota(jnp.int32, (tokens, rows), 1).astype(F32) + base
    gates = jnp.zeros((tokens, rows), F32)
    for j in range(top_k):
        gates = jnp.where(meta[:, j:j + 1] == row_ids, meta[:, top_k + j:top_k + j + 1], gates)
    high = gates.astype(BF16)
    rest = gates - high.astype(F32)
    mid = rest.astype(BF16)
    low = (rest - mid.astype(F32)).astype(BF16)
    out = o_ref[0]
    y_ref[0] = dot(high, out) + dot(mid, out) + dot(low, out) + dot(h_ref[0], w2_ref[...])
    select = jnp.where(gates != 0.0, 1.0, 0.0).astype(BF16)
    dx_ref[0] = dot(select, dr_ref[0]) + dot_nt(da_ref[0], wa_ref[...])


def combine(ids, meta_own, o, dr, h, da, wa, w2, local, cap, top_k):
    groups, rows, dim = o.shape
    tokens = h.shape[1]
    by_source = lambda s, ids: (s, 0, 0)
    fixed = lambda s, ids: (0, 0)
    out = jax.ShapeDtypeStruct((groups, tokens, dim), F32)
    out_spec = pl.BlockSpec((1, tokens, dim), by_source)
    return pl.pallas_call(
        functools.partial(combine_kernel, local, cap, top_k),
        grid_spec=pltpu.PrefetchScalarGridSpec(
            num_scalar_prefetch=1, grid=(groups,),
            in_specs=[pl.BlockSpec((1, tokens, 2 * top_k), by_source), pl.BlockSpec((1, rows, dim), by_source),
                      pl.BlockSpec((1, rows, dim), by_source), pl.BlockSpec((1, tokens, 2 * SLICE), by_source),
                      pl.BlockSpec((1, tokens, 4 * SLICE), by_source), pl.BlockSpec(wa.shape, fixed),
                      pl.BlockSpec(w2.shape, fixed)],
            out_specs=[out_spec, out_spec]),
        out_shape=[out, out], compiler_params=params(1), name="combine",
        cost_estimate=pl.CostEstimate(flops=8 * groups * tokens * rows * dim,
                                      bytes_accessed=groups * (4 * rows + 8 * tokens) * dim, transcendentals=0),
    )(ids, meta_own, o, dr, h, da, wa, w2)


def solution(mesh):
    ep_size, tp_size = mesh.shape["ep"], mesh.shape["tp"]
    row_spec = P(("ep", "tp"), None)
    expert_spec = P("ep", None, None)
    expert_grad_spec = P("ep", "tp", None)
    swap = [(0, 1), (1, 0)]

    def device_fn(tokens, grad_y, expert_ids, gate_vals, slot_ids,
                  shared_w1, shared_w3, shared_w2, expert_w1, expert_w3, expert_w2):
        rows_dev, dim = tokens.shape
        top_k = expert_ids.shape[1]
        local = expert_w1.shape[0]
        experts = local * ep_size
        cap = (2 * rows_dev * top_k + experts - 1) // experts
        tp_id, ep_id = lax.axis_index("tp"), lax.axis_index("ep")
        ids = jnp.stack([tp_id, ep_id]).astype(jnp.int32)

        pos = jnp.where(slot_ids >= 0, expert_ids * cap + slot_ids, -1).astype(F32)
        meta = jnp.concatenate([pos.T, gate_vals.T], axis=0)
        meta_all = lax.all_gather(meta, ("ep", "tp")).reshape(ep_size, tp_size, 2 * top_k, rows_dev)
        x_all = lax.all_gather(tokens, ("ep", "tp"), axis=0, tiled=True).reshape(ep_size, tp_size, rows_dev, dim)
        dy_all = lax.all_gather(grad_y, ("ep", "tp"), axis=0, tiled=True).reshape(ep_size, tp_size, rows_dev, dim)

        ff = shared_w1.shape[1]
        padded = ep_size * SLICE
        wide_pad = ((0, 0), (0, padded - ff))
        start = ep_id * SLICE
        w1s = lax.dynamic_slice(jnp.pad(shared_w1, wide_pad), (0, start), (dim, SLICE))
        w3s = lax.dynamic_slice(jnp.pad(shared_w3, wide_pad), (0, start), (dim, SLICE))
        w2s = lax.dynamic_slice(jnp.pad(shared_w2, ((0, padded - ff), (0, 0))), (start, 0), (SLICE, dim))
        wa_own = jnp.concatenate([w1s, w3s], axis=1)
        wa = jnp.concatenate([wa_own, lax.ppermute(wa_own, "tp", swap)], axis=1)
        w2a = jnp.concatenate([w2s, lax.ppermute(w2s, "tp", swap)], axis=0)

        xd, qd = dispatch(ids, x_all, dy_all, meta_all, local, cap, top_k, 1, 0)
        sh, sda, sga, sg2 = shared_expert(ids, x_all, dy_all, wa, w2a)
        o, dr, h, da1, da3 = own_experts(xd, qd, expert_w1, expert_w3, expert_w2, cap)
        meta_own = lax.dynamic_index_in_dim(meta_all, tp_id, axis=1, keepdims=False).transpose(0, 2, 1)
        y_part, dx_part = combine(ids, meta_own, o, dr, sh, sda, wa, w2a, local, cap, top_k)
        y_sum = lax.psum_scatter(y_part.reshape(-1, dim), "ep", scatter_dimension=0, tiled=True)
        dx_sum = lax.psum_scatter(dx_part.reshape(-1, dim), "ep", scatter_dimension=0, tiled=True)

        xp, qp = dispatch(ids, x_all, dy_all, meta_all, local, cap, top_k, 1, 1)
        g1, g3, g2 = expert_grads(ids, xd, qd, xp, qp, h, da1, da3, expert_w1, expert_w3, expert_w2, tp_size)

        sga_all = lax.all_gather(sga, "ep")
        sg2_all = lax.all_gather(sg2, "ep")
        sg1 = sga_all[:, :, :SLICE].transpose(1, 0, 2).reshape(dim, padded)[:, :ff]
        sg3 = sga_all[:, :, SLICE:].transpose(1, 0, 2).reshape(dim, padded)[:, :ff]
        sg2 = sg2_all.reshape(padded, dim)[:ff]
        out_y = (tokens.astype(F32) + y_sum).astype(BF16)
        grad_tokens = (grad_y.astype(F32) + dx_sum).astype(BF16)
        return out_y, grad_tokens, sg1, sg3, sg2, g1, g3, g2

    return jax.shard_map(
        device_fn, mesh=mesh,
        in_specs=(row_spec, row_spec, row_spec, row_spec, row_spec,
                  P(None, "tp"), P(None, "tp"), P("tp", None), expert_spec, expert_spec, expert_spec),
        out_specs=(row_spec, row_spec, P(None, "tp"), P(None, "tp"), P("tp", None),
                   expert_grad_spec, expert_grad_spec, expert_grad_spec),
        check_vma=False)
```

time: 1700 us -> 598 us (0.35)
  waiting for transfers between devices: 661 us -> 224 us
  blocking collectives: 376 us -> 25.9 us
  Pallas kernels: 0 us -> 308 us
  matrix products: 284 us -> 0 us
  local copies, waits for them, and re-layouts: 236 us -> 14 us
  other arithmetic: 96.9 us -> 8.17 us
  starting transfers between devices: 22.8 us -> 3.98 us
    psum x1 -> x0, blocking collectives: 376 us -> none  [device_fn(): lax.psum(jnp.einsum('td,tf->df', tokens_all, shared_da_one, preferred_ele...]
    reduce_scatter x5 -> x2, waiting for transfers between devices: 383 us -> 69.9 us  [the longest x1 69.9 us: device_fn(): lax.psum_scatter(y_part.reshape(-1, dim), 'ep', scatter_dimension=0, tile...]
    pallas_call x0 -> x6, Pallas kernels: none -> 308 us  [the longest x1 98.3 us: expert_grads(): pl.pallas_call(functools.partial(grads_kernel, parts), grid_spec=pltpu.Pr...]
    dot_general x18 -> x0, matrix products: 284 us -> none  [the longest x1 34.7 us: device_fn(): jnp.einsum('lrd,ldf->lrf', recv_x, expert_w1, preferred_element_type=jnp....]
    all_to_all x4 -> x0, waiting for transfers between devices: 270 us -> none  [the longest x1 97.4 us: device_fn(): lax.all_to_all(send_x.reshape(experts, capacity, model_dim), 'ep', 0, 1,...]
    all_gather x2 -> x4, waiting for transfers between devices: 7.04 us -> 122 us  [the longest x1 74.8 us: device_fn(): lax.all_gather(grad_y, ('ep', 'tp'), axis=0, tiled=True)]
    gather x5 -> x0, local copies, waits for them, and re-layouts: 92.7 us -> none  [the longest x1 24.1 us: device_fn(): jnp.take(gate_vals.reshape(-1), copy_of_row, axis=0, mode='fill', fill_va...]
    convert_element_type x4 -> x0, local copies, waits for them, and re-layouts: 79.7 us -> none  [the longest x1 26.2 us: device_fn(): routed_dx = routed_dx.astype(jnp.bfloat16)]
  transfers between devices with their start and end apart: 11 -> 8, of which waited for: 5 -> 4; matrix products, arithmetic and copies ran while one was open for 32% -> 3% of each run, Pallas kernels for 0% -> 45%
where the time goes in v1:
time: 598 us
  Pallas kernels  308 us (52%)
  waiting for transfers between devices  224 us (37%)
  blocking collectives  25.9 us (4%)
  between operations  14.3 us (2%)
  local copies, waits for them, and re-layouts  14 us (2%)
  other arithmetic  8.17 us (1%)
    pallas_call x1, Pallas kernels, expert_grads(): pl.pallas_call(functools.partial(grads_kernel, parts), grid_spec=pltpu.Pr...  98.3 us
    pallas_call x1, Pallas kernels, own_experts(): pl.pallas_call(functools.partial(own_kernel, cap), grid=(local,), in_spec...  82.6 us
    all_gather x1, waiting for transfers between devices, device_fn(): lax.all_gather(grad_y, ('ep', 'tp'), axis=0, tiled=True)  74.8 us
    reduce_scatter x1, waiting for transfers between devices, device_fn(): lax.psum_scatter(y_part.reshape(-1, dim), 'ep', scatter_dimension=0, tile...  69.9 us
    all_gather x1, waiting for transfers between devices, device_fn(): lax.all_gather(tokens, ('ep', 'tp'), axis=0, tiled=True)  47.6 us
    pallas_call x1, Pallas kernels, combine(): pl.pallas_call(functools.partial(combine_kernel, local, cap, top_k), grid...  45.8 us
    pallas_call x2, Pallas kernels, dispatch(): pl.pallas_call(functools.partial(dispatch_kernel, local, cap, top_k), gri...  42.1 us
    pallas_call x1, Pallas kernels, shared_expert(): pl.pallas_call(shared_kernel, grid_spec=pltpu.PrefetchScalarGridSpec(num_...  38.8 us
  transfers between devices with their start and end apart: 8, of which 4 were waited for; matrix products, arithmetic and copies ran while one was open for 3% of the time, Pallas kernels for 45%

profile of v1, /device:TPU:0, one launch (start us, length us, event | category | flops | bytes accessed | tf_op | source)
XLA Modules:
  0.0 597.6 jit_solution(802121829918966501)
XLA Ops:
  7.2 0.0 all-gather.9.cloned.1.call-start
  7.2 0.7 all-gather.9.cloned.1.call-update
  7.9 0.0 all-gather.11.cloned.1.call-start
  7.9 0.7 all-gather.11.cloned.1.call-update
  8.7 0.0 all-gather.15.cloned.1.call-start
  8.7 0.0 copy-start.2
  8.7 1.4 pad_dynamic-slice_fusion.1
  10.1 0.1 pad_maximum_fusion.1
  10.2 3.3 collective-permute-start
  13.5 0.1 pad_dynamic-slice_fusion
  13.6 0.4 collective-permute-start.1
  14.0 0.6 pad_add_fusion.ids
  14.6 28.7 %collective-permute-done.1 = bf16[128,1280]{1,0:T(8,128)(2,1)S(1)} collective-permute-done((bf16[128,1280]{1,0:T(8,128)(2,1)S(1)}, bf16[128,1280]{1,0:T(8,128)(2,1)S(1)}, u32[]{:S(2)}, u32[]{:S(2)}) %collective-permute-start.1) | collective-permute-done | bytes 327712 | tf_op jit(solution)/shard_map/ppermute | solution.py:305
  43.3 0.9 pad_maximum_fusion.2.w2_ref
  44.2 0.0 collective-permute-done
  44.2 1.2 pad_maximum_fusion.wa_ref
  45.4 47.6 %all-gather.9.cloned.1.call-done = bf16[6144,1280]{1,0:T(8,128)(2,1)} async-done(((bf16[384,1280]{1,0:T(8,128)(2,1)}), bf16[6144,1280]{1,0:T(8,128)(2,1)}) %all-gather.9.cloned.1.call-update) | async-done | bytes 15728656 | tf_op jit(solution)/shard_map/all_gather | solution.py:293
  93.0 74.8 %all-gather.11.cloned.1.call-done = bf16[6144,1280]{1,0:T(8,128)(2,1)} async-done(((bf16[384,1280]{1,0:T(8,128)(2,1)}), bf16[6144,1280]{1,0:T(8,128)(2,1)}) %all-gather.11.cloned.1.call-update) | async-done | bytes 15728656 | tf_op jit(solution)/shard_map/all_gather | solution.py:294
  167.8 38.8 %shared.1 = (bf16[9,384,256]{2,1,0:T(8,128)(2,1)}, bf16[9,384,512]{2,1,0:T(8,128)(2,1)}, bf16[1280,256]{1,0:T(8,128)(2,1)}, bf16[128,1280]{1,0:T(8,128)(2,1)}) custom-call(s32[2]{0:T(128)} %pad_add_fusion.ids, bf16[8,2,384,1280]{3,2,1,0:T(8,128)(2,1)} %bitcast.38, bf16[8,2,384,1280]{3,2,1,0:T(8,128)(2,1)} %bitcast.41, ...), custom_call_target="tpu_custom_call" | custom-call | flops 18119393280 | bytes 31457280 | tf_op jit(solution)/shard_map/shared/pallas_call | solution.py:214
  206.6 0.0 all-gather.15.cloned.1.call-update
  206.6 0.0 all-gather.13.cloned.1.call-start
  206.7 0.5 all-gather.13.cloned.1.call-update
  207.2 0.0 reduce-scatter.5.cloned.1.call-start
  207.3 0.0 copy-done.4
  207.3 0.0 copy-done.5
  207.3 25.9 %all-gather.3 = f32[16,12,384]{2,1,0:T(8,128)S(1)} all-gather(f32[1,12,384]{2,1,0:T(8,128)S(1)} %maximum_bitcast_fusion), channel_id=2, replica_groups=mesh['tp'=2,'ep'=8] {'ep','tp'}, dimensions={0}, use_global_device_ids=true | all-gather | bytes 313344 | tf_op jit(solution)/shard_map/all_gather | solution.py:292
  233.2 0.0 copy-start.3
  233.3 1.7 copy.26
  234.9 21.1 %dispatch0.1 = (bf16[1,8,576,1280]{3,2,1,0:T(8,128)(2,1)}, bf16[1,8,576,1280]{3,2,1,0:T(8,128)(2,1)}) custom-call(s32[2]{0:T(128)} %pad_add_fusion.ids, bf16[8,2,384,1280]{3,2,1,0:T(8,128)(2,1)} %bitcast.39, bf16[8,2,384,1280]{3,2,1,0:T(8,128)(2,1)} %bitcast.42, f32[8,2,12,384]{3,2,1,0:T(8,128)} %bitcast.35), custom_call_target="tpu_custom_call" | custom-call | flops 9059696640 | bytes 39321600 | tf_op jit(solution)/shard_map/dispatch0/pallas_call | solution.py:68
  256.0 82.6 %own.1 = (bf16[8,576,1280]{2,1,0:T(8,128)(2,1)}, bf16[8,576,1280]{2,1,0:T(8,128)(2,1)}, bf16[8,576,896]{2,1,0:T(8,128)(2,1)}, bf16[8,576,896]{2,1,0:T(8,128)(2,1)}, bf16[8,576,896]{2,1,0:T(8,128)(2,1)}) custom-call(bf16[1,8,576,1280]{3,2,1,0:T(8,128)(2,1)} %get-tuple-element.26.x_ref, bf16[1,8,576,1280]{3,2,1,0:T(8,128)(2,1)} %get-tuple-element.27.q_ref, ...), custom_call_target="tpu_custom_call" | custom-call | flops 63417876480 | bytes 127008768 | tf_op jit(solution)/shard_map/own/pallas_call | solution.py:113
  338.6 45.8 %combine.1 = (f32[8,384,1280]{2,1,0:T(8,128)}, f32[8,384,1280]{2,1,0:T(8,128)}) custom-call(s32[2]{0:T(128)} %pad_add_fusion.ids, f32[8,384,12]{2,1,0:T(8,128)} %bitcast.33, bf16[8,576,1280]{2,1,0:T(8,128)(2,1)} %get-tuple-element.28.o_ref, bf16[8,576,1280]{2,1,0:T(8,128)(2,1)} %get-tuple-element.29.dr_ref, bf16[9,384,256]{2,1,0:T(8,128)(2,1)} %get-tuple-element.30.h_ref, ...), custom_call_target="tpu_custom_call" | custom-call | flops 18119393280 | bytes 55050240 | tf_op jit(solution)/shard_map/combine/pallas_call | solution.py:258
  384.4 0.0 reduce-scatter.5.cloned.1.call-update
  384.4 0.0 reduce-scatter.3.cloned.1.call-start
  384.5 0.5 reduce-scatter.3.cloned.1.call-update
  385.0 21.0 %dispatch1.1 = (bf16[1,8,576,1280]{3,2,1,0:T(8,128)(2,1)}, bf16[1,8,576,1280]{3,2,1,0:T(8,128)(2,1)}) custom-call(s32[2]{0:T(128)} %pad_add_fusion.ids, bf16[8,2,384,1280]{3,2,1,0:T(8,128)(2,1)} %bitcast.40, bf16[8,2,384,1280]{3,2,1,0:T(8,128)(2,1)} %bitcast.43, f32[8,2,12,384]{3,2,1,0:T(8,128)} %bitcast.36), custom_call_target="tpu_custom_call" | custom-call | flops 9059696640 | bytes 39321600 | tf_op jit(solution)/shard_map/dispatch1/pallas_call | solution.py:68
  406.1 98.3 %grads.1 = (bf16[8,640,896]{2,1,0:T(8,128)(2,1)}, bf16[8,640,896]{2,1,0:T(8,128)(2,1)}, bf16[8,448,1280]{2,1,0:T(8,128)(2,1)}) custom-call(s32[2]{0:T(128)} %pad_add_fusion.ids, bf16[1,8,576,1280]{3,2,1,0:T(8,128)(2,1)} %get-tuple-element.26.x_ref, bf16[1,8,576,1280]{3,2,1,0:T(8,128)(2,1)} %get-tuple-element.27.q_ref, ...), custom_call_target="tpu_custom_call" | custom-call | flops 63417876480 | bytes 154533888 | tf_op jit(solution)/shard_map/grads/pallas_call | solution.py:168
  504.4 0.0 all-gather.15.cloned.1.call-done
  504.4 3.2 slice.29
  507.6 3.0 slice_bitcast_fusion
  510.6 0.7 copy.35
  511.4 1.6 slice.28
  513.0 0.7 copy.36
  513.7 0.0 copy-start
  513.7 1.6 slice.26
  515.4 2.8 add_convert_fusion
  518.1 69.9 %reduce-scatter.3.cloned.1.call-done = f32[384,1280]{1,0:T(8,128)} async-done(((f32[3072,1280]{1,0:T(8,128)}), f32[384,1280]{1,0:T(8,128)}) %reduce-scatter.3.cloned.1.call-update) | async-done | bytes 1966096 | tf_op jit(solution)/shard_map/reduce_scatter | solution.py:312
  588.1 0.0 copy-done.1
  588.1 2.7 add_convert_fusion.1
  (13 shorter events, 0.1 us)
Async XLA Ops:
  7.2 85.8 %all-gather.9.cloned.1.call-start = ((), (), s32[]{:S(2)}) async-start(), calls=%async_computation.2 | async-start | bytes 16711680 | tf_op jit(solution)/shard_map/all_gather | solution.py:293
  7.9 159.9 %all-gather.11.cloned.1.call-start = ((), (), s32[]{:S(2)}) async-start(), calls=%async_computation.3 | async-start | bytes 16711680 | tf_op jit(solution)/shard_map/all_gather | solution.py:294
  8.7 495.8 %all-gather.15.cloned.1.call-start = ((), (), s32[]{:S(2)}) async-start(), calls=%async_computation.7 | async-start | bytes 2949120 | tf_op jit(solution)/shard_map/all_gather | solution.py:319
  8.7 4.8 copy-start.2
  10.2 34.0 %collective-permute-start = (bf16[1280,256]{1,0:T(8,128)(2,1)S(1)}, bf16[1280,256]{1,0:T(8,128)(2,1)S(1)}, u32[]{:S(2)}, u32[]{:S(2)}) collective-permute-start(bf16[1280,256]{1,0:T(8,128)(2,1)S(1)} %pad_maximum_fusion.1), channel_id=1, source_target_pairs={{0,8},{8,0},{1,9},{9,1},{2,10},{10,2},{3,11},{11,3},{4,12},{12,4},... | collective-permute-start | bytes 1966088 | tf_op jit(solution)/shard_map/ppermute | solution.py:304
  13.6 29.7 %collective-permute-start.1 = (bf16[128,1280]{1,0:T(8,128)(2,1)S(1)}, bf16[128,1280]{1,0:T(8,128)(2,1)S(1)}, u32[]{:S(2)}, u32[]{:S(2)}) collective-permute-start(bf16[128,1280]{1,0:T(8,128)(2,1)S(1)} %pad_dynamic-slice_fusion), channel_id=1, source_target_pairs={{0,8},{8,0},{1,9},{9,1},{2,10},{10,2},{3,11},{11,3},{4,12},{12,4},... | collective-permute-start | bytes 983048 | tf_op jit(solution)/shard_map/ppermute | solution.py:305
  167.8 39.4 %copy-start.4 = (s32[384,6]{0,1:T(8,128)S(1)}, s32[384,6]{0,1:T(8,128)}, u32[]{:S(2)}) copy-start(s32[384,6]{0,1:T(8,128)} %param.15) | copy-start | bytes 27652
  167.8 39.4 %copy-start.5 = (s32[384,6]{0,1:T(8,128)S(1)}, s32[384,6]{0,1:T(8,128)}, u32[]{:S(2)}) copy-start(s32[384,6]{0,1:T(8,128)} %param.13) | copy-start | bytes 27652
  167.8 39.4 %copy-start.6 = (f32[384,6]{0,1:T(8,128)S(1)}, f32[384,6]{0,1:T(8,128)}, u32[]{:S(2)}) copy-start(f32[384,6]{0,1:T(8,128)} %param.14) | copy-start | bytes 27652
  206.6 301.0 %all-gather.13.cloned.1.call-start = ((), (), s32[]{:S(2)}) async-start(), calls=%async_computation.6 | async-start | bytes 5898240 | tf_op jit(solution)/shard_map/all_gather | solution.py:318
  207.2 308.2 %reduce-scatter.5.cloned.1.call-start = ((), (), s32[]{:S(2)}) async-start(), calls=%async_computation.5 | async-start | bytes 17694720 | tf_op jit(solution)/shard_map/reduce_scatter | solution.py:313
  233.2 1.7 copy-start.3
  384.4 203.6 %reduce-scatter.3.cloned.1.call-start = ((), (), s32[]{:S(2)}) async-start(), calls=%async_computation.4 | async-start | bytes 17694720 | tf_op jit(solution)/shard_map/reduce_scatter | solution.py:312
  513.7 1.6 copy-start
  515.4 72.7 %copy-start.1 = (bf16[384,1280]{1,0:T(8,128)(2,1)S(1)}, bf16[384,1280]{1,0:T(8,128)(2,1)}, u32[]{:S(2)}) copy-start(bf16[384,1280]{1,0:T(8,128)(2,1)} %param.11) | copy-start | bytes 2949124
Sparse Core Ops, SparseCore 0:
  10.2 82.7 all-gather.8
  95.2 72.5 all-gather.10
  206.7 27.4 all-gather.14
  236.5 36.9 all-gather.12
  384.6 99.8 reduce-scatter.4
  487.7 100.2 reduce-scatter.2

commit v2 on v1

v2 whole, which is shorter than its diff:
```python
import functools

import jax
import jax.numpy as jnp
from jax import lax
from jax.experimental import pallas as pl
from jax.experimental.pallas import tpu as pltpu
from jax.sharding import PartitionSpec as P


F32 = jnp.float32
BF16 = jnp.bfloat16
SLICE = 128
VMEM_LIMIT = 64_000_000
MESH = pl.DeviceIdType.MESH
NT = (((1,), (1,)), ((), ()))
TN = (((0,), (0,)), ((), ()))


def dot(a, b):
    return jnp.dot(a, b, preferred_element_type=F32)


def dot_nt(a, b):
    return lax.dot_general(a, b, NT, preferred_element_type=F32)


def dot_tn(a, b):
    return lax.dot_general(a, b, TN, preferred_element_type=F32)


def swiglu_parts(one, three, grad_hidden):
    sig = jax.nn.sigmoid(one)
    silu = one * sig
    dh = grad_hidden.astype(BF16).astype(F32)
    hidden = (silu * three).astype(BF16)
    da_one = (dh * three * (sig + silu * (1.0 - sig))).astype(BF16)
    da_three = (dh * silu).astype(BF16)
    return hidden, da_one, da_three


def params(axes):
    return pltpu.CompilerParams(dimension_semantics=("arbitrary",) * axes, vmem_limit_bytes=VMEM_LIMIT)


def gather_kernel(ep_size, x_ref, dy_ref, meta_ref, own_ref, near_x_ref, near_y_ref, other_own_ref, other_x_ref, other_y_ref,
                  far_own_ref, far_other_ref, meta_all_ref, mine, mine_meta, load_sem, store_sem, send_sem, recv_sem):
    me = lax.axis_index("ep")
    core_peer = me + 1 - 2 * (me % 2)
    x_peer = me + 2 - 4 * ((me // 2) % 2)
    y_peer = me + 4 - 8 * (me // 4)
    z_peer = 1 - lax.axis_index("tp")

    barrier = pltpu.get_barrier_semaphore()
    for k in range(1, ep_size):
        pl.semaphore_signal(barrier, inc=1, device_id={"ep": (me + k) % ep_size}, device_id_type=MESH)
    pl.semaphore_signal(barrier, inc=1, device_id={"tp": z_peer}, device_id_type=MESH)

    loads = [pltpu.make_async_copy(x_ref, mine.at[0], load_sem.at[0]),
             pltpu.make_async_copy(dy_ref, mine.at[1], load_sem.at[1]),
             pltpu.make_async_copy(meta_ref, mine_meta, load_sem.at[2])]
    for copy in loads:
        copy.start()
    for copy in loads:
        copy.wait()
    stores = [pltpu.make_async_copy(mine, own_ref.at[0], store_sem.at[0]),
              pltpu.make_async_copy(mine_meta, meta_all_ref.at[me], store_sem.at[1])]
    pl.semaphore_wait(barrier, ep_size)

    half = x_ref.shape[0] // 2
    low, high = pl.ds(0, half), pl.ds(half, half)
    started = []

    def send(device, src, dst):
        n = len(started)
        copy = pltpu.make_async_remote_copy(src_ref=src, dst_ref=dst, send_sem=send_sem.at[n], recv_sem=recv_sem.at[n],
                                            device_id=device, device_id_type=MESH)
        copy.start()
        started.append(copy)
        return copy

    to_x, to_y, to_core = {"ep": x_peer}, {"ep": y_peer}, {"ep": core_peer}
    from_x_low = send(to_x, mine.at[:, low], near_x_ref.at[0, :, low])
    from_y_high = send(to_y, mine.at[:, high], near_y_ref.at[0, :, high])
    from_z = send({"tp": z_peer}, mine, far_own_ref.at[0])
    from_x_high = send(to_x, mine.at[:, high], near_x_ref.at[0, :, high])
    from_y_low = send(to_y, mine.at[:, low], near_y_ref.at[0, :, low])
    waiting = [send({"ep": (me + k) % ep_size}, mine_meta, meta_all_ref.at[me]) for k in range(1, ep_size)]
    waiting.append(send(to_core, mine, other_own_ref.at[0]))
    for copy in stores:
        copy.start()
    from_x_low.wait_recv()
    corner_low = send(to_y, near_x_ref.at[0, :, low], near_y_ref.at[1, :, low])
    waiting.append(send(to_core, near_x_ref.at[0, :, low], other_x_ref.at[0, :, low]))
    from_y_high.wait_recv()
    corner_high = send(to_x, near_y_ref.at[0, :, high], near_y_ref.at[1, :, high])
    waiting.append(send(to_core, near_y_ref.at[0, :, high], other_y_ref.at[0, :, high]))
    from_x_high.wait_recv()
    waiting.append(send(to_core, near_x_ref.at[0, :, high], other_x_ref.at[0, :, high]))
    from_y_low.wait_recv()
    waiting.append(send(to_core, near_y_ref.at[0, :, low], other_y_ref.at[0, :, low]))
    from_z.wait_recv()
    waiting.append(send(to_core, far_own_ref.at[0], far_other_ref.at[0]))
    corner_low.wait_recv()
    waiting.append(send(to_core, near_y_ref.at[1, :, low], other_y_ref.at[1, :, low]))
    corner_high.wait_recv()
    waiting.append(send(to_core, near_y_ref.at[1, :, high], other_y_ref.at[1, :, high]))
    for copy in waiting:
        copy.wait_recv()
    for copy in started:
        copy.wait_send()
    for copy in stores:
        copy.wait()


def gather_layer(tokens, grad_y, meta, ep_size):
    rows, dim = tokens.shape
    one = jax.ShapeDtypeStruct((1, 2, rows, dim), tokens.dtype)
    two = jax.ShapeDtypeStruct((2, 2, rows, dim), tokens.dtype)
    anywhere = pl.BlockSpec(memory_space=pl.ANY)
    copies = 5 + (ep_size - 1) + 1 + 2 + 7
    return pl.pallas_call(
        functools.partial(gather_kernel, ep_size),
        in_specs=[anywhere] * 3, out_specs=[anywhere] * 9,
        out_shape=[one, one, two, one, one, two, one, one, jax.ShapeDtypeStruct((ep_size,) + meta.shape, meta.dtype)],
        scratch_shapes=[pltpu.VMEM((2, rows, dim), tokens.dtype), pltpu.VMEM(meta.shape, meta.dtype),
                        pltpu.SemaphoreType.DMA((3,)), pltpu.SemaphoreType.DMA((2,)),
                        pltpu.SemaphoreType.DMA((copies,)), pltpu.SemaphoreType.DMA((copies,))],
        compiler_params=pltpu.CompilerParams(collective_id=0, has_side_effects=True), name="gather",
        cost_estimate=pl.CostEstimate(flops=60_000_000_000, bytes_accessed=ep_size * rows * dim * 8, transcendentals=0),
    )(tokens, grad_y, meta)


def ep_of(source, ids):
    core = jnp.where(source < 4, ids[1] % 2, 1 - ids[1] % 2)
    return 2 * jnp.bitwise_xor(ids[1] // 2, source % 4) + core


def stream(refs, per_step, buffer, sem):
    blocks = [(ref, i) for ref in refs for i in range(ref.shape[0])]
    step = pl.program_id(0)
    steps = len(blocks) // per_step

    def copies(k):
        return [pltpu.make_async_copy(ref.at[i], buffer.at[k % 2, n], sem.at[k % 2, n])
                for n, (ref, i) in enumerate(blocks[k * per_step:(k + 1) * per_step])]

    @pl.when(step == 0)
    def _():
        for copy in copies(0):
            copy.start()

    for k in range(steps):
        @pl.when(step == k)
        def _():
            if k + 1 < steps:
                for copy in copies(k + 1):
                    copy.start()
            for copy in copies(k):
                copy.wait()

    return step % 2


def dispatch_kernel(local, cap, top_k, ids, *refs):
    *blocks, meta_ref, xd_ref, qd_ref, buffer, sem = refs
    slot = stream(blocks, 1, buffer, sem)
    tokens = buffer.shape[-2]
    rows = local * cap
    meta = meta_ref[0]
    base = (ids[1] * rows).astype(F32)
    row_ids = lax.broadcasted_iota(jnp.int32, (rows, tokens), 0).astype(F32) + base
    gates = jnp.zeros((rows, tokens), F32)
    for j in range(top_k):
        gates = jnp.where(meta[j][None, :] == row_ids, meta[top_k + j][None, :], gates)
    select = jnp.where(gates != 0.0, 1.0, 0.0).astype(BF16)
    row_gate = jnp.sum(gates, axis=1, keepdims=True)
    got_x = dot(select, buffer[slot, 0, 0])
    for l in range(local):
        xd_ref[l] = got_x[l * cap:(l + 1) * cap].astype(BF16)
    got_dy = dot(select, buffer[slot, 0, 1]) * row_gate
    for l in range(local):
        qd_ref[l] = got_dy[l * cap:(l + 1) * cap].astype(BF16)


def dispatch(ids, blocks, meta_all, local, cap, top_k):
    _, _, tokens, dim = blocks[0].shape
    groups = sum(block.shape[0] for block in blocks)
    out = jax.ShapeDtypeStruct((local, groups * cap, dim), BF16)
    out_spec = pl.BlockSpec((local, cap, dim), lambda s, ids: (0, s, 0))
    return pl.pallas_call(
        functools.partial(dispatch_kernel, local, cap, top_k),
        grid_spec=pltpu.PrefetchScalarGridSpec(
            num_scalar_prefetch=1, grid=(groups,),
            in_specs=[pl.BlockSpec(memory_space=pl.ANY)] * len(blocks)
            + [pl.BlockSpec((1, 2 * top_k, tokens), lambda s, ids: (ep_of(s, ids), 0, 0))],
            out_specs=[out_spec, out_spec],
            scratch_shapes=[pltpu.VMEM((2, 1, 2, tokens, dim), BF16), pltpu.SemaphoreType.DMA((2, 1))]),
        out_shape=[out, out], compiler_params=params(1),
        cost_estimate=pl.CostEstimate(flops=4 * groups * local * cap * tokens * dim,
                                      bytes_accessed=groups * (tokens + local * cap) * dim * 4, transcendentals=0),
    )(ids, *blocks, meta_all)


def own_kernel(cap, x_ref, q_ref, w1_ref, w3_ref, w2_ref, o_ref, h_ref, da1_ref, da3_ref):
    rows = x_ref.shape[-2]
    half = rows // 2
    per = half // cap
    for part in range(2):
        span = slice(part * half, (part + 1) * half)
        x = x_ref[0, span]
        hidden, da_one, da_three = swiglu_parts(dot(x, w1_ref[0]), dot(x, w3_ref[0]), dot_nt(q_ref[0, span], w2_ref[0]))
        h_ref[0, span] = hidden
        da1_ref[0, span] = da_one
        da3_ref[0, span] = da_three
        out = dot(hidden, w2_ref[0])
        for s in range(per):
            o_ref[part * per + s] = out[s * cap:(s + 1) * cap].astype(BF16)


def own_experts(xd, qd, w1, w3, w2, cap):
    local, rows, dim = xd.shape
    ff = w1.shape[-1]
    groups = rows // cap
    by_expert = lambda l: (l, 0, 0)
    row_spec = pl.BlockSpec((1, rows, dim), by_expert)
    hid = jax.ShapeDtypeStruct((local, rows, ff), BF16)
    hid_spec = pl.BlockSpec((1, rows, ff), by_expert)
    wide, tall = pl.BlockSpec((1, dim, ff), by_expert), pl.BlockSpec((1, ff, dim), by_expert)
    return pl.pallas_call(
        functools.partial(own_kernel, cap), grid=(local,),
        in_specs=[row_spec, row_spec, wide, wide, tall],
        out_specs=[pl.BlockSpec((groups, cap, dim), lambda l: (0, l, 0)), hid_spec, hid_spec, hid_spec],
        out_shape=[jax.ShapeDtypeStruct((groups, local * cap, dim), BF16), hid, hid, hid],
        compiler_params=params(1), name="own",
        cost_estimate=pl.CostEstimate(flops=8 * local * rows * dim * ff,
                                      bytes_accessed=local * (6 * rows * dim + 6 * rows * ff + 6 * dim * ff),
                                      transcendentals=local * rows * ff),
    )(xd, qd, w1, w3, w2)


def back_kernel(cap, da1_ref, da3_ref, w1_ref, w3_ref, dr_ref):
    grad = dot_nt(da1_ref[0], w1_ref[0]) + dot_nt(da3_ref[0], w3_ref[0])
    for s in range(dr_ref.shape[0]):
        dr_ref[s] = grad[s * cap:(s + 1) * cap].astype(BF16)


def own_back(da1, da3, w1, w3, cap):
    local, rows, ff = da1.shape
    dim = w1.shape[1]
    groups = rows // cap
    by_expert = lambda l: (l, 0, 0)
    hid_spec, wide = pl.BlockSpec((1, rows, ff), by_expert), pl.BlockSpec((1, dim, ff), by_expert)
    return pl.pallas_call(
        functools.partial(back_kernel, cap), grid=(local,),
        in_specs=[hid_spec, hid_spec, wide, wide],
        out_specs=pl.BlockSpec((groups, cap, dim), lambda l: (0, l, 0)),
        out_shape=jax.ShapeDtypeStruct((groups, local * cap, dim), BF16),
        compiler_params=params(1), name="back",
        cost_estimate=pl.CostEstimate(flops=4 * local * rows * dim * ff,
                                      bytes_accessed=local * (2 * rows * dim + 4 * rows * ff + 4 * dim * ff),
                                      transcendentals=0),
    )(da1, da3, w1, w3)


def grads_kernel(ids, x_ref, q_ref, xp_ref, qp_ref, h_ref, da1_ref, da3_ref, w1_ref, w3_ref, w2_ref,
                 g1_ref, g3_ref, g2_ref, rows_x, rows_q, hid, da_one, da_three, tall):
    rows = x_ref.shape[-2]
    half = rows // 2
    part = ids[0]
    width = g1_ref.shape[1]
    columns = pl.ds(pl.multiple_of(part * width, 128), width)
    ff = w1_ref.shape[-1]
    reach = tall.shape[0]
    chunk = pl.ds(pl.multiple_of(part * (ff - reach), 128), reach)
    rows_x[:rows] = x_ref[0, :, columns]
    rows_x[rows:] = xp_ref[0, :, columns]
    rows_q[:rows] = q_ref[0]
    rows_q[rows:] = qp_ref[0]
    hid[:rows] = h_ref[0]
    da_one[:rows] = da1_ref[0]
    da_three[:rows] = da3_ref[0]
    for piece in range(2):
        span = slice(piece * half, (piece + 1) * half)
        dest = slice(rows + piece * half, rows + (piece + 1) * half)
        x = xp_ref[0, span]
        hidden, one, three = swiglu_parts(dot(x, w1_ref[0]), dot(x, w3_ref[0]), dot_nt(qp_ref[0, span], w2_ref[0]))
        hid[dest] = hidden
        da_one[dest] = one
        da_three[dest] = three
    g1_ref[0] = dot_tn(rows_x[...], da_one[...]).astype(BF16)
    g3_ref[0] = dot_tn(rows_x[...], da_three[...]).astype(BF16)
    height = g2_ref.shape[1]
    tall[...] = dot_tn(hid[:, chunk], rows_q[...])
    skip = pl.multiple_of(part * (height - (ff - reach)), 8)
    g2_ref[0] = tall[pl.ds(skip, height)].astype(BF16)


def expert_grads(ids, xd, qd, xp, qp, h, da1, da3, w1, w3, w2, parts):
    local, rows, dim = xd.shape
    ff = w1.shape[-1]
    by_expert = lambda l, ids: (l, 0, 0)
    row_spec, hid_spec = pl.BlockSpec((1, rows, dim), by_expert), pl.BlockSpec((1, rows, ff), by_expert)
    wide, tall = pl.BlockSpec((1, dim, ff), by_expert), pl.BlockSpec((1, ff, dim), by_expert)
    g1 = jax.ShapeDtypeStruct((local, dim // parts, ff), BF16)
    g2 = jax.ShapeDtypeStruct((local, ff // parts, dim), BF16)
    g1_spec, g2_spec = pl.BlockSpec((1, dim // parts, ff), by_expert), pl.BlockSpec((1, ff // parts, dim), by_expert)
    reach = -(-(ff // parts) // 128) * 128
    return pl.pallas_call(
        grads_kernel,
        grid_spec=pltpu.PrefetchScalarGridSpec(
            num_scalar_prefetch=1, grid=(local,),
            in_specs=[row_spec, row_spec, row_spec, row_spec, hid_spec, hid_spec, hid_spec, wide, wide, tall],
            out_specs=[g1_spec, g1_spec, g2_spec],
            scratch_shapes=[pltpu.VMEM((2 * rows, dim // parts), BF16), pltpu.VMEM((2 * rows, dim), BF16)]
            + [pltpu.VMEM((2 * rows, ff), BF16)] * 3 + [pltpu.VMEM((reach, dim), F32)]),
        out_shape=[g1, g1, g2], compiler_params=params(1), name="grads",
        cost_estimate=pl.CostEstimate(flops=12 * local * rows * dim * ff,
                                      bytes_accessed=local * (8 * rows * dim + 6 * rows * ff + 9 * dim * ff),
                                      transcendentals=local * rows * ff),
    )(ids, xd, qd, xp, qp, h, da1, da3, w1, w3, w2)


def shared_kernel(*refs):
    *blocks, wa_ref, w2_ref, h_ref, da_ref, g_ref, g_far_ref, buffer, sem = refs
    slot = stream(blocks, 2, buffer, sem)

    @pl.when(pl.program_id(0) == 0)
    def _():
        g_ref[...] = jnp.zeros_like(g_ref)
        g_far_ref[...] = jnp.zeros_like(g_far_ref)

    _, pair, _, tokens, dim = buffer.shape
    x = buffer[slot, :, 0].reshape(pair * tokens, dim)
    dy = buffer[slot, :, 1].reshape(pair * tokens, dim)
    proj = dot(x, wa_ref[...])
    dh = dot_nt(dy, w2_ref[...])
    for half, grad_ref in enumerate((g_ref, g_far_ref)):
        one = proj[:, 2 * half * SLICE:(2 * half + 1) * SLICE]
        three = proj[:, (2 * half + 1) * SLICE:(2 * half + 2) * SLICE]
        hidden, da_one, da_three = swiglu_parts(one, three, dh[:, half * SLICE:(half + 1) * SLICE])
        da = jnp.concatenate([da_one, da_three], axis=1)
        h_ref[:, :, half * SLICE:(half + 1) * SLICE] = hidden.reshape(pair, tokens, SLICE)
        da_ref[:, :, 2 * half * SLICE:2 * (half + 1) * SLICE] = da.reshape(pair, tokens, 2 * SLICE)
        grad_ref[:2 * SLICE] += dot_tn(da, x)
        grad_ref[2 * SLICE:] += dot_tn(hidden, dy)


def shared_expert(blocks, wa, w2):
    _, _, tokens, dim = blocks[0].shape
    groups = sum(block.shape[0] for block in blocks)
    by_pair, fixed = lambda s: (s, 0, 0), lambda s: (0, 0)
    grad = jax.ShapeDtypeStruct((3 * SLICE, dim), F32)
    return pl.pallas_call(
        shared_kernel, grid=(groups // 2,),
        in_specs=[pl.BlockSpec(memory_space=pl.ANY)] * len(blocks)
        + [pl.BlockSpec(wa.shape, fixed), pl.BlockSpec(w2.shape, fixed)],
        out_specs=[pl.BlockSpec((2, tokens, 2 * SLICE), by_pair), pl.BlockSpec((2, tokens, 4 * SLICE), by_pair),
                   pl.BlockSpec(grad.shape, fixed), pl.BlockSpec(grad.shape, fixed)],
        out_shape=[jax.ShapeDtypeStruct((groups, tokens, 2 * SLICE), BF16),
                   jax.ShapeDtypeStruct((groups, tokens, 4 * SLICE), BF16), grad, grad],
        scratch_shapes=[pltpu.VMEM((2, 2, 2, tokens, dim), BF16), pltpu.SemaphoreType.DMA((2, 2))],
        compiler_params=params(1), name="shared",
        cost_estimate=pl.CostEstimate(flops=18 * groups * tokens * dim * SLICE,
                                      bytes_accessed=4 * groups * tokens * dim, transcendentals=0),
    )(*blocks, wa, w2)


def gate_matrix(meta, ids, rows, top_k):
    tokens = meta.shape[0]
    base = (ids[1] * rows).astype(F32)
    row_ids = lax.broadcasted_iota(jnp.int32, (tokens, rows), 1).astype(F32) + base
    gates = jnp.zeros((tokens, rows), F32)
    for j in range(top_k):
        gates = jnp.where(meta[:, j:j + 1] == row_ids, meta[:, top_k + j:top_k + j + 1], gates)
    return gates


def combine_out_kernel(top_k, ids, meta_ref, o_ref, h_ref, w2_ref, y_ref):
    tokens = h_ref.shape[1]
    gates = gate_matrix(meta_ref[0], ids, o_ref.shape[1], top_k)
    high = gates.astype(BF16)
    rest = gates - high.astype(F32)
    mid = rest.astype(BF16)
    low = (rest - mid.astype(F32)).astype(BF16)
    sums = dot(jnp.concatenate([high, mid, low], axis=0), o_ref[0])
    y_ref[0] = sums[:tokens] + sums[tokens:2 * tokens] + sums[2 * tokens:] + dot(h_ref[0], w2_ref[...])


def combine_back_kernel(top_k, ids, meta_ref, dr_ref, da_ref, wa_ref, dx_ref):
    gates = gate_matrix(meta_ref[0], ids, dr_ref.shape[1], top_k)
    select = jnp.where(gates != 0.0, 1.0, 0.0).astype(BF16)
    dx_ref[0] = dot(select, dr_ref[0]) + dot_nt(da_ref[0], wa_ref[...])


def combine(kernel, ids, meta_own, returned, hidden, weight, top_k, passes):
    groups, rows, dim = returned.shape
    tokens, width = hidden.shape[1:]
    by_source = lambda s, ids: (s, 0, 0)
    by_ep = lambda s, ids: (ep_of(s, ids), 0, 0)
    return pl.pallas_call(
        functools.partial(kernel, top_k),
        grid_spec=pltpu.PrefetchScalarGridSpec(
            num_scalar_prefetch=1, grid=(groups,),
            in_specs=[pl.BlockSpec((1, tokens, 2 * top_k), by_ep), pl.BlockSpec((1, rows, dim), by_source),
                      pl.BlockSpec((1, tokens, width), by_source), pl.BlockSpec(weight.shape, lambda s, ids: (0, 0))],
            out_specs=pl.BlockSpec((1, tokens, dim), by_ep)),
        out_shape=jax.ShapeDtypeStruct((groups, tokens, dim), F32), compiler_params=params(1),
        cost_estimate=pl.CostEstimate(flops=2 * passes * groups * tokens * rows * dim,
                                      bytes_accessed=groups * (2 * rows + 4 * tokens) * dim, transcendentals=0),
    )(ids, meta_own, returned, hidden, weight)


def solution(mesh):
    ep_size, tp_size = mesh.shape["ep"], mesh.shape["tp"]
    row_spec = P(("ep", "tp"), None)
    expert_spec = P("ep", None, None)
    expert_grad_spec = P("ep", "tp", None)
    swap = [(0, 1), (1, 0)]
    cores = [(i, i ^ 1) for i in range(ep_size)]

    def device_fn(tokens, grad_y, expert_ids, gate_vals, slot_ids,
                  shared_w1, shared_w3, shared_w2, expert_w1, expert_w3, expert_w2):
        rows_dev, dim = tokens.shape
        top_k = expert_ids.shape[1]
        local = expert_w1.shape[0]
        experts = local * ep_size
        cap = (2 * rows_dev * top_k + experts - 1) // experts
        tp_id, ep_id = lax.axis_index("tp"), lax.axis_index("ep")
        ids = jnp.stack([tp_id, ep_id]).astype(jnp.int32)

        pos = jnp.where(slot_ids >= 0, expert_ids * cap + slot_ids, -1).astype(F32)
        meta = jnp.concatenate([pos.T, gate_vals.T], axis=0)
        *gathered, meta_all = gather_layer(tokens, grad_y, meta, ep_size)
        blocks, (far_own, far_other) = gathered[:6], gathered[6:]
        far_meta = lax.ppermute(meta_all, "tp", swap)
        far_x = lax.ppermute(blocks[1], "tp", swap)
        far_y = lax.ppermute(blocks[2], "tp", swap)
        cross_x = lax.ppermute(far_x, "ep", cores)
        cross_y = lax.ppermute(far_y, "ep", cores)

        ff = shared_w1.shape[1]
        padded = ep_size * SLICE
        wide_pad = ((0, 0), (0, padded - ff))
        start = ep_id * SLICE
        w1s = lax.dynamic_slice(jnp.pad(shared_w1, wide_pad), (0, start), (dim, SLICE))
        w3s = lax.dynamic_slice(jnp.pad(shared_w3, wide_pad), (0, start), (dim, SLICE))
        w2s = lax.dynamic_slice(jnp.pad(shared_w2, ((0, padded - ff), (0, 0))), (start, 0), (SLICE, dim))
        wa_own = jnp.concatenate([w1s, w3s], axis=1)
        wa = jnp.concatenate([wa_own, lax.ppermute(wa_own, "tp", swap)], axis=1)
        w2a = jnp.concatenate([w2s, lax.ppermute(w2s, "tp", swap)], axis=0)

        xd, qd = dispatch(ids, blocks, meta_all, local, cap, top_k)
        sh, sda, shared_grad, shared_far = shared_expert(blocks, wa, w2a)
        o, h, da1, da3 = own_experts(xd, qd, expert_w1, expert_w3, expert_w2, cap)
        meta_own = meta_all.transpose(0, 2, 1)
        y_part = combine(combine_out_kernel, ids, meta_own, o, sh, w2a, top_k, 3)
        y_sum = lax.psum_scatter(y_part.reshape(-1, dim), "ep", scatter_dimension=0, tiled=True)
        dr = own_back(da1, da3, expert_w1, expert_w3, cap)
        dx_part = combine(combine_back_kernel, ids, meta_own, dr, sda, wa, top_k, 1)
        dx_sum = lax.psum_scatter(dx_part.reshape(-1, dim), "ep", scatter_dimension=0, tiled=True)

        xp, qp = dispatch(ids, (far_own, far_x, far_y, far_other, cross_x, cross_y), far_meta, local, cap, top_k)
        g1, g3, g2 = expert_grads(ids, xd, qd, xp, qp, h, da1, da3, expert_w1, expert_w3, expert_w2, tp_size)

        shared_grad = shared_grad + lax.ppermute(shared_far, "tp", swap)
        shared_all = lax.all_gather(shared_grad.astype(BF16), "ep")
        sg1, sg3, sg2 = [shared_all[:, i * SLICE:(i + 1) * SLICE].reshape(padded, dim)[:ff] for i in range(3)]
        sg1, sg3 = sg1.T, sg3.T
        out_y = (tokens.astype(F32) + y_sum).astype(BF16)
        grad_tokens = (grad_y.astype(F32) + dx_sum).astype(BF16)
        return out_y, grad_tokens, sg1, sg3, sg2, g1, g3, g2

    return jax.shard_map(
        device_fn, mesh=mesh,
        in_specs=(row_spec, row_spec, row_spec, row_spec, row_spec,
                  P(None, "tp"), P(None, "tp"), P("tp", None), expert_spec, expert_spec, expert_spec),
        out_specs=(row_spec, row_spec, P(None, "tp"), P(None, "tp"), P("tp", None),
                   expert_grad_spec, expert_grad_spec, expert_grad_spec),
        check_vma=False)
```

time: 598 us -> 613 us (1.025)
  Pallas kernels: 308 us -> 381 us
  waiting for transfers between devices: 224 us -> 176 us
  blocking collectives: 25.9 us -> 0 us
  starting transfers between devices: 3.98 us -> 10.3 us
    ppermute x0 -> x6, waiting for transfers between devices: none -> 176 us  [the longest x1 85 us: device_fn(): far_y = lax.ppermute(blocks[2], 'tp', swap)]
    all_gather x4 -> x1, waiting for transfers between devices: 122 us -> 0.02 us  [device_fn(): shared_all = lax.all_gather(shared_grad.astype(BF16), 'ep')]
    pallas_call x3 -> x6, Pallas kernels: 183 us -> 278 us  [the longest x1 91 us: expert_grads(): pl.pallas_call(grads_kernel, grid_spec=pltpu.PrefetchScalarGridSpec(num_s...]
    reduce_scatter x1, waiting for transfers between devices: 69.9 us -> 0.01 us  [device_fn(): lax.psum_scatter(y_part.reshape(-1, dim), 'ep', scatter_dimension=0, tile...]
    ppermute x1, waiting for transfers between devices: 28.7 us -> 0.01 us  [device_fn(): w2a = jnp.concatenate([w2s, lax.ppermute(w2s, 'tp', swap)], axis=0)]
    all_gather x1 -> x0, blocking collectives: 25.9 us -> none  [device_fn(): lax.all_gather(meta, ('ep', 'tp'))]
    pallas_call x1, Pallas kernels: 82.6 us -> 58.5 us  [own_experts(): pl.pallas_call(functools.partial(own_kernel, cap), grid=(local,), in_spec...]
    unnamed x15 -> x30, local copies, waits for them, and re-layouts: 3.02 us -> 10.1 us
  transfers between devices with their start and end apart: 8 -> 11, of which waited for: 4 -> 4; matrix products, arithmetic and copies ran while one was open for 3% -> 3% of each run, Pallas kernels for 45% -> 59%
where the time goes in v2:
time: 613 us; the launch traced here: 612 us
  Pallas kernels  381 us (62%)
  waiting for transfers between devices  176 us (29%)
  local copies, waits for them, and re-layouts  19 us (3%)
  between operations  13.9 us (2%)
  other arithmetic  11.6 us (2%)
  starting transfers between devices  10.3 us (2%)
    pallas_call x1, Pallas kernels, expert_grads(): pl.pallas_call(grads_kernel, grid_spec=pltpu.PrefetchScalarGridSpec(num_s...  91 us
    ppermute x1, waiting for transfers between devices, device_fn(): far_y = lax.ppermute(blocks[2], 'tp', swap)  85 us
    pallas_call x1, Pallas kernels, gather_layer(): pl.pallas_call(functools.partial(gather_kernel, ep_size), in_specs=[anywh...  73.9 us
    pallas_call x1, Pallas kernels, own_experts(): pl.pallas_call(functools.partial(own_kernel, cap), grid=(local,), in_spec...  58.5 us
    pallas_call x2, Pallas kernels, combine(): pl.pallas_call(functools.partial(kernel, top_k), grid_spec=pltpu.Prefetch...  55.5 us
    pallas_call x2, Pallas kernels, dispatch(): pl.pallas_call(functools.partial(dispatch_kernel, local, cap, top_k), gri...  44.6 us
    ppermute x1, waiting for transfers between devices, device_fn(): shared_grad = shared_grad + lax.ppermute(shared_far, 'tp', swap)  43.8 us
    ppermute x1, waiting for transfers between devices, device_fn(): far_x = lax.ppermute(blocks[1], 'tp', swap)  41.4 us
  transfers between devices with their start and end apart: 11, of which 4 were waited for; matrix products, arithmetic and copies ran while one was open for 3% of the time, Pallas kernels for 59%

profile of v2, /device:TPU:0, one launch (start us, length us, event | category | flops | bytes accessed | tf_op | source)
XLA Modules:
  0.0 611.8 jit_solution(18172516432929971131)
XLA Ops:
  7.2 0.0 all-gather.3.cloned.1.call-start
  7.2 1.4 pad_dynamic-slice_fusion.1
  8.6 0.0 copy-start.5
  8.6 0.0 copy-start.6
  8.6 0.0 copy-start.7
  8.6 0.1 pad_maximum_fusion.1
  8.7 3.3 collective-permute-start
  12.0 0.1 pad_dynamic-slice_fusion
  12.1 0.4 collective-permute-start.1
  12.5 0.6 pad_maximum_fusion.3.meta_ref
  13.1 73.9 %gather.1 = (bf16[1,2,384,1280]{3,2,1,0:T(8,128)(2,1)}, bf16[1,2,384,1280]{3,2,1,0:T(8,128)(2,1)}, bf16[2,2,384,1280]{3,2,1,0:T(8,128)(2,1)}, bf16[1,2,384,1280]...) custom-call(bf16[384,1280]{1,0:T(8,128)(2,1)} %x_ref.1, ...), custom_call_target="tpu_custom_call" | custom-call | flops 60000002048 | bytes 31457280 | tf_op jit(solution)/shard_map/gather/pallas_call | solution.py:122
  87.0 0.0 collective-permute-done.1
  87.0 0.9 pad_maximum_fusion.2.refs_7_.w2_ref
  87.9 1.2 pad_maximum_fusion.refs_6_.wa_ref
  89.1 22.6 %shared.1 = (bf16[8,384,256]{2,1,0:T(8,128)(2,1)}, bf16[8,384,512]{2,1,0:T(8,128)(2,1)}, f32[384,1280]{1,0:T(8,128)}, f32[384,1280]{1,0:T(8,128)}) custom-call(bf16[1,2,384,1280]{3,2,1,0:T(8,128)(2,1)} %get-tuple-element.33.refs_0_, bf16[1,2,384,1280]{3,2,1,0:T(8,128)(2,1)} %get-tuple-element.34.refs_1_, ...), custom_call_target="tpu_custom_call" | custom-call | flops 9059696640 | bytes 15728640 | tf_op jit(solution)/shard_map/shared/pallas_call | solution.py:354
  111.7 1.6 collective-permute-start.2
  113.3 43.8 %collective-permute-done.2 = f32[384,1280]{1,0:T(8,128)S(1)} collective-permute-done((f32[384,1280]{1,0:T(8,128)}, f32[384,1280]{1,0:T(8,128)S(1)}, u32[]{:S(2)}, u32[]{:S(2)}) %collective-permute-start.2) | collective-permute-done | bytes 1966112 | tf_op jit(solution)/shard_map/ppermute | solution.py:466
  157.1 2.8 add_convert_fusion
  159.9 0.0 all-gather.3.cloned.1.call-update
  159.9 0.2 reduce-scatter.3.cloned.1.call-start
  160.1 1.7 copy.22
  161.8 0.7 pad_add_fusion.ids
  162.5 22.4 %shard_map.170 = (bf16[8,576,1280]{2,1,0:T(8,128)(2,1)}, bf16[8,576,1280]{2,1,0:T(8,128)(2,1)}) custom-call(s32[2]{0:T(128)} %pad_add_fusion.ids, bf16[1,2,384,1280]{3,2,1,0:T(8,128)(2,1)} %get-tuple-element.33.refs_0_, bf16[1,2,384,1280]{3,2,1,0:T(8,128)(2,1)} %get-tuple-element.34.refs_1_, bf16[2,2,384,1280]{3,2,1,0:T(8,128)(2,1)} %get-tuple-element.35.refs_2_, ...), custom_call_target="tpu_custom_call" | custom-call | flops 9059696640 | bytes 39321600 | tf_op jit(solution)/shard_map/pallas_call | solution.py:191
  184.9 58.5 %own.1 = (bf16[8,576,1280]{2,1,0:T(8,128)(2,1)}, bf16[8,576,896]{2,1,0:T(8,128)(2,1)}, bf16[8,576,896]{2,1,0:T(8,128)(2,1)}, bf16[8,576,896]{2,1,0:T(8,128)(2,1)}) custom-call(bf16[8,576,1280]{2,1,0:T(8,128)(2,1)} %get-tuple-element.39.x_ref, bf16[8,576,1280]{2,1,0:T(8,128)(2,1)} %get-tuple-element.40.q_ref, bf16[8,1280,896]{2,1,0:T(8,128)(2,1)} %w1_ref.5, ...), custom_call_target="tpu_custom_call" | custom-call | flops 42278584320 | bytes 115212288 | tf_op jit(solution)/shard_map/own/pallas_call | solution.py:230
  243.4 33.8 %shard_map.171 = f32[8,384,1280]{2,1,0:T(8,128)} custom-call(s32[2]{0:T(128)} %pad_add_fusion.ids, f32[8,384,12]{2,1,0:T(8,128)} %bitcast.20, bf16[8,576,1280]{2,1,0:T(8,128)(2,1)} %get-tuple-element.41.o_ref, bf16[8,384,256]{2,1,0:T(8,128)(2,1)} %get-tuple-element.42.h_ref, bf16[256,1280]{1,0:T(8,128)(2,1)} %pad_maximum_fusion.2.refs_7_.w2_ref), custom_call_target="tpu_custom_call" | custom-call | flops 13589544960 | bytes 27525120 | tf_op jit(solution)/shard_map/pallas_call | solution.py:401
  277.1 0.0 reduce-scatter.3.cloned.1.call-update
  277.2 0.3 reduce-scatter.5.cloned.1.call-start
  277.4 34.7 %back.1.dr_ref = bf16[8,576,1280]{2,1,0:T(8,128)(2,1)} custom-call(bf16[8,576,896]{2,1,0:T(8,128)(2,1)} %get-tuple-element.43.da1_ref, bf16[8,576,896]{2,1,0:T(8,128)(2,1)} %get-tuple-element.44.da3_ref, bf16[8,1280,896]{2,1,0:T(8,128)(2,1)} %w1_ref.5, bf16[8,1280,896]{2,1,0:T(8,128)(2,1)} %w3_ref.5), custom_call_target="tpu_custom_call" | custom-call | flops 21139292160 | bytes 65011712 | tf_op jit(solution)/shard_map/back/pallas_call | solution.py:254
  312.1 21.7 %shard_map.172 = f32[8,384,1280]{2,1,0:T(8,128)} custom-call(s32[2]{0:T(128)} %pad_add_fusion.ids, f32[8,384,12]{2,1,0:T(8,128)} %bitcast.21, bf16[8,576,1280]{2,1,0:T(8,128)(2,1)} %back.1.dr_ref, bf16[8,384,512]{2,1,0:T(8,128)(2,1)} %get-tuple-element.45.da_ref, bf16[1280,512]{1,0:T(8,128)(2,1)} %pad_maximum_fusion.refs_6_.wa_ref), custom_call_target="tpu_custom_call" | custom-call | flops 4529848320 | bytes 27525120 | tf_op jit(solution)/shard_map/pallas_call | solution.py:401
  333.9 0.0 reduce-scatter.5.cloned.1.call-update
  333.9 1.6 collective-permute-start.4
  335.5 1.5 collective-permute-start.3
  336.9 85.0 %collective-permute-done.4.refs_2_ = bf16[2,2,384,1280]{3,2,1,0:T(8,128)(2,1)S(1)} collective-permute-done((bf16[2,2,384,1280]{3,2,1,0:T(8,128)(2,1)}, bf16[2,2,384,1280]{3,2,1,0:T(8,128)(2,1)S(1)}, u32[]{:S(2)}, u32[]{:S(2)}) %collective-permute-start.4) | collective-permute-done | bytes 3932192 | tf_op jit(solution)/shard_map/ppermute | solution.py:438
  422.0 41.4 %collective-permute-done.3.refs_1_ = bf16[1,2,384,1280]{3,2,1,0:T(8,128)(2,1)S(1)} collective-permute-done((bf16[1,2,384,1280]{3,2,1,0:T(8,128)(2,1)S(1)}, bf16[1,2,384,1280]{3,2,1,0:T(8,128)(2,1)S(1)}, u32[]{:S(2)}, u32[]{:S(2)}) %collective-permute-start.3) | collective-permute-done | bytes 1966112 | tf_op jit(solution)/shard_map/ppermute | solution.py:437
  463.4 1.4 collective-permute-start.7
  464.8 5.9 collective-permute-done.7.refs_6_
  470.7 0.0 copy-start.12
  470.7 0.0 copy-start.9
  470.8 1.9 copy-done.9
  472.7 0.6 copy-done.12
  473.3 22.2 %shard_map.173 = (bf16[8,576,1280]{2,1,0:T(8,128)(2,1)}, bf16[8,576,1280]{2,1,0:T(8,128)(2,1)}) custom-call(s32[2]{0:T(128)} %pad_add_fusion.ids, bf16[1,2,384,1280]{3,2,1,0:T(8,128)(2,1)} %get-tuple-element.48.refs_0_, bf16[1,2,384,1280]{3,2,1,0:T(8,128)(2,1)} %copy-done.11, bf16[2,2,384,1280]{3,2,1,0:T(8,128)(2,1)} %copy-done.8, ...), custom_call_target="tpu_custom_call" | custom-call | flops 9059696640 | bytes 39321600 | tf_op jit(solution)/shard_map/pallas_call | solution.py:191
  495.5 91.0 %grads.1 = (bf16[8,640,896]{2,1,0:T(8,128)(2,1)}, bf16[8,640,896]{2,1,0:T(8,128)(2,1)}, bf16[8,448,1280]{2,1,0:T(8,128)(2,1)}) custom-call(s32[2]{0:T(128)} %pad_add_fusion.ids, bf16[8,576,1280]{2,1,0:T(8,128)(2,1)} %get-tuple-element.39.x_ref, bf16[8,576,1280]{2,1,0:T(8,128)(2,1)} %get-tuple-element.40.q_ref, ...), custom_call_target="tpu_custom_call" | custom-call | flops 63417876480 | bytes 154533888 | tf_op jit(solution)/shard_map/grads/pallas_call | solution.py:309
  586.6 0.0 all-gather.3.cloned.1.call-done
  586.6 5.8 fusion
  592.4 4.3 copy.23
  596.6 3.2 copy.24
  599.9 2.8 add_convert_fusion.2
  602.6 2.7 add_convert_fusion.1
  (29 shorter events, 0.1 us)
Async XLA Ops:
  7.2 579.4 %all-gather.3.cloned.1.call-start = ((), (), s32[]{:S(2)}) async-start(), calls=%async_computation.4 | async-start | bytes 8847360 | tf_op jit(solution)/shard_map/all_gather | solution.py:467
  7.2 4.8 copy-start
  8.6 3.9 copy-start.5
  8.6 3.9 copy-start.6
  8.6 3.9 copy-start.7
  8.7 79.2 %collective-permute-start = (bf16[1280,256]{1,0:T(8,128)(2,1)S(1)}, bf16[1280,256]{1,0:T(8,128)(2,1)S(1)}, u32[]{:S(2)}, u32[]{:S(2)}) collective-permute-start(bf16[1280,256]{1,0:T(8,128)(2,1)S(1)} %pad_maximum_fusion.1), channel_id=1, source_target_pairs={{0,8},{8,0},{1,9},{9,1},{2,10},{10,2},{3,11},{11,3},{4,12},{12,4},... | collective-permute-start | bytes 1966088 | tf_op jit(solution)/shard_map/ppermute | solution.py:450
  12.1 74.9 %collective-permute-start.1 = (bf16[128,1280]{1,0:T(8,128)(2,1)S(1)}, bf16[128,1280]{1,0:T(8,128)(2,1)S(1)}, u32[]{:S(2)}, u32[]{:S(2)}) collective-permute-start(bf16[128,1280]{1,0:T(8,128)(2,1)S(1)} %pad_dynamic-slice_fusion), channel_id=1, source_target_pairs={{0,8},{8,0},{1,9},{9,1},{2,10},{10,2},{3,11},{11,3},{4,12},{12,4},... | collective-permute-start | bytes 983048 | tf_op jit(solution)/shard_map/ppermute | solution.py:451
  111.7 45.4 %collective-permute-start.2 = (f32[384,1280]{1,0:T(8,128)}, f32[384,1280]{1,0:T(8,128)S(1)}, u32[]{:S(2)}, u32[]{:S(2)}) collective-permute-start(f32[384,1280]{1,0:T(8,128)} %get-tuple-element.47), channel_id=1, source_target_pairs={{0,8},{8,0},{1,9},{9,1},{2,10},{10,2},{3,11},{11,3},{4,12},{12,4},... | collective-permute-start | bytes 5898248 | tf_op jit(solution)/shard_map/ppermute | solution.py:466
  157.1 3.0 copy-start.3
  159.9 440.0 %reduce-scatter.3.cloned.1.call-start = ((), (), s32[]{:S(2)}) async-start(), calls=%async_computation.2 | async-start | bytes 17694720 | tf_op jit(solution)/shard_map/reduce_scatter | solution.py:458
  277.2 325.5 %reduce-scatter.5.cloned.1.call-start = ((), (), s32[]{:S(2)}) async-start(), calls=%async_computation.3 | async-start | bytes 17694720 | tf_op jit(solution)/shard_map/reduce_scatter | solution.py:461
  333.9 1.6 copy-start.10
  333.9 129.5 %copy-start.4 = (f32[8,12,384]{2,1,0:T(8,128)S(1)}, f32[8,12,384]{2,1,0:T(8,128)}, u32[]{:S(2)}) copy-start(f32[8,12,384]{2,1,0:T(8,128)} %get-tuple-element.32.refs_6_) | copy-start | bytes 442372
  333.9 88.1 %collective-permute-start.4 = (bf16[2,2,384,1280]{3,2,1,0:T(8,128)(2,1)}, bf16[2,2,384,1280]{3,2,1,0:T(8,128)(2,1)S(1)}, u32[]{:S(2)}, u32[]{:S(2)}) collective-permute-start(bf16[2,2,384,1280]{3,2,1,0:T(8,128)(2,1)} %get-tuple-element.35.refs_2_), channel_id=1, source_target_pairs={{0,8},{8,0},{1,9},{9,1},{2,10},{10,2},{3,11},{11,3},{4,12},{12,4},... | collective-permute-start | bytes 11796488 | tf_op jit(solution)/shard_map/ppermute | solution.py:438
  335.5 127.9 %collective-permute-start.3 = (bf16[1,2,384,1280]{3,2,1,0:T(8,128)(2,1)S(1)}, bf16[1,2,384,1280]{3,2,1,0:T(8,128)(2,1)S(1)}, u32[]{:S(2)}, u32[]{:S(2)}) collective-permute-start(bf16[1,2,384,1280]{3,2,1,0:T(8,128)(2,1)S(1)} %copy-done.10), channel_id=1, source_target_pairs={{0,8},{8,0},{1,9},{9,1},{2,10},{10,2},{3,11},{11,3},{4,12},{12,4},... | collective-permute-start | bytes 5898248 | tf_op jit(solution)/shard_map/ppermute | solution.py:437
  422.0 48.7 %copy-start.8 = (bf16[2,2,384,1280]{3,2,1,0:T(8,128)(2,1)}, bf16[2,2,384,1280]{3,2,1,0:T(8,128)(2,1)S(1)}, u32[]{:S(2)}) copy-start(bf16[2,2,384,1280]{3,2,1,0:T(8,128)(2,1)S(1)} %collective-permute-done.4.refs_2_) | copy-start | bytes 11796484
  422.0 48.8 %collective-permute-start.6 = (bf16[2,2,384,1280]{3,2,1,0:T(8,128)(2,1)S(1)}, bf16[2,2,384,1280]{3,2,1,0:T(8,128)(2,1)S(1)}, u32[]{:S(2)}, u32[]{:S(2)}) collective-permute-start(bf16[2,2,384,1280]{3,2,1,0:T(8,128)(2,1)S(1)} %collective-permute-done.4.refs_2_), channel_id=1, source_target_pairs={{0,1},{1,0},{2,3},{3,2},{4,5},{5,4},{6,7},{7,6},{8,9},{9,8},{10,11... | collective-permute-start | bytes 11796488 | tf_op jit(solution)/shard_map/ppermute | solution.py:440
  463.4 9.3 %copy-start.11 = (bf16[1,2,384,1280]{3,2,1,0:T(8,128)(2,1)}, bf16[1,2,384,1280]{3,2,1,0:T(8,128)(2,1)S(1)}, u32[]{:S(2)}) copy-start(bf16[1,2,384,1280]{3,2,1,0:T(8,128)(2,1)S(1)} %collective-permute-done.3.refs_1_) | copy-start | bytes 5898244
  463.4 7.3 %collective-permute-start.5 = (bf16[1,2,384,1280]{3,2,1,0:T(8,128)(2,1)S(1)}, bf16[1,2,384,1280]{3,2,1,0:T(8,128)(2,1)S(1)}, u32[]{:S(2)}, u32[]{:S(2)}) collective-permute-start(bf16[1,2,384,1280]{3,2,1,0:T(8,128)(2,1)S(1)} %collective-permute-done.3.refs_1_), channel_id=1, source_target_pairs={{0,1},{1,0},{2,3},{3,2},{4,5},{5,4},{6,7},{7,6},{8,9},{9,8},{10,11... | collective-permute-start | bytes 5898248 | tf_op jit(solution)/shard_map/ppermute | solution.py:439
  463.4 7.3 %collective-permute-start.7 = (f32[8,12,384]{2,1,0:T(8,128)S(1)}, f32[8,12,384]{2,1,0:T(8,128)S(1)}, u32[]{:S(2)}, u32[]{:S(2)}) collective-permute-start(f32[8,12,384]{2,1,0:T(8,128)S(1)} %copy-done.4), channel_id=1, source_target_pairs={{0,8},{8,0},{1,9},{9,1},{2,10},{10,2},{3,11},{11,3},{4,12},{12,4},... | collective-permute-start | bytes 442376 | tf_op jit(solution)/shard_map/ppermute | solution.py:436
  470.7 2.0 copy-start.13
  470.7 2.6 copy-start.12
  470.7 2.0 copy-start.9
  596.6 3.2 copy-start.1
  599.9 2.8 copy-start.2
Sparse Core Ops, SparseCore 0:
  160.0 48.4 all-gather.2
  277.3 104.8 reduce-scatter.2
  385.6 104.3 reduce-scatter.4

commit v3 on v2

v3 whole, which is shorter than its diff:
```python
import functools

import jax
import jax.numpy as jnp
from jax import lax
from jax.experimental import pallas as pl
from jax.experimental.pallas import tpu as pltpu
from jax.sharding import PartitionSpec as P


F32 = jnp.float32
BF16 = jnp.bfloat16
SLICE = 128
VMEM_LIMIT = 64_000_000
MESH = pl.DeviceIdType.MESH
NT = (((1,), (1,)), ((), ()))
TN = (((0,), (0,)), ((), ()))


def dot(a, b):
    return jnp.dot(a, b, preferred_element_type=F32)


def dot_nt(a, b):
    return lax.dot_general(a, b, NT, preferred_element_type=F32)


def dot_tn(a, b):
    return lax.dot_general(a, b, TN, preferred_element_type=F32)


def swiglu_parts(one, three, grad_hidden):
    sig = jax.nn.sigmoid(one)
    silu = one * sig
    dh = grad_hidden.astype(BF16).astype(F32)
    hidden = (silu * three).astype(BF16)
    da_one = (dh * three * (sig + silu * (1.0 - sig))).astype(BF16)
    da_three = (dh * silu).astype(BF16)
    return hidden, da_one, da_three


def params(axes):
    return pltpu.CompilerParams(dimension_semantics=("arbitrary",) * axes, vmem_limit_bytes=VMEM_LIMIT)


def gather_kernel(ep_size, x_ref, dy_ref, meta_ref, near_x_ref, near_y_ref, other_own_ref, other_x_ref, other_y_ref,
                  far_own_ref, far_other_ref, meta_all_ref, dy_out_ref, mine, mine_dy, mine_meta,
                  load_sem, store_sem, send_sem, recv_sem):
    me = lax.axis_index("ep")
    core_peer = me + 1 - 2 * (me % 2)
    x_peer = me + 2 - 4 * ((me // 2) % 2)
    y_peer = me + 4 - 8 * (me // 4)
    z_peer = 1 - lax.axis_index("tp")

    barrier = pltpu.get_barrier_semaphore()
    for k in range(1, ep_size):
        pl.semaphore_signal(barrier, inc=1, device_id={"ep": (me + k) % ep_size}, device_id_type=MESH)
    pl.semaphore_signal(barrier, inc=1, device_id={"tp": z_peer}, device_id_type=MESH)

    loads = [pltpu.make_async_copy(x_ref, mine, load_sem.at[0]),
             pltpu.make_async_copy(meta_ref, mine_meta, load_sem.at[1]),
             pltpu.make_async_copy(dy_ref, mine_dy, load_sem.at[2])]
    for copy in loads:
        copy.start()
    for copy in loads:
        copy.wait()
    stores = [pltpu.make_async_copy(mine_dy, dy_out_ref, store_sem.at[0]),
              pltpu.make_async_copy(mine_meta, meta_all_ref.at[me], store_sem.at[1])]
    pl.semaphore_wait(barrier, ep_size)

    half = x_ref.shape[0] // 2
    low, high = pl.ds(0, half), pl.ds(half, half)
    started = []

    def send(device, src, dst):
        n = len(started)
        copy = pltpu.make_async_remote_copy(src_ref=src, dst_ref=dst, send_sem=send_sem.at[n], recv_sem=recv_sem.at[n],
                                            device_id=device, device_id_type=MESH)
        copy.start()
        started.append(copy)
        return copy

    to_x, to_y, to_core = {"ep": x_peer}, {"ep": y_peer}, {"ep": core_peer}
    from_x_low = send(to_x, mine.at[low], near_x_ref.at[0, low])
    from_y_high = send(to_y, mine.at[high], near_y_ref.at[0, high])
    from_z = send({"tp": z_peer}, mine, far_own_ref.at[0])
    from_x_high = send(to_x, mine.at[high], near_x_ref.at[0, high])
    from_y_low = send(to_y, mine.at[low], near_y_ref.at[0, low])
    waiting = [send({"ep": (me + k) % ep_size}, mine_meta, meta_all_ref.at[me]) for k in range(1, ep_size)]
    waiting.append(send(to_core, mine, other_own_ref.at[0]))
    for copy in stores:
        copy.start()
    from_x_low.wait_recv()
    corner_low = send(to_y, near_x_ref.at[0, low], near_y_ref.at[1, low])
    waiting.append(send(to_core, near_x_ref.at[0, low], other_x_ref.at[0, low]))
    from_y_high.wait_recv()
    corner_high = send(to_x, near_y_ref.at[0, high], near_y_ref.at[1, high])
    waiting.append(send(to_core, near_y_ref.at[0, high], other_y_ref.at[0, high]))
    from_x_high.wait_recv()
    waiting.append(send(to_core, near_x_ref.at[0, high], other_x_ref.at[0, high]))
    from_y_low.wait_recv()
    waiting.append(send(to_core, near_y_ref.at[0, low], other_y_ref.at[0, low]))
    from_z.wait_recv()
    waiting.append(send(to_core, far_own_ref.at[0], far_other_ref.at[0]))
    corner_low.wait_recv()
    waiting.append(send(to_core, near_y_ref.at[1, low], other_y_ref.at[1, low]))
    corner_high.wait_recv()
    waiting.append(send(to_core, near_y_ref.at[1, high], other_y_ref.at[1, high]))
    for copy in waiting:
        copy.wait_recv()
    for copy in started:
        copy.wait_send()
    for copy in stores:
        copy.wait()


def gather_layer(tokens, grad_y, meta, ep_size):
    rows, dim = tokens.shape
    one = jax.ShapeDtypeStruct((1, rows, dim), tokens.dtype)
    two = jax.ShapeDtypeStruct((2, rows, dim), tokens.dtype)
    anywhere = pl.BlockSpec(memory_space=pl.ANY)
    copies = 5 + (ep_size - 1) + 1 + 2 + 7
    return pl.pallas_call(
        functools.partial(gather_kernel, ep_size),
        in_specs=[anywhere] * 3, out_specs=[anywhere] * 9,
        out_shape=[one, two, one, one, two, one, one, jax.ShapeDtypeStruct((ep_size,) + meta.shape, meta.dtype),
                   jax.ShapeDtypeStruct(grad_y.shape, grad_y.dtype)],
        scratch_shapes=[pltpu.VMEM((rows, dim), tokens.dtype), pltpu.VMEM((rows, dim), grad_y.dtype),
                        pltpu.VMEM(meta.shape, meta.dtype), pltpu.SemaphoreType.DMA((3,)), pltpu.SemaphoreType.DMA((2,)),
                        pltpu.SemaphoreType.DMA((copies,)), pltpu.SemaphoreType.DMA((copies,))],
        compiler_params=pltpu.CompilerParams(collective_id=0, has_side_effects=True), name="gather",
        cost_estimate=pl.CostEstimate(flops=30_000_000_000, bytes_accessed=ep_size * rows * dim * 8, transcendentals=0),
    )(tokens, grad_y, meta)


def ep_of(source, ids):
    core = jnp.where(source < 4, ids[1] % 2, 1 - ids[1] % 2)
    return 2 * jnp.bitwise_xor(ids[1] // 2, source % 4) + core


def stream(refs, per_step, buffer, sem):
    blocks = [(ref, i) for ref in refs for i in range(ref.shape[0])]
    step = pl.program_id(0)
    steps = len(blocks) // per_step

    def copies(k):
        return [pltpu.make_async_copy(ref.at[i], buffer.at[k % 2, n], sem.at[k % 2, n])
                for n, (ref, i) in enumerate(blocks[k * per_step:(k + 1) * per_step])]

    @pl.when(step == 0)
    def _():
        for copy in copies(0):
            copy.start()

    for k in range(steps):
        @pl.when(step == k)
        def _():
            if k + 1 < steps:
                for copy in copies(k + 1):
                    copy.start()
            for copy in copies(k):
                copy.wait()

    return step % 2


def lay_rows(local, cap, got, out_ref):
    for l in range(local):
        out_ref[l] = got[l * cap:(l + 1) * cap].astype(BF16)


def gate_rows(meta, ids, rows, top_k):
    tokens = meta.shape[1]
    base = (ids[1] * rows).astype(F32)
    row_ids = lax.broadcasted_iota(jnp.int32, (rows, tokens), 0).astype(F32) + base
    gates = jnp.zeros((rows, tokens), F32)
    for j in range(top_k):
        gates = jnp.where(meta[j][None, :] == row_ids, meta[top_k + j][None, :], gates)
    return gates, jnp.where(gates != 0.0, 1.0, 0.0).astype(BF16)


def dispatch_x_kernel(local, cap, top_k, ids, *refs):
    *blocks, meta_ref, xd_ref, select_ref, gate_ref, buffer, sem = refs
    slot = stream(blocks, 1, buffer, sem)
    gates, select = gate_rows(meta_ref[0], ids, local * cap, top_k)
    select_ref[0] = select
    gate_ref[0] = jnp.broadcast_to(jnp.sum(gates, axis=1, keepdims=True), gate_ref.shape[1:])
    lay_rows(local, cap, dot(select, buffer[slot, 0]), xd_ref)


def dispatch_x(ids, blocks, meta_all, local, cap, top_k):
    tokens, dim = blocks[0].shape[-2:]
    groups = sum(block.shape[0] for block in blocks)
    rows = local * cap
    return pl.pallas_call(
        functools.partial(dispatch_x_kernel, local, cap, top_k),
        grid_spec=pltpu.PrefetchScalarGridSpec(
            num_scalar_prefetch=1, grid=(groups,),
            in_specs=[pl.BlockSpec(memory_space=pl.ANY)] * len(blocks)
            + [pl.BlockSpec((1, 2 * top_k, tokens), lambda s, ids: (ep_of(s, ids), 0, 0))],
            out_specs=[pl.BlockSpec((local, cap, dim), lambda s, ids: (0, s, 0)),
                       pl.BlockSpec((1, rows, tokens), lambda s, ids: (s, 0, 0)),
                       pl.BlockSpec((1, rows, 128), lambda s, ids: (s, 0, 0))],
            scratch_shapes=[pltpu.VMEM((2, 1, tokens, dim), BF16), pltpu.SemaphoreType.DMA((2, 1))]),
        out_shape=[jax.ShapeDtypeStruct((local, groups * cap, dim), BF16),
                   jax.ShapeDtypeStruct((groups, rows, tokens), BF16), jax.ShapeDtypeStruct((groups, rows, 128), F32)],
        compiler_params=params(1), name="dispatch_x",
        cost_estimate=pl.CostEstimate(flops=2 * groups * rows * tokens * dim,
                                      bytes_accessed=groups * (tokens + rows) * dim * 2, transcendentals=0),
    )(ids, *blocks, meta_all)


def dispatch_dy_kernel(local, cap, ids, dy_ref, select_ref, gate_ref, qd_ref):
    lay_rows(local, cap, dot(select_ref[0], dy_ref[0]) * gate_ref[0][:, :1], qd_ref)


def dispatch_dy(ids, dy_all, select, gate, local, cap):
    groups, tokens, dim = dy_all.shape
    rows = local * cap
    by_place = lambda s, ids: (s, 0, 0)
    return pl.pallas_call(
        functools.partial(dispatch_dy_kernel, local, cap),
        grid_spec=pltpu.PrefetchScalarGridSpec(
            num_scalar_prefetch=1, grid=(groups,),
            in_specs=[pl.BlockSpec((1, tokens, dim), lambda s, ids: (ep_of(s, ids), 0, 0)),
                      pl.BlockSpec((1, rows, tokens), by_place), pl.BlockSpec((1, rows, 128), by_place)],
            out_specs=pl.BlockSpec((local, cap, dim), lambda s, ids: (0, s, 0))),
        out_shape=jax.ShapeDtypeStruct((local, groups * cap, dim), BF16), compiler_params=params(1), name="dispatch_dy",
        cost_estimate=pl.CostEstimate(flops=2 * groups * rows * tokens * dim,
                                      bytes_accessed=groups * (tokens + rows) * dim * 2, transcendentals=0),
    )(ids, dy_all, select, gate)


def dispatch_far_kernel(local, cap, top_k, ids, *refs):
    *blocks, dy_ref, meta_ref, xd_ref, qd_ref, buffer, sem = refs
    slot = stream(blocks, 1, buffer, sem)
    gates, select = gate_rows(meta_ref[0], ids, local * cap, top_k)
    lay_rows(local, cap, dot(select, buffer[slot, 0]), xd_ref)
    lay_rows(local, cap, dot(select, dy_ref[0]) * jnp.sum(gates, axis=1, keepdims=True), qd_ref)


def dispatch_far(ids, blocks, dy_all, meta_all, local, cap, top_k):
    groups, tokens, dim = dy_all.shape
    by_ep = lambda s, ids: (ep_of(s, ids), 0, 0)
    out = jax.ShapeDtypeStruct((local, groups * cap, dim), BF16)
    out_spec = pl.BlockSpec((local, cap, dim), lambda s, ids: (0, s, 0))
    return pl.pallas_call(
        functools.partial(dispatch_far_kernel, local, cap, top_k),
        grid_spec=pltpu.PrefetchScalarGridSpec(
            num_scalar_prefetch=1, grid=(groups,),
            in_specs=[pl.BlockSpec(memory_space=pl.ANY)] * len(blocks)
            + [pl.BlockSpec((1, tokens, dim), by_ep), pl.BlockSpec((1, 2 * top_k, tokens), by_ep)],
            out_specs=[out_spec, out_spec],
            scratch_shapes=[pltpu.VMEM((2, 1, tokens, dim), BF16), pltpu.SemaphoreType.DMA((2, 1))]),
        out_shape=[out, out], compiler_params=params(1), name="dispatch_far",
        cost_estimate=pl.CostEstimate(flops=4 * groups * local * cap * tokens * dim,
                                      bytes_accessed=groups * (tokens + local * cap) * dim * 4, transcendentals=0),
    )(ids, *blocks, dy_all, meta_all)


def forward_kernel(cap, x_ref, w1_ref, w3_ref, w2_ref, o_ref, h_ref, a1_ref, a3_ref):
    rows = x_ref.shape[-2]
    half = rows // 2
    per = half // cap
    for part in range(2):
        span = slice(part * half, (part + 1) * half)
        x = x_ref[0, span]
        one, three = dot(x, w1_ref[0]), dot(x, w3_ref[0])
        hidden = (one * jax.nn.sigmoid(one) * three).astype(BF16)
        h_ref[0, span] = hidden
        a1_ref[0, span] = one
        a3_ref[0, span] = three
        out = dot(hidden, w2_ref[0])
        for s in range(per):
            o_ref[part * per + s] = out[s * cap:(s + 1) * cap].astype(BF16)


def forward(xd, w1, w3, w2, cap):
    local, rows, dim = xd.shape
    ff = w1.shape[-1]
    groups = rows // cap
    by_expert = lambda l: (l, 0, 0)
    hid_spec = pl.BlockSpec((1, rows, ff), by_expert)
    wide, tall = pl.BlockSpec((1, dim, ff), by_expert), pl.BlockSpec((1, ff, dim), by_expert)
    proj = jax.ShapeDtypeStruct((local, rows, ff), F32)
    return pl.pallas_call(
        functools.partial(forward_kernel, cap), grid=(local,),
        in_specs=[pl.BlockSpec((1, rows, dim), by_expert), wide, wide, tall],
        out_specs=[pl.BlockSpec((groups, cap, dim), lambda l: (0, l, 0)), hid_spec, hid_spec, hid_spec],
        out_shape=[jax.ShapeDtypeStruct((groups, local * cap, dim), BF16), jax.ShapeDtypeStruct((local, rows, ff), BF16),
                   proj, proj],
        compiler_params=params(1), name="forward",
        cost_estimate=pl.CostEstimate(flops=6 * local * rows * dim * ff,
                                      bytes_accessed=local * (4 * rows * dim + 10 * rows * ff + 6 * dim * ff),
                                      transcendentals=local * rows * ff),
    )(xd, w1, w3, w2)


def backward_kernel(cap, q_ref, a1_ref, a3_ref, w1_ref, w3_ref, w2_ref, dr_ref, da1_ref, da3_ref):
    rows = q_ref.shape[-2]
    half = rows // 2
    per = half // cap
    for part in range(2):
        span = slice(part * half, (part + 1) * half)
        _, da_one, da_three = swiglu_parts(a1_ref[0, span], a3_ref[0, span], dot_nt(q_ref[0, span], w2_ref[0]))
        da1_ref[0, span] = da_one
        da3_ref[0, span] = da_three
        grad = dot_nt(da_one, w1_ref[0]) + dot_nt(da_three, w3_ref[0])
        for s in range(per):
            dr_ref[part * per + s] = grad[s * cap:(s + 1) * cap].astype(BF16)


def backward(qd, a1, a3, w1, w3, w2, cap):
    local, rows, dim = qd.shape
    ff = w1.shape[-1]
    groups = rows // cap
    by_expert = lambda l: (l, 0, 0)
    hid_spec = pl.BlockSpec((1, rows, ff), by_expert)
    wide, tall = pl.BlockSpec((1, dim, ff), by_expert), pl.BlockSpec((1, ff, dim), by_expert)
    hid = jax.ShapeDtypeStruct((local, rows, ff), BF16)
    return pl.pallas_call(
        functools.partial(backward_kernel, cap), grid=(local,),
        in_specs=[pl.BlockSpec((1, rows, dim), by_expert), hid_spec, hid_spec, wide, wide, tall],
        out_specs=[pl.BlockSpec((groups, cap, dim), lambda l: (0, l, 0)), hid_spec, hid_spec],
        out_shape=[jax.ShapeDtypeStruct((groups, local * cap, dim), BF16), hid, hid],
        compiler_params=params(1), name="backward",
        cost_estimate=pl.CostEstimate(flops=6 * local * rows * dim * ff,
                                      bytes_accessed=local * (4 * rows * dim + 12 * rows * ff + 6 * dim * ff),
                                      transcendentals=local * rows * ff),
    )(qd, a1, a3, w1, w3, w2)


def grads_kernel(ids, x_ref, q_ref, xp_ref, qp_ref, h_ref, da1_ref, da3_ref, w1_ref, w3_ref, w2_ref,
                 g1_ref, g3_ref, g2_ref, rows_x, rows_q, hid, da_one, da_three, tall):
    rows = x_ref.shape[-2]
    half = rows // 2
    part = ids[0]
    width = g1_ref.shape[1]
    columns = pl.ds(pl.multiple_of(part * width, 128), width)
    ff = w1_ref.shape[-1]
    reach = tall.shape[0]
    chunk = pl.ds(pl.multiple_of(part * (ff - reach), 128), reach)
    rows_x[:rows] = x_ref[0, :, columns]
    rows_x[rows:] = xp_ref[0, :, columns]
    rows_q[:rows] = q_ref[0]
    rows_q[rows:] = qp_ref[0]
    hid[:rows] = h_ref[0]
    da_one[:rows] = da1_ref[0]
    da_three[:rows] = da3_ref[0]
    for piece in range(2):
        span = slice(piece * half, (piece + 1) * half)
        dest = slice(rows + piece * half, rows + (piece + 1) * half)
        x = xp_ref[0, span]
        hidden, one, three = swiglu_parts(dot(x, w1_ref[0]), dot(x, w3_ref[0]), dot_nt(qp_ref[0, span], w2_ref[0]))
        hid[dest] = hidden
        da_one[dest] = one
        da_three[dest] = three
    g1_ref[0] = dot_tn(rows_x[...], da_one[...]).astype(BF16)
    g3_ref[0] = dot_tn(rows_x[...], da_three[...]).astype(BF16)
    height = g2_ref.shape[1]
    tall[...] = dot_tn(hid[:, chunk], rows_q[...])
    skip = pl.multiple_of(part * (height - (ff - reach)), 8)
    g2_ref[0] = tall[pl.ds(skip, height)].astype(BF16)


def expert_grads(ids, xd, qd, xp, qp, h, da1, da3, w1, w3, w2, parts):
    local, rows, dim = xd.shape
    ff = w1.shape[-1]
    by_expert = lambda l, ids: (l, 0, 0)
    row_spec, hid_spec = pl.BlockSpec((1, rows, dim), by_expert), pl.BlockSpec((1, rows, ff), by_expert)
    wide, tall = pl.BlockSpec((1, dim, ff), by_expert), pl.BlockSpec((1, ff, dim), by_expert)
    g1 = jax.ShapeDtypeStruct((local, dim // parts, ff), BF16)
    g2 = jax.ShapeDtypeStruct((local, ff // parts, dim), BF16)
    g1_spec, g2_spec = pl.BlockSpec((1, dim // parts, ff), by_expert), pl.BlockSpec((1, ff // parts, dim), by_expert)
    reach = -(-(ff // parts) // 128) * 128
    return pl.pallas_call(
        grads_kernel,
        grid_spec=pltpu.PrefetchScalarGridSpec(
            num_scalar_prefetch=1, grid=(local,),
            in_specs=[row_spec, row_spec, row_spec, row_spec, hid_spec, hid_spec, hid_spec, wide, wide, tall],
            out_specs=[g1_spec, g1_spec, g2_spec],
            scratch_shapes=[pltpu.VMEM((2 * rows, dim // parts), BF16), pltpu.VMEM((2 * rows, dim), BF16)]
            + [pltpu.VMEM((2 * rows, ff), BF16)] * 3 + [pltpu.VMEM((reach, dim), F32)]),
        out_shape=[g1, g1, g2], compiler_params=params(1), name="grads",
        cost_estimate=pl.CostEstimate(flops=12 * local * rows * dim * ff,
                                      bytes_accessed=local * (8 * rows * dim + 6 * rows * ff + 9 * dim * ff),
                                      transcendentals=local * rows * ff),
    )(ids, xd, qd, xp, qp, h, da1, da3, w1, w3, w2)


def shared_kernel(ids, *refs):
    *blocks, dy_one_ref, dy_two_ref, wa_ref, wa_far_ref, w2_ref, w2_far_ref, h_ref, da_ref, g_ref, g_far_ref, buffer, sem = refs
    slot = stream(blocks, 2, buffer, sem)

    @pl.when(pl.program_id(0) == 0)
    def _():
        g_ref[...] = jnp.zeros_like(g_ref)
        g_far_ref[...] = jnp.zeros_like(g_far_ref)

    _, pair, tokens, dim = buffer.shape
    x = buffer[slot].reshape(pair * tokens, dim)
    dy = jnp.concatenate([dy_one_ref[0], dy_two_ref[0]], axis=0)
    for half, (grad_ref, up_ref, down_ref) in enumerate(((g_ref, wa_ref, w2_ref), (g_far_ref, wa_far_ref, w2_far_ref))):
        proj = dot(x, up_ref[...])
        hidden, da_one, da_three = swiglu_parts(proj[:, :SLICE], proj[:, SLICE:], dot_nt(dy, down_ref[...]))
        da = jnp.concatenate([da_one, da_three], axis=1)
        h_ref[:, :, half * SLICE:(half + 1) * SLICE] = hidden.reshape(pair, tokens, SLICE)
        da_ref[:, :, 2 * half * SLICE:2 * (half + 1) * SLICE] = da.reshape(pair, tokens, 2 * SLICE)
        grad_ref[:2 * SLICE] += dot_tn(da, x)
        grad_ref[2 * SLICE:] += dot_tn(hidden, dy)


def shared_expert(ids, blocks, dy_all, weights):
    groups, tokens, dim = dy_all.shape
    by_pair, fixed = lambda s, ids: (s, 0, 0), lambda s, ids: (0, 0)
    grad = jax.ShapeDtypeStruct((3 * SLICE, dim), F32)
    return pl.pallas_call(
        shared_kernel,
        grid_spec=pltpu.PrefetchScalarGridSpec(
            num_scalar_prefetch=1, grid=(groups // 2,),
            in_specs=[pl.BlockSpec(memory_space=pl.ANY)] * len(blocks)
            + [pl.BlockSpec((1, tokens, dim), lambda s, ids: (ep_of(2 * s, ids), 0, 0)),
               pl.BlockSpec((1, tokens, dim), lambda s, ids: (ep_of(2 * s + 1, ids), 0, 0)),
               ] + [pl.BlockSpec(weight.shape, fixed) for weight in weights],
            out_specs=[pl.BlockSpec((2, tokens, 2 * SLICE), by_pair), pl.BlockSpec((2, tokens, 4 * SLICE), by_pair),
                       pl.BlockSpec(grad.shape, fixed), pl.BlockSpec(grad.shape, fixed)],
            scratch_shapes=[pltpu.VMEM((2, 2, tokens, dim), BF16), pltpu.SemaphoreType.DMA((2, 2))]),
        out_shape=[jax.ShapeDtypeStruct((groups, tokens, 2 * SLICE), BF16),
                   jax.ShapeDtypeStruct((groups, tokens, 4 * SLICE), BF16), grad, grad],
        compiler_params=params(1), name="shared",
        cost_estimate=pl.CostEstimate(flops=18 * groups * tokens * dim * SLICE,
                                      bytes_accessed=4 * groups * tokens * dim, transcendentals=0),
    )(ids, *blocks, dy_all, dy_all, *weights)


def gate_matrix(meta, ids, rows, top_k):
    tokens = meta.shape[0]
    base = (ids[1] * rows).astype(F32)
    row_ids = lax.broadcasted_iota(jnp.int32, (tokens, rows), 1).astype(F32) + base
    gates = jnp.zeros((tokens, rows), F32)
    for j in range(top_k):
        gates = jnp.where(meta[:, j:j + 1] == row_ids, meta[:, top_k + j:top_k + j + 1], gates)
    return gates


def combine_out_kernel(top_k, ids, meta_ref, o_ref, h_ref, w2_ref, w2_far_ref, y_ref):
    tokens = h_ref.shape[1]
    gates = gate_matrix(meta_ref[0].T, ids, o_ref.shape[1], top_k)
    high = gates.astype(BF16)
    rest = gates - high.astype(F32)
    mid = rest.astype(BF16)
    low = (rest - mid.astype(F32)).astype(BF16)
    sums = dot(jnp.concatenate([high, mid, low], axis=0), o_ref[0])
    width = w2_ref.shape[0]
    y_ref[0] = (sums[:tokens] + sums[tokens:2 * tokens] + sums[2 * tokens:]
                + dot(h_ref[0, :, :width], w2_ref[...]) + dot(h_ref[0, :, width:], w2_far_ref[...]))


def combine_back_kernel(top_k, ids, meta_ref, dr_ref, da_ref, wa_ref, wa_far_ref, dx_ref):
    gates = gate_matrix(meta_ref[0].T, ids, dr_ref.shape[1], top_k)
    select = jnp.where(gates != 0.0, 1.0, 0.0).astype(BF16)
    width = wa_ref.shape[1]
    dx_ref[0] = (dot(select, dr_ref[0]) + dot_nt(da_ref[0, :, :width], wa_ref[...])
                 + dot_nt(da_ref[0, :, width:], wa_far_ref[...]))


def combine(kernel, ids, meta_all, returned, hidden, weights, top_k, passes):
    groups, rows, dim = returned.shape
    tokens, width = hidden.shape[1:]
    by_place = lambda s, ids: (s, 0, 0)
    by_ep = lambda s, ids: (ep_of(s, ids), 0, 0)
    return pl.pallas_call(
        functools.partial(kernel, top_k),
        grid_spec=pltpu.PrefetchScalarGridSpec(
            num_scalar_prefetch=1, grid=(groups,),
            in_specs=[pl.BlockSpec((1, 2 * top_k, tokens), by_ep), pl.BlockSpec((1, rows, dim), by_place),
                      pl.BlockSpec((1, tokens, width), by_place)]
            + [pl.BlockSpec(weight.shape, lambda s, ids: (0, 0)) for weight in weights],
            out_specs=pl.BlockSpec((1, tokens, dim), by_ep)),
        out_shape=jax.ShapeDtypeStruct((groups, tokens, dim), F32), compiler_params=params(1),
        cost_estimate=pl.CostEstimate(flops=2 * passes * groups * tokens * rows * dim,
                                      bytes_accessed=groups * (2 * rows + 4 * tokens) * dim, transcendentals=0),
    )(ids, meta_all, returned, hidden, *weights)


def finish_kernel(ids, near_ref, corner_ref, other_near_ref, other_corner_ref, g1_ref, g3_ref, g2_ref):
    def lay(ref):
        g1_ref[...] = ref[0, :SLICE].T
        g3_ref[...] = ref[0, SLICE:2 * SLICE].T
        g2_ref[...] = ref[0, 2 * SLICE:]

    device = pl.program_id(0)
    same = device % 2 == ids[1] % 2
    near = jnp.bitwise_xor(device // 2, ids[1] // 2) < 3
    pl.when(same & near)(lambda: lay(near_ref))
    pl.when(same & jnp.logical_not(near))(lambda: lay(corner_ref))
    pl.when(jnp.logical_not(same) & near)(lambda: lay(other_near_ref))
    pl.when(jnp.logical_not(same) & jnp.logical_not(near))(lambda: lay(other_corner_ref))


def finish(ids, slices, ff):
    _, height, dim = slices[0].shape
    near = pl.BlockSpec((1, height, dim), lambda e, ids: (jnp.minimum(jnp.bitwise_xor(e // 2, ids[1] // 2), 2), 0, 0))
    corner = pl.BlockSpec((1, height, dim), lambda e, ids: (0, 0, 0))
    wide, tall = jax.ShapeDtypeStruct((dim, ff), BF16), jax.ShapeDtypeStruct((ff, dim), BF16)
    return pl.pallas_call(
        finish_kernel,
        grid_spec=pltpu.PrefetchScalarGridSpec(
            num_scalar_prefetch=1, grid=(ff // SLICE,), in_specs=[near, corner, near, corner],
            out_specs=[pl.BlockSpec((dim, SLICE), lambda e, ids: (0, e)), pl.BlockSpec((dim, SLICE), lambda e, ids: (0, e)),
                       pl.BlockSpec((SLICE, dim), lambda e, ids: (e, 0))]),
        out_shape=[wide, wide, tall], compiler_params=params(1), name="finish",
        cost_estimate=pl.CostEstimate(flops=1_000_000_000, bytes_accessed=16 * height * dim * 2, transcendentals=0),
    )(ids, *slices)


def solution(mesh):
    ep_size, tp_size = mesh.shape["ep"], mesh.shape["tp"]
    row_spec = P(("ep", "tp"), None)
    expert_spec = P("ep", None, None)
    expert_grad_spec = P("ep", "tp", None)
    swap = [(0, 1), (1, 0)]
    cores, along_x, along_y = ([(i, i ^ bit) for i in range(ep_size)] for bit in (1, 2, 4))

    def move(value, axis, route):
        return lax.ppermute(value, axis, route)

    def device_fn(tokens, grad_y, expert_ids, gate_vals, slot_ids,
                  shared_w1, shared_w3, shared_w2, expert_w1, expert_w3, expert_w2):
        rows_dev, dim = tokens.shape
        top_k = expert_ids.shape[1]
        local = expert_w1.shape[0]
        experts = local * ep_size
        cap = (2 * rows_dev * top_k + experts - 1) // experts
        tp_id, ep_id = lax.axis_index("tp"), lax.axis_index("ep")
        ids = jnp.stack([tp_id, ep_id]).astype(jnp.int32)

        pos = jnp.where(slot_ids >= 0, expert_ids * cap + slot_ids, -1).astype(F32)
        meta = jnp.concatenate([pos.T, gate_vals.T], axis=0)
        near_x, near_y, *others, far_own, far_other, meta_all, late_dy = gather_layer(tokens, grad_y, meta, ep_size)
        blocks = (tokens[None], near_x, near_y, *others)
        dy_all = lax.all_gather(late_dy, "ep")
        far_dy_all = lax.all_gather(move(late_dy, "tp", swap), "ep")
        far_meta = move(meta_all, "tp", swap)
        far_x, far_y = move(near_x, "tp", swap), move(near_y, "tp", swap)
        far_blocks = (far_own, far_x, far_y, far_other, move(far_x, "ep", cores), move(far_y, "ep", cores))

        ff = shared_w1.shape[1]
        padded = ep_size * SLICE
        wide_pad = ((0, 0), (0, padded - ff))
        start = ep_id * SLICE
        w1s = lax.dynamic_slice(jnp.pad(shared_w1, wide_pad), (0, start), (dim, SLICE))
        w3s = lax.dynamic_slice(jnp.pad(shared_w3, wide_pad), (0, start), (dim, SLICE))
        w2s = lax.dynamic_slice(jnp.pad(shared_w2, ((0, padded - ff), (0, 0))), (start, 0), (SLICE, dim))
        wa_own = jnp.concatenate([w1s, w3s], axis=1)
        wide = (wa_own, move(wa_own, "tp", swap))
        tall = (w2s, move(w2s, "tp", swap))

        sizes = (local, cap, top_k)
        xd, rows_select, rows_gate = dispatch_x(ids, blocks, meta_all, *sizes)
        o, h, a1, a3 = forward(xd, expert_w1, expert_w3, expert_w2, cap)
        qd = dispatch_dy(ids, dy_all, rows_select, rows_gate, local, cap)
        sh, sda, shared_grad, shared_far = shared_expert(ids, blocks, dy_all, wide + tall)
        y_part = combine(combine_out_kernel, ids, meta_all, o, sh, tall, top_k, 3)
        y_sum = lax.psum_scatter(y_part.reshape(-1, dim), "ep", scatter_dimension=0, tiled=True)
        dr, da1, da3 = backward(qd, a1, a3, expert_w1, expert_w3, expert_w2, cap)
        dx_part = combine(combine_back_kernel, ids, meta_all, dr, sda, wide, top_k, 1)
        dx_sum = lax.psum_scatter(dx_part.reshape(-1, dim), "ep", scatter_dimension=0, tiled=True)

        xp, qp = dispatch_far(ids, far_blocks, far_dy_all, far_meta, *sizes)
        g1, g3, g2 = expert_grads(ids, xd, qd, xp, qp, h, da1, da3, expert_w1, expert_w3, expert_w2, tp_size)

        shared_grad = shared_grad + move(shared_far, "tp", swap)
        mine = shared_grad.astype(BF16)
        from_x, from_y = move(mine, "ep", along_x), move(mine, "ep", along_y)
        chips = jnp.stack([mine, from_x, from_y])
        corner = move(from_x, "ep", along_y)
        slices = (chips, corner[None], move(chips, "ep", cores), move(corner, "ep", cores)[None])
        sg1, sg3, sg2 = finish(ids, slices, ff)
        out_y = (tokens.astype(F32) + y_sum).astype(BF16)
        grad_tokens = (grad_y.astype(F32) + dx_sum).astype(BF16)
        return out_y, grad_tokens, sg1, sg3, sg2, g1, g3, g2

    return jax.shard_map(
        device_fn, mesh=mesh,
        in_specs=(row_spec, row_spec, row_spec, row_spec, row_spec,
                  P(None, "tp"), P(None, "tp"), P("tp", None), expert_spec, expert_spec, expert_spec),
        out_specs=(row_spec, row_spec, P(None, "tp"), P(None, "tp"), P("tp", None),
                   expert_grad_spec, expert_grad_spec, expert_grad_spec),
        check_vma=False)
```

time: 613 us -> 580 us (0.946)
  waiting for transfers between devices: 176 us -> 145 us
  local copies, waits for them, and re-layouts: 19 us -> 5.75 us
  Pallas kernels: 381 us -> 389 us
    pallas_call x5 -> x7, Pallas kernels: 160 us -> 194 us  [the longest x1 57.3 us: backward(): pl.pallas_call(functools.partial(backward_kernel, cap), grid=(local,), in...]
    ppermute x8 -> x14, waiting for transfers between devices: 176 us -> 145 us  [move(): return lax.ppermute(value, axis, route)]
    pallas_call x1, Pallas kernels: 73.9 us -> 42.5 us  [gather_layer(): pl.pallas_call(functools.partial(gather_kernel, ep_size), in_specs=[anywh...]
    ppermute x8 -> x14, starting transfers between devices: 9.75 us -> 14.2 us  [move(): return lax.ppermute(value, axis, route)]
  transfers between devices with their start and end apart: 11 -> 18, of which waited for: 4 -> 5; matrix products, arithmetic and copies ran while one was open for 3% -> 1% of each run, Pallas kernels for 59% -> 60%
where the time goes in v3:
time: 580 us; the launch traced here: 578 us
  Pallas kernels  389 us (67%)
  waiting for transfers between devices  145 us (25%)
  starting transfers between devices  14.6 us (3%)
  between operations  14 us (2%)
  other arithmetic  10.6 us (2%)
    ppermute x14, waiting for transfers between devices, move(): return lax.ppermute(value, axis, route)  145 us
    pallas_call x1, Pallas kernels, expert_grads(): pl.pallas_call(grads_kernel, grid_spec=pltpu.PrefetchScalarGridSpec(num_s...  91 us
    pallas_call x2, Pallas kernels, combine(): pl.pallas_call(functools.partial(kernel, top_k), grid_spec=pltpu.Prefetch...  61.1 us
    pallas_call x1, Pallas kernels, backward(): pl.pallas_call(functools.partial(backward_kernel, cap), grid=(local,), in...  57.3 us
    pallas_call x1, Pallas kernels, forward(): pl.pallas_call(functools.partial(forward_kernel, cap), grid=(local,), in_...  49.4 us
    pallas_call x1, Pallas kernels, gather_layer(): pl.pallas_call(functools.partial(gather_kernel, ep_size), in_specs=[anywh...  42.5 us
    pallas_call x1, Pallas kernels, shared_expert(): pl.pallas_call(shared_kernel, grid_spec=pltpu.PrefetchScalarGridSpec(num_...  23 us
    pallas_call x1, Pallas kernels, dispatch_far(): pl.pallas_call(functools.partial(dispatch_far_kernel, local, cap, top_k),...  22.1 us
  transfers between devices with their start and end apart: 18, of which 5 were waited for; matrix products, arithmetic and copies ran while one was open for 1% of the time, Pallas kernels for 60%

profile of v3, /device:TPU:0, one launch (start us, length us, event | category | flops | bytes accessed | tf_op | source)
XLA Modules:
  0.0 578.2 jit_solution(17936503815778484105)
XLA Ops:
  7.2 0.0 all-gather.5.cloned.1.call-start
  7.2 0.7 convert_bitcast_fusion
  7.9 1.3 pad_maximum_fusion.2.meta_ref
  9.3 42.5 %gather.1 = (bf16[1,384,1280]{2,1,0:T(8,128)(2,1)}, bf16[2,384,1280]{2,1,0:T(8,128)(2,1)}, bf16[1,384,1280]{2,1,0:T(8,128)(2,1)}, bf16[1,384,1280]{2,1,0:T(8,128...) custom-call(bf16[384,1280]{1,0:T(8,128)(2,1)} %x_ref.1, ...), custom_call_target="tpu_custom_call" | custom-call | flops 30000001024 | bytes 31457280 | tf_op jit(solution)/shard_map/gather/pallas_call | solution.py:123
  51.8 0.0 all-gather.7.cloned.1.call-start
  51.8 1.6 collective-permute-start.12
  53.4 22.7 %collective-permute-done.12 = bf16[384,1280]{1,0:T(8,128)(2,1)S(1)} collective-permute-done((bf16[384,1280]{1,0:T(8,128)(2,1)}, bf16[384,1280]{1,0:T(8,128)(2,1)S(1)}, u32[]{:S(2)}, u32[]{:S(2)}) %collective-permute-start.12) | collective-permute-done | bytes 983072 | tf_op jit(solution)/shard_map/ppermute | solution.py:526
  76.1 0.9 copy-done.6
  77.1 0.0 reduce-scatter.3.cloned.1.call-start
  77.2 1.3 pad_dynamic-slice_fusion.1
  78.4 0.1 pad_maximum_fusion.1.refs_8_.wa_ref
  78.5 1.6 collective-permute-start
  80.1 0.1 pad_dynamic-slice_fusion.refs_10_.w2_ref
  80.2 0.5 collective-permute-start.1
  80.7 0.6 pad_add_fusion.ids
  81.3 16.6 %dispatch_x.1 = (bf16[8,576,1280]{2,1,0:T(8,128)(2,1)}, bf16[8,576,384]{2,1,0:T(8,128)(2,1)}, f32[8,576,128]{2,1,0:T(8,128)}) custom-call(s32[2]{0:T(128)} %pad_add_fusion.ids, bf16[1,384,1280]{2,1,0:T(8,128)(2,1)} %bitcast.22, bf16[1,384,1280]{2,1,0:T(8,128)(2,1)} %get-tuple-element.40.refs_1_, bf16[2,384,1280]{2,1,0:T(8,128)(2,1)} %get-tuple-element.41.refs_2_, ...), custom_call_target="tpu_custom_call" | custom-call | flops 4529848320 | bytes 19660800 | tf_op jit(solution)/shard_map/dispatch_x/pallas_call | solution.py:195
  97.9 49.4 %forward.1 = (bf16[8,576,1280]{2,1,0:T(8,128)(2,1)}, bf16[8,576,896]{2,1,0:T(8,128)(2,1)}, f32[8,576,896]{2,1,0:T(8,128)}, f32[8,576,896]{2,1,0:T(8,128)}) custom-call(bf16[8,576,1280]{2,1,0:T(8,128)(2,1)} %get-tuple-element.45.x_ref, bf16[8,1280,896]{2,1,0:T(8,128)(2,1)} %w1_ref.5, bf16[8,1280,896]{2,1,0:T(8,128)(2,1)} %w3_ref.5, bf16[8,896,1280]{2,1,0:T(8,128)(2,1)} %w2_ref.5), custom_call_target="tpu_custom_call" | custom-call | flops 31708938240 | bytes 119930880 | tf_op jit(solution)/shard_map/forward/pallas_call | solution.py:286
  147.4 0.7 copy-done.16
  148.0 0.2 copy-done.10
  148.3 23.0 %shared.1 = (bf16[8,384,256]{2,1,0:T(8,128)(2,1)}, bf16[8,384,512]{2,1,0:T(8,128)(2,1)}, f32[384,1280]{1,0:T(8,128)}, f32[384,1280]{1,0:T(8,128)}) custom-call(s32[2]{0:T(128)} %pad_add_fusion.ids, bf16[1,384,1280]{2,1,0:T(8,128)(2,1)} %bitcast.23, bf16[1,384,1280]{2,1,0:T(8,128)(2,1)} %get-tuple-element.40.refs_1_, ...), custom_call_target="tpu_custom_call" | custom-call | flops 9059696640 | bytes 15728640 | tf_op jit(solution)/shard_map/shared/pallas_call | solution.py:417
  171.3 36.4 %shard_map.170 = f32[8,384,1280]{2,1,0:T(8,128)} custom-call(s32[2]{0:T(128)} %pad_add_fusion.ids, f32[8,12,384]{2,1,0:T(8,128)} %get-tuple-element.39.refs_6_.meta_ref, bf16[8,576,1280]{2,1,0:T(8,128)(2,1)} %get-tuple-element.46.o_ref, bf16[8,384,256]{2,1,0:T(8,128)(2,1)} %get-tuple-element.48.h_ref, bf16[128,1280]{1,0:T(8,128)(2,1)} %copy-done.11, ...), custom_call_target="tpu_custom_call" | custom-call | flops 13589544960 | bytes 27525120 | tf_op jit(solution)/shard_map/pallas_call | solution.py:472
  207.7 0.2 reduce-scatter.5.cloned.1.call-start
  207.9 15.4 %dispatch_dy.1.q_ref = bf16[8,576,1280]{2,1,0:T(8,128)(2,1)} custom-call(s32[2]{0:T(128)} %pad_add_fusion.ids, bf16[8,384,1280]{2,1,0:T(8,128)(2,1)} %bitcast.19, bf16[8,576,384]{2,1,0:T(8,128)(2,1)} %get-tuple-element.49.select_ref, f32[8,576,128]{2,1,0:T(8,128)} %get-tuple-element.50.gate_ref), custom_call_target="tpu_custom_call" | custom-call | flops 4529848320 | bytes 19660800 | tf_op jit(solution)/shard_map/dispatch_dy/pallas_call | solution.py:221
  223.4 57.3 %backward.1 = (bf16[8,576,1280]{2,1,0:T(8,128)(2,1)}, bf16[8,576,896]{2,1,0:T(8,128)(2,1)}, bf16[8,576,896]{2,1,0:T(8,128)(2,1)}) custom-call(bf16[8,576,1280]{2,1,0:T(8,128)(2,1)} %dispatch_dy.1.q_ref, f32[8,576,896]{2,1,0:T(8,128)} %get-tuple-element.51.a1_ref, f32[8,576,896]{2,1,0:T(8,128)} %get-tuple-element.52.a3_ref, bf16[8,1280,896]{2,1,0:T(8,128)(2,1)} %w1_ref.5, ...), custom_call_target="tpu_custom_call" | custom-call | flops 31708938240 | bytes 128188416 | tf_op jit(solution)/shard_map/backward/pallas_call | solution.py:321
  280.7 24.7 %shard_map.171 = f32[8,384,1280]{2,1,0:T(8,128)} custom-call(s32[2]{0:T(128)} %pad_add_fusion.ids, f32[8,12,384]{2,1,0:T(8,128)} %get-tuple-element.39.refs_6_.meta_ref, bf16[8,576,1280]{2,1,0:T(8,128)(2,1)} %get-tuple-element.53.dr_ref, bf16[8,384,512]{2,1,0:T(8,128)(2,1)} %get-tuple-element.54.da_ref, bf16[1280,256]{1,0:T(8,128)(2,1)} %copy-done.2, ...), custom_call_target="tpu_custom_call" | custom-call | flops 4529848320 | bytes 27525120 | tf_op jit(solution)/shard_map/pallas_call | solution.py:472
  305.4 1.8 collective-permute-start.9
  307.2 0.3 collective-permute-start.2
  307.5 1.7 collective-permute-start.8
  309.2 42.2 %collective-permute-done.9.refs_2_ = bf16[2,384,1280]{2,1,0:T(8,128)(2,1)S(1)} collective-permute-done((bf16[2,384,1280]{2,1,0:T(8,128)(2,1)}, bf16[2,384,1280]{2,1,0:T(8,128)(2,1)S(1)}, u32[]{:S(2)}, u32[]{:S(2)}) %collective-permute-start.9) | collective-permute-done | bytes 1966112 | tf_op jit(solution)/shard_map/ppermute | solution.py:526
  351.3 42.1 %collective-permute-done.2 = f32[384,1280]{1,0:T(8,128)S(1)} collective-permute-done((f32[384,1280]{1,0:T(8,128)}, f32[384,1280]{1,0:T(8,128)S(1)}, u32[]{:S(2)}, u32[]{:S(2)}) %collective-permute-start.2) | collective-permute-done | bytes 1966112 | tf_op jit(solution)/shard_map/ppermute | solution.py:526
  393.5 0.2 add_convert_fusion
  393.7 1.7 collective-permute-start.3
  395.4 18.3 %collective-permute-done.8.refs_1_ = bf16[1,384,1280]{2,1,0:T(8,128)(2,1)S(1)} collective-permute-done((bf16[1,384,1280]{2,1,0:T(8,128)(2,1)}, bf16[1,384,1280]{2,1,0:T(8,128)(2,1)S(1)}, u32[]{:S(2)}, u32[]{:S(2)}) %collective-permute-start.8) | collective-permute-done | bytes 983072 | tf_op jit(solution)/shard_map/ppermute | solution.py:526
  413.7 1.7 collective-permute-start.13
  415.4 1.3 collective-permute-start.4
  416.7 19.3 %collective-permute-done.3 = bf16[384,1280]{1,0:T(8,128)(2,1)} collective-permute-done((bf16[384,1280]{1,0:T(8,128)(2,1)S(1)}, bf16[384,1280]{1,0:T(8,128)(2,1)}, u32[]{:S(2)}, u32[]{:S(2)}) %collective-permute-start.3) | collective-permute-done | bytes 983072 | tf_op jit(solution)/shard_map/ppermute | solution.py:526
  436.0 1.5 collective-permute-start.5
  437.6 0.7 copy-done.17
  438.2 0.9 copy-done.15
  439.2 22.1 %dispatch_far.1 = (bf16[8,576,1280]{2,1,0:T(8,128)(2,1)}, bf16[8,576,1280]{2,1,0:T(8,128)(2,1)}) custom-call(s32[2]{0:T(128)} %pad_add_fusion.ids, bf16[1,384,1280]{2,1,0:T(8,128)(2,1)} %get-tuple-element.60.refs_0_, bf16[1,384,1280]{2,1,0:T(8,128)(2,1)} %copy-done.14, bf16[2,384,1280]{2,1,0:T(8,128)(2,1)} %copy-done.13, ...), custom_call_target="tpu_custom_call" | custom-call | flops 9059696640 | bytes 39321600 | tf_op jit(solution)/shard_map/dispatch_far/pallas_call | solution.py:247
  461.3 0.9 copy-done.7
  462.3 2.1 pad_maximum_fusion.near_ref
  464.4 0.0 collective-permute-start.6
  464.4 0.5 collective-permute-start.7
  464.9 91.0 %grads.1 = (bf16[8,640,896]{2,1,0:T(8,128)(2,1)}, bf16[8,640,896]{2,1,0:T(8,128)(2,1)}, bf16[8,448,1280]{2,1,0:T(8,128)(2,1)}) custom-call(s32[2]{0:T(128)} %pad_add_fusion.ids, bf16[8,576,1280]{2,1,0:T(8,128)(2,1)} %get-tuple-element.45.x_ref, bf16[8,576,1280]{2,1,0:T(8,128)(2,1)} %dispatch_dy.1.q_ref, bf16[8,576,1280]{2,1,0:T(8,128)(2,1)} %get-tuple-element.62.xp_ref, ...), custom_call_target="tpu_custom_call" | custom-call | flops 63417876480 | bytes 154533888 | tf_op jit(solution)/shard_map/grads/pallas_call | solution.py:376
  556.0 10.2 %finish.1 = (bf16[1280,896]{1,0:T(8,128)(2,1)}, bf16[1280,896]{1,0:T(8,128)(2,1)}, bf16[896,1280]{1,0:T(8,128)(2,1)}) custom-call(s32[2]{0:T(128)} %pad_add_fusion.ids, bf16[3,384,1280]{2,1,0:T(8,128)(2,1)} %copy-done, bf16[1,384,1280]{2,1,0:T(8,128)(2,1)} %bitcast.11.corner_ref, bf16[3,384,1280]{2,1,0:T(8,128)(2,1)} %collective-permute-done.6.other_near_ref, ...), custom_call_target="tpu_custom_call" | custom-call | flops 1000000000 | bytes 15728640 | tf_op jit(solution)/shard_map/finish/pallas_call | solution.py:506
  566.2 2.8 add_convert_fusion.2
  569.0 2.7 add_convert_fusion.1
  (49 shorter events, 0.2 us)
Async XLA Ops:
  7.2 140.2 %all-gather.5.cloned.1.call-start = ((), (), s32[]{:S(2)}) async-start(), calls=%async_computation.4 | async-start | bytes 8847360 | tf_op jit(solution)/shard_map/all_gather | solution.py:542
  9.3 67.9 %copy-start.4 = (bf16[1280,896]{1,0:T(8,128)(2,1)S(1)}, bf16[1280,896]{1,0:T(8,128)(2,1)}, u32[]{:S(2)}) copy-start(bf16[1280,896]{1,0:T(8,128)(2,1)} %param.17) | copy-start | bytes 6881284
  51.8 386.5 %all-gather.7.cloned.1.call-start = ((), (), s32[]{:S(2)}) async-start(), calls=%async_computation.5 | async-start | bytes 8847360 | tf_op jit(solution)/shard_map/all_gather | solution.py:543
  51.8 24.3 %collective-permute-start.12 = (bf16[384,1280]{1,0:T(8,128)(2,1)}, bf16[384,1280]{1,0:T(8,128)(2,1)S(1)}, u32[]{:S(2)}, u32[]{:S(2)}) collective-permute-start(bf16[384,1280]{1,0:T(8,128)(2,1)} %get-tuple-element.47), channel_id=1, source_target_pairs={{0,8},{8,0},{1,9},{9,1},{2,10},{10,2},{3,11},{11,3},{4,12},{12,4},... | collective-permute-start | bytes 2949128 | tf_op jit(solution)/shard_map/ppermute | solution.py:526
  76.1 0.9 copy-start.6
  77.1 489.1 %reduce-scatter.3.cloned.1.call-start = ((), (), s32[]{:S(2)}) async-start(), calls=%async_computation.2 | async-start | bytes 17694720 | tf_op jit(solution)/shard_map/reduce_scatter | solution.py:565
  77.2 3.0 copy-start.3
  78.5 19.3 %copy-start.2 = (bf16[1280,256]{1,0:T(8,128)(2,1)}, bf16[1280,256]{1,0:T(8,128)(2,1)S(1)}, u32[]{:S(2)}) copy-start(bf16[1280,256]{1,0:T(8,128)(2,1)S(1)} %pad_maximum_fusion.1.refs_8_.wa_ref) | copy-start | bytes 1966084
  78.5 68.8 %collective-permute-start = (bf16[1280,256]{1,0:T(8,128)(2,1)S(1)}, bf16[1280,256]{1,0:T(8,128)(2,1)S(1)}, u32[]{:S(2)}, u32[]{:S(2)}) collective-permute-start(bf16[1280,256]{1,0:T(8,128)(2,1)S(1)} %pad_maximum_fusion.1.refs_8_.wa_ref), channel_id=1, source_target_pairs={{0,8},{8,0},{1,9},{9,1},{2,10},{10,2},{3,11},{11,3},{4,12},{12,4},... | collective-permute-start | bytes 1966088 | tf_op jit(solution)/shard_map/ppermute | solution.py:526
  80.2 17.7 %copy-start.11 = (bf16[128,1280]{1,0:T(8,128)(2,1)}, bf16[128,1280]{1,0:T(8,128)(2,1)S(1)}, u32[]{:S(2)}) copy-start(bf16[128,1280]{1,0:T(8,128)(2,1)S(1)} %pad_dynamic-slice_fusion.refs_10_.w2_ref) | copy-start | bytes 983044
  80.2 67.1 %collective-permute-start.1 = (bf16[128,1280]{1,0:T(8,128)(2,1)S(1)}, bf16[128,1280]{1,0:T(8,128)(2,1)S(1)}, u32[]{:S(2)}, u32[]{:S(2)}) collective-permute-start(bf16[128,1280]{1,0:T(8,128)(2,1)S(1)} %pad_dynamic-slice_fusion.refs_10_.w2_ref), channel_id=1, source_target_pairs={{0,8},{8,0},{1,9},{9,1},{2,10},{10,2},{3,11},{11,3},{4,12},{12,4},... | collective-permute-start | bytes 983048 | tf_op jit(solution)/shard_map/ppermute | solution.py:526
  147.3 0.7 copy-start.16
  147.3 0.9 copy-start.10
  207.7 361.3 %reduce-scatter.5.cloned.1.call-start = ((), (), s32[]{:S(2)}) async-start(), calls=%async_computation.3 | async-start | bytes 17694720 | tf_op jit(solution)/shard_map/reduce_scatter | solution.py:568
  305.4 88.1 %copy-start.5 = (f32[384,1280]{1,0:T(8,128)S(1)}, f32[384,1280]{1,0:T(8,128)}, u32[]{:S(2)}) copy-start(f32[384,1280]{1,0:T(8,128)} %get-tuple-element.55) | copy-start | bytes 5898244
  305.4 108.3 %copy-start.12 = (f32[8,12,384]{2,1,0:T(8,128)S(1)}, f32[8,12,384]{2,1,0:T(8,128)}, u32[]{:S(2)}) copy-start(f32[8,12,384]{2,1,0:T(8,128)} %get-tuple-element.39.refs_6_.meta_ref) | copy-start | bytes 442372
  305.4 45.9 %collective-permute-start.9 = (bf16[2,384,1280]{2,1,0:T(8,128)(2,1)}, bf16[2,384,1280]{2,1,0:T(8,128)(2,1)S(1)}, u32[]{:S(2)}, u32[]{:S(2)}) collective-permute-start(bf16[2,384,1280]{2,1,0:T(8,128)(2,1)} %get-tuple-element.41.refs_2_), channel_id=1, source_target_pairs={{0,8},{8,0},{1,9},{9,1},{2,10},{10,2},{3,11},{11,3},{4,12},{12,4},... | collective-permute-start | bytes 5898248 | tf_op jit(solution)/shard_map/ppermute | solution.py:526
  307.2 86.3 %collective-permute-start.2 = (f32[384,1280]{1,0:T(8,128)}, f32[384,1280]{1,0:T(8,128)S(1)}, u32[]{:S(2)}, u32[]{:S(2)}) collective-permute-start(f32[384,1280]{1,0:T(8,128)} %get-tuple-element.56), channel_id=1, source_target_pairs={{0,8},{8,0},{1,9},{9,1},{2,10},{10,2},{3,11},{11,3},{4,12},{12,4},... | collective-permute-start | bytes 5898248 | tf_op jit(solution)/shard_map/ppermute | solution.py:526
  307.5 106.2 %collective-permute-start.8 = (bf16[1,384,1280]{2,1,0:T(8,128)(2,1)}, bf16[1,384,1280]{2,1,0:T(8,128)(2,1)S(1)}, u32[]{:S(2)}, u32[]{:S(2)}) collective-permute-start(bf16[1,384,1280]{2,1,0:T(8,128)(2,1)} %get-tuple-element.40.refs_1_), channel_id=1, source_target_pairs={{0,8},{8,0},{1,9},{9,1},{2,10},{10,2},{3,11},{11,3},{4,12},{12,4},... | collective-permute-start | bytes 2949128 | tf_op jit(solution)/shard_map/ppermute | solution.py:526
  351.3 86.2 %copy-start.13 = (bf16[2,384,1280]{2,1,0:T(8,128)(2,1)}, bf16[2,384,1280]{2,1,0:T(8,128)(2,1)S(1)}, u32[]{:S(2)}) copy-start(bf16[2,384,1280]{2,1,0:T(8,128)(2,1)S(1)} %collective-permute-done.9.refs_2_) | copy-start | bytes 5898244
  351.3 86.9 %collective-permute-start.11 = (bf16[2,384,1280]{2,1,0:T(8,128)(2,1)S(1)}, bf16[2,384,1280]{2,1,0:T(8,128)(2,1)}, u32[]{:S(2)}, u32[]{:S(2)}) collective-permute-start(bf16[2,384,1280]{2,1,0:T(8,128)(2,1)S(1)} %collective-permute-done.9.refs_2_), channel_id=1, source_target_pairs={{0,1},{1,0},{2,3},{3,2},{4,5},{5,4},{6,7},{7,6},{8,9},{9,8},{10,11... | collective-permute-start | bytes 5898248 | tf_op jit(solution)/shard_map/ppermute | solution.py:526
  393.7 67.6 %copy-start.1 = (bf16[384,1280]{1,0:T(8,128)(2,1)}, bf16[384,1280]{1,0:T(8,128)(2,1)S(1)}, u32[]{:S(2)}) copy-start(bf16[384,1280]{1,0:T(8,128)(2,1)S(1)} %add_convert_fusion) | copy-start | bytes 2949124
  393.7 42.3 %collective-permute-start.3 = (bf16[384,1280]{1,0:T(8,128)(2,1)S(1)}, bf16[384,1280]{1,0:T(8,128)(2,1)}, u32[]{:S(2)}, u32[]{:S(2)}) collective-permute-start(bf16[384,1280]{1,0:T(8,128)(2,1)S(1)} %add_convert_fusion), channel_id=1, source_target_pairs={{0,2},{1,3},{2,0},{3,1},{4,6},{5,7},{6,4},{7,5},{8,10},{9,11},{10,... | collective-permute-start | bytes 2949128 | tf_op jit(solution)/shard_map/ppermute | solution.py:526
  413.7 23.9 %copy-start.14 = (bf16[1,384,1280]{2,1,0:T(8,128)(2,1)}, bf16[1,384,1280]{2,1,0:T(8,128)(2,1)S(1)}, u32[]{:S(2)}) copy-start(bf16[1,384,1280]{2,1,0:T(8,128)(2,1)S(1)} %collective-permute-done.8.refs_1_) | copy-start | bytes 2949124
  413.7 23.8 %collective-permute-start.10 = (bf16[1,384,1280]{2,1,0:T(8,128)(2,1)S(1)}, bf16[1,384,1280]{2,1,0:T(8,128)(2,1)S(1)}, u32[]{:S(2)}, u32[]{:S(2)}) collective-permute-start(bf16[1,384,1280]{2,1,0:T(8,128)(2,1)S(1)} %collective-permute-done.8.refs_1_), channel_id=1, source_target_pairs={{0,1},{1,0},{2,3},{3,2},{4,5},{5,4},{6,7},{7,6},{8,9},{9,8},{10,11... | collective-permute-start | bytes 2949128 | tf_op jit(solution)/shard_map/ppermute | solution.py:526
  413.7 23.8 %collective-permute-start.13 = (f32[8,12,384]{2,1,0:T(8,128)S(1)}, f32[8,12,384]{2,1,0:T(8,128)S(1)}, u32[]{:S(2)}, u32[]{:S(2)}) collective-permute-start(f32[8,12,384]{2,1,0:T(8,128)S(1)} %copy-done.12), channel_id=1, source_target_pairs={{0,8},{8,0},{1,9},{9,1},{2,10},{10,2},{3,11},{11,3},{4,12},{12,4},... | collective-permute-start | bytes 442376 | tf_op jit(solution)/shard_map/ppermute | solution.py:526
  415.4 45.9 %collective-permute-start.4 = (bf16[384,1280]{1,0:T(8,128)(2,1)S(1)}, bf16[384,1280]{1,0:T(8,128)(2,1)S(1)}, u32[]{:S(2)}, u32[]{:S(2)}) collective-permute-start(bf16[384,1280]{1,0:T(8,128)(2,1)S(1)} %add_convert_fusion), channel_id=1, source_target_pairs={{0,4},{1,5},{2,6},{3,7},{4,0},{5,1},{6,2},{7,3},{8,12},{9,13},{10,... | collective-permute-start | bytes 2949128 | tf_op jit(solution)/shard_map/ppermute | solution.py:526
  436.0 28.4 %collective-permute-start.5 = (bf16[384,1280]{1,0:T(8,128)(2,1)}, bf16[384,1280]{1,0:T(8,128)(2,1)}, u32[]{:S(2)}, u32[]{:S(2)}) collective-permute-start(bf16[384,1280]{1,0:T(8,128)(2,1)} %collective-permute-done.3), channel_id=1, source_target_pairs={{0,4},{1,5},{2,6},{3,7},{4,0},{5,1},{6,2},{7,3},{8,12},{9,13},{10,... | collective-permute-start | bytes 2949128 | tf_op jit(solution)/shard_map/ppermute | solution.py:526
  437.6 0.7 copy-start.17
  438.2 0.9 copy-start.15
  461.3 0.9 copy-start.7
  464.4 91.6 %copy-start = (bf16[3,384,1280]{2,1,0:T(8,128)(2,1)}, bf16[3,384,1280]{2,1,0:T(8,128)(2,1)S(1)}, u32[]{:S(2)}) copy-start(bf16[3,384,1280]{2,1,0:T(8,128)(2,1)S(1)} %pad_maximum_fusion.near_ref) | copy-start | bytes 8847364
  464.4 91.6 %collective-permute-start.6 = (bf16[3,384,1280]{2,1,0:T(8,128)(2,1)S(1)}, bf16[3,384,1280]{2,1,0:T(8,128)(2,1)}, u32[]{:S(2)}, u32[]{:S(2)}) collective-permute-start(bf16[3,384,1280]{2,1,0:T(8,128)(2,1)S(1)} %pad_maximum_fusion.near_ref), channel_id=1, source_target_pairs={{0,1},{1,0},{2,3},{3,2},{4,5},{5,4},{6,7},{7,6},{8,9},{9,8},{10,11... | collective-permute-start | bytes 8847368 | tf_op jit(solution)/shard_map/ppermute | solution.py:526
  464.4 91.5 %collective-permute-start.7 = (bf16[384,1280]{1,0:T(8,128)(2,1)}, bf16[384,1280]{1,0:T(8,128)(2,1)}, u32[]{:S(2)}, u32[]{:S(2)}) collective-permute-start(bf16[384,1280]{1,0:T(8,128)(2,1)} %collective-permute-done.5), channel_id=1, source_target_pairs={{0,1},{1,0},{2,3},{3,2},{4,5},{5,4},{6,7},{7,6},{8,9},{9,8},{10,11... | collective-permute-start | bytes 2949128 | tf_op jit(solution)/shard_map/ppermute | solution.py:526
  556.0 10.2 %copy-start.8 = (bf16[384,1280]{1,0:T(8,128)(2,1)S(1)}, bf16[384,1280]{1,0:T(8,128)(2,1)}, u32[]{:S(2)}) copy-start(bf16[384,1280]{1,0:T(8,128)(2,1)} %x_ref.1) | copy-start | bytes 2949124
  566.2 2.8 copy-start.9
Sparse Core Ops, SparseCore 0:
  51.9 48.4 all-gather.4
  102.2 48.2 all-gather.6
  207.8 105.6 reduce-scatter.2
  316.8 122.0 reduce-scatter.4

commit v4 on v3

--- a/solution.py
+++ b/solution.py
@@ -443,53 +443,77 @@
     return gates
 
 
-def combine_out_kernel(top_k, ids, meta_ref, o_ref, h_ref, w2_ref, w2_far_ref, y_ref):
+def combine_out_kernel(top_k, ids, meta_ref, o_ref, h_ref, w2_ref, w2_far_ref, y_ref, select_ref):
     tokens = h_ref.shape[1]
-    gates = gate_matrix(meta_ref[0].T, ids, o_ref.shape[1], top_k)
-    high = gates.astype(BF16)
-    rest = gates - high.astype(F32)
-    mid = rest.astype(BF16)
-    low = (rest - mid.astype(F32)).astype(BF16)
-    sums = dot(jnp.concatenate([high, mid, low], axis=0), o_ref[0])
+    meta = meta_ref[0].T
     width = w2_ref.shape[0]
-    y_ref[0] = (sums[:tokens] + sums[tokens:2 * tokens] + sums[2 * tokens:]
-                + dot(h_ref[0, :, :width], w2_ref[...]) + dot(h_ref[0, :, width:], w2_far_ref[...]))
-
-
-def combine_back_kernel(top_k, ids, meta_ref, dr_ref, da_ref, wa_ref, wa_far_ref, dx_ref):
-    gates = gate_matrix(meta_ref[0].T, ids, dr_ref.shape[1], top_k)
-    select = jnp.where(gates != 0.0, 1.0, 0.0).astype(BF16)
-    width = wa_ref.shape[1]
-    dx_ref[0] = (dot(select, dr_ref[0]) + dot_nt(da_ref[0, :, :width], wa_ref[...])
-                 + dot_nt(da_ref[0, :, width:], wa_far_ref[...]))
-
-
-def combine(kernel, ids, meta_all, returned, hidden, weights, top_k, passes):
-    groups, rows, dim = returned.shape
-    tokens, width = hidden.shape[1:]
+    part = tokens // 2
+    for first in range(0, tokens, part):
+        span = slice(first, first + part)
+        gates = gate_matrix(meta[span], ids, o_ref.shape[1], top_k)
+        select_ref[0, span] = jnp.where(gates != 0.0, 1.0, 0.0).astype(BF16)
+        high = gates.astype(BF16)
+        rest = gates - high.astype(F32)
+        mid = rest.astype(BF16)
+        low = (rest - mid.astype(F32)).astype(BF16)
+        sums = dot(jnp.concatenate([high, mid, low], axis=0), o_ref[0])
+        y_ref[0, span] = (sums[:part] + sums[part:2 * part] + sums[2 * part:]
+                          + dot(h_ref[0, span, :width], w2_ref[...]) + dot(h_ref[0, span, width:], w2_far_ref[...]))
+
+
+def combine_out(ids, meta_all, o, h, weights, top_k):
+    groups, rows, dim = o.shape
+    tokens, width = h.shape[1:]
     by_place = lambda s, ids: (s, 0, 0)
     by_ep = lambda s, ids: (ep_of(s, ids), 0, 0)
     return pl.pallas_call(
-        functools.partial(kernel, top_k),
+        functools.partial(combine_out_kernel, top_k),
         grid_spec=pltpu.PrefetchScalarGridSpec(
             num_scalar_prefetch=1, grid=(groups,),
             in_specs=[pl.BlockSpec((1, 2 * top_k, tokens), by_ep), pl.BlockSpec((1, rows, dim), by_place),
                       pl.BlockSpec((1, tokens, width), by_place)]
             + [pl.BlockSpec(weight.shape, lambda s, ids: (0, 0)) for weight in weights],
-            out_specs=pl.BlockSpec((1, tokens, dim), by_ep)),
-        out_shape=jax.ShapeDtypeStruct((groups, tokens, dim), F32), compiler_params=params(1),
-        cost_estimate=pl.CostEstimate(flops=2 * passes * groups * tokens * rows * dim,
+            out_specs=[pl.BlockSpec((1, tokens, dim), by_ep), pl.BlockSpec((1, tokens, rows), by_place)]),
+        out_shape=[jax.ShapeDtypeStruct((groups, tokens, dim), F32), jax.ShapeDtypeStruct((groups, tokens, rows), BF16)],
+        compiler_params=params(1), name="combine_out",
+        cost_estimate=pl.CostEstimate(flops=6 * groups * tokens * rows * dim,
                                       bytes_accessed=groups * (2 * rows + 4 * tokens) * dim, transcendentals=0),
-    )(ids, meta_all, returned, hidden, *weights)
+    )(ids, meta_all, o, h, *weights)
+
+
+def combine_back_kernel(ids, select_ref, dr_ref, da_ref, wa_ref, wa_far_ref, dx_ref):
+    width = wa_ref.shape[1]
+    dx_ref[0] = (dot(select_ref[0], dr_ref[0]) + dot_nt(da_ref[0, :, :width], wa_ref[...])
+                 + dot_nt(da_ref[0, :, width:], wa_far_ref[...]))
+
+
+def combine_back(ids, select, dr, da, weights):
+    groups, rows, dim = dr.shape
+    tokens, width = da.shape[1:]
+    by_place = lambda s, ids: (s, 0, 0)
+    return pl.pallas_call(
+        combine_back_kernel,
+        grid_spec=pltpu.PrefetchScalarGridSpec(
+            num_scalar_prefetch=1, grid=(groups,),
+            in_specs=[pl.BlockSpec((1, tokens, rows), by_place), pl.BlockSpec((1, rows, dim), by_place),
+                      pl.BlockSpec((1, tokens, width), by_place)]
+            + [pl.BlockSpec(weight.shape, lambda s, ids: (0, 0)) for weight in weights],
+            out_specs=pl.BlockSpec((1, tokens, dim), lambda s, ids: (ep_of(s, ids), 0, 0))),
+        out_shape=jax.ShapeDtypeStruct((groups, tokens, dim), F32), compiler_params=params(1), name="combine_back",
+        cost_estimate=pl.CostEstimate(flops=2 * groups * tokens * (rows + width) * dim,
+                                      bytes_accessed=groups * (2 * rows + 4 * tokens) * dim, transcendentals=0),
+    )(ids, select, dr, da, *weights)
 
 
 def finish_kernel(ids, near_ref, corner_ref, other_near_ref, other_corner_ref, g1_ref, g3_ref, g2_ref):
+    device = pl.program_id(0)
+    place = pl.ds(pl.multiple_of(device * SLICE, SLICE), SLICE)
+
     def lay(ref):
-        g1_ref[...] = ref[0, :SLICE].T
-        g3_ref[...] = ref[0, SLICE:2 * SLICE].T
-        g2_ref[...] = ref[0, 2 * SLICE:]
-
-    device = pl.program_id(0)
+        g1_ref[:, place] = ref[0, :SLICE].T
+        g3_ref[:, place] = ref[0, SLICE:2 * SLICE].T
+        g2_ref[place] = ref[0, 2 * SLICE:]
+
     same = device % 2 == ids[1] % 2
     near = jnp.bitwise_xor(device // 2, ids[1] // 2) < 3
     pl.when(same & near)(lambda: lay(near_ref))
@@ -507,8 +531,7 @@
         finish_kernel,
         grid_spec=pltpu.PrefetchScalarGridSpec(
             num_scalar_prefetch=1, grid=(ff // SLICE,), in_specs=[near, corner, near, corner],
-            out_specs=[pl.BlockSpec((dim, SLICE), lambda e, ids: (0, e)), pl.BlockSpec((dim, SLICE), lambda e, ids: (0, e)),
-                       pl.BlockSpec((SLICE, dim), lambda e, ids: (e, 0))]),
+            out_specs=[pl.BlockSpec(out.shape, lambda e, ids: (0, 0)) for out in (wide, wide, tall)]),
         out_shape=[wide, wide, tall], compiler_params=params(1), name="finish",
         cost_estimate=pl.CostEstimate(flops=1_000_000_000, bytes_accessed=16 * height * dim * 2, transcendentals=0),
     )(ids, *slices)
@@ -561,10 +584,10 @@
         o, h, a1, a3 = forward(xd, expert_w1, expert_w3, expert_w2, cap)
         qd = dispatch_dy(ids, dy_all, rows_select, rows_gate, local, cap)
         sh, sda, shared_grad, shared_far = shared_expert(ids, blocks, dy_all, wide + tall)
-        y_part = combine(combine_out_kernel, ids, meta_all, o, sh, tall, top_k, 3)
+        y_part, select = combine_out(ids, meta_all, o, sh, tall, top_k)
         y_sum = lax.psum_scatter(y_part.reshape(-1, dim), "ep", scatter_dimension=0, tiled=True)
         dr, da1, da3 = backward(qd, a1, a3, expert_w1, expert_w3, expert_w2, cap)
-        dx_part = combine(combine_back_kernel, ids, meta_all, dr, sda, wide, top_k, 1)
+        dx_part = combine_back(ids, select, dr, sda, wide)
         dx_sum = lax.psum_scatter(dx_part.reshape(-1, dim), "ep", scatter_dimension=0, tiled=True)
 
         xp, qp = dispatch_far(ids, far_blocks, far_dy_all, far_meta, *sizes)

time: 580 us -> 574 us (0.990)
  Pallas kernels: 389 us -> 380 us
    pallas_call x2, Pallas kernels: 61.1 us -> 52.9 us  [the longest x1 33.3 us: combine_out(): pl.pallas_call(functools.partial(combine_out_kernel, top_k), grid_spec=pl...]
  transfers between devices with their start and end apart: 18 -> 18, of which waited for: 5 -> 6; matrix products, arithmetic and copies ran while one was open for 1% -> 1% of each run, Pallas kernels for 60% -> 59%
where the time goes in v4:
time: 574 us; the launch traced here: 572 us
  Pallas kernels  380 us (66%)
  waiting for transfers between devices  147 us (26%)
  starting transfers between devices  14.4 us (3%)
  between operations  14 us (2%)
  other arithmetic  10.6 us (2%)
  local copies, waits for them, and re-layouts  5.76 us (1%)
    ppermute x14, waiting for transfers between devices, move(): return lax.ppermute(value, axis, route)  147 us
    pallas_call x1, Pallas kernels, expert_grads(): pl.pallas_call(grads_kernel, grid_spec=pltpu.PrefetchScalarGridSpec(num_s...  91 us
    pallas_call x1, Pallas kernels, backward(): pl.pallas_call(functools.partial(backward_kernel, cap), grid=(local,), in...  57.4 us
    pallas_call x1, Pallas kernels, forward(): pl.pallas_call(functools.partial(forward_kernel, cap), grid=(local,), in_...  49.4 us
    pallas_call x1, Pallas kernels, gather_layer(): pl.pallas_call(functools.partial(gather_kernel, ep_size), in_specs=[anywh...  42.5 us
    pallas_call x1, Pallas kernels, combine_out(): pl.pallas_call(functools.partial(combine_out_kernel, top_k), grid_spec=pl...  33.3 us
    pallas_call x1, Pallas kernels, shared_expert(): pl.pallas_call(shared_kernel, grid_spec=pltpu.PrefetchScalarGridSpec(num_...  23 us
    pallas_call x1, Pallas kernels, dispatch_far(): pl.pallas_call(functools.partial(dispatch_far_kernel, local, cap, top_k),...  22.1 us
  transfers between devices with their start and end apart: 18, of which 6 were waited for; matrix products, arithmetic and copies ran while one was open for 1% of the time, Pallas kernels for 59%

profile of v4, /device:TPU:0, one launch (start us, length us, event | category | flops | bytes accessed | tf_op | source)
XLA Modules:
  0.0 572.2 jit_solution(5622803939811448610)
XLA Ops:
  7.2 0.0 all-gather.5.cloned.1.call-start
  7.2 0.7 convert_bitcast_fusion
  7.9 1.3 pad_maximum_fusion.2.meta_ref
  9.3 42.5 %gather.1 = (bf16[1,384,1280]{2,1,0:T(8,128)(2,1)}, bf16[2,384,1280]{2,1,0:T(8,128)(2,1)}, bf16[1,384,1280]{2,1,0:T(8,128)(2,1)}, bf16[1,384,1280]{2,1,0:T(8,128...) custom-call(bf16[384,1280]{1,0:T(8,128)(2,1)} %x_ref.1, ...), custom_call_target="tpu_custom_call" | custom-call | flops 30000001024 | bytes 31457280 | tf_op jit(solution)/shard_map/gather/pallas_call | solution.py:123
  51.8 0.0 all-gather.7.cloned.1.call-start
  51.8 1.6 collective-permute-start.12
  53.4 22.7 %collective-permute-done.12 = bf16[384,1280]{1,0:T(8,128)(2,1)S(1)} collective-permute-done((bf16[384,1280]{1,0:T(8,128)(2,1)}, bf16[384,1280]{1,0:T(8,128)(2,1)S(1)}, u32[]{:S(2)}, u32[]{:S(2)}) %collective-permute-start.12) | collective-permute-done | bytes 983072 | tf_op jit(solution)/shard_map/ppermute | solution.py:549
  76.1 0.9 copy-done.6
  77.1 0.0 reduce-scatter.3.cloned.1.call-start
  77.2 1.3 pad_dynamic-slice_fusion.1
  78.4 0.1 pad_maximum_fusion.1.refs_8_.wa_ref
  78.5 1.6 collective-permute-start
  80.1 0.1 pad_dynamic-slice_fusion.refs_10_.w2_ref
  80.2 0.5 collective-permute-start.1
  80.7 0.6 pad_add_fusion.ids
  81.3 16.5 %dispatch_x.1 = (bf16[8,576,1280]{2,1,0:T(8,128)(2,1)}, bf16[8,576,384]{2,1,0:T(8,128)(2,1)}, f32[8,576,128]{2,1,0:T(8,128)}) custom-call(s32[2]{0:T(128)} %pad_add_fusion.ids, bf16[1,384,1280]{2,1,0:T(8,128)(2,1)} %bitcast.22, bf16[1,384,1280]{2,1,0:T(8,128)(2,1)} %get-tuple-element.42.refs_1_, bf16[2,384,1280]{2,1,0:T(8,128)(2,1)} %get-tuple-element.43.refs_2_, ...), custom_call_target="tpu_custom_call" | custom-call | flops 4529848320 | bytes 19660800 | tf_op jit(solution)/shard_map/dispatch_x/pallas_call | solution.py:195
  97.9 49.4 %forward.1 = (bf16[8,576,1280]{2,1,0:T(8,128)(2,1)}, bf16[8,576,896]{2,1,0:T(8,128)(2,1)}, f32[8,576,896]{2,1,0:T(8,128)}, f32[8,576,896]{2,1,0:T(8,128)}) custom-call(bf16[8,576,1280]{2,1,0:T(8,128)(2,1)} %get-tuple-element.47.x_ref, bf16[8,1280,896]{2,1,0:T(8,128)(2,1)} %w1_ref.5, bf16[8,1280,896]{2,1,0:T(8,128)(2,1)} %w3_ref.5, bf16[8,896,1280]{2,1,0:T(8,128)(2,1)} %w2_ref.5), custom_call_target="tpu_custom_call" | custom-call | flops 31708938240 | bytes 119930880 | tf_op jit(solution)/shard_map/forward/pallas_call | solution.py:286
  147.4 0.7 copy-done.15
  148.0 0.2 copy-done.10
  148.2 23.0 %shared.1 = (bf16[8,384,256]{2,1,0:T(8,128)(2,1)}, bf16[8,384,512]{2,1,0:T(8,128)(2,1)}, f32[384,1280]{1,0:T(8,128)}, f32[384,1280]{1,0:T(8,128)}) custom-call(s32[2]{0:T(128)} %pad_add_fusion.ids, bf16[1,384,1280]{2,1,0:T(8,128)(2,1)} %bitcast.23, bf16[1,384,1280]{2,1,0:T(8,128)(2,1)} %get-tuple-element.42.refs_1_, ...), custom_call_target="tpu_custom_call" | custom-call | flops 9059696640 | bytes 15728640 | tf_op jit(solution)/shard_map/shared/pallas_call | solution.py:417
  171.3 33.3 %combine_out.1 = (f32[8,384,1280]{2,1,0:T(8,128)}, bf16[8,384,576]{2,1,0:T(8,128)(2,1)}) custom-call(s32[2]{0:T(128)} %pad_add_fusion.ids, f32[8,12,384]{2,1,0:T(8,128)} %get-tuple-element.41.refs_6_.meta_ref, bf16[8,576,1280]{2,1,0:T(8,128)(2,1)} %get-tuple-element.48.o_ref, bf16[8,384,256]{2,1,0:T(8,128)(2,1)} %get-tuple-element.50.h_ref, ...), custom_call_target="tpu_custom_call" | custom-call | flops 13589544960 | bytes 27525120 | tf_op jit(solution)/shard_map/combine_out/pallas_call | solution.py:469
  204.6 0.2 reduce-scatter.5.cloned.1.call-start
  204.8 15.3 %dispatch_dy.1.q_ref = bf16[8,576,1280]{2,1,0:T(8,128)(2,1)} custom-call(s32[2]{0:T(128)} %pad_add_fusion.ids, bf16[8,384,1280]{2,1,0:T(8,128)(2,1)} %bitcast.19, bf16[8,576,384]{2,1,0:T(8,128)(2,1)} %get-tuple-element.53.select_ref, f32[8,576,128]{2,1,0:T(8,128)} %get-tuple-element.54.gate_ref), custom_call_target="tpu_custom_call" | custom-call | flops 4529848320 | bytes 19660800 | tf_op jit(solution)/shard_map/dispatch_dy/pallas_call | solution.py:221
  220.2 57.4 %backward.1 = (bf16[8,576,1280]{2,1,0:T(8,128)(2,1)}, bf16[8,576,896]{2,1,0:T(8,128)(2,1)}, bf16[8,576,896]{2,1,0:T(8,128)(2,1)}) custom-call(bf16[8,576,1280]{2,1,0:T(8,128)(2,1)} %dispatch_dy.1.q_ref, f32[8,576,896]{2,1,0:T(8,128)} %get-tuple-element.55.a1_ref, f32[8,576,896]{2,1,0:T(8,128)} %get-tuple-element.56.a3_ref, bf16[8,1280,896]{2,1,0:T(8,128)(2,1)} %w1_ref.5, ...), custom_call_target="tpu_custom_call" | custom-call | flops 31708938240 | bytes 128188416 | tf_op jit(solution)/shard_map/backward/pallas_call | solution.py:321
  277.6 19.6 %combine_back.1 = f32[8,384,1280]{2,1,0:T(8,128)} custom-call(s32[2]{0:T(128)} %pad_add_fusion.ids, bf16[8,384,576]{2,1,0:T(8,128)(2,1)} %get-tuple-element.52.select_ref, bf16[8,576,1280]{2,1,0:T(8,128)(2,1)} %get-tuple-element.57.dr_ref, bf16[8,384,512]{2,1,0:T(8,128)(2,1)} %get-tuple-element.58.da_ref, bf16[1280,256]{1,0:T(8,128)(2,1)} %copy-done.2, ...), custom_call_target="tpu_custom_call" | custom-call | flops 8556380160 | bytes 27525120 | tf_op jit(solution)/shard_map/combine_back/pallas_call | solution.py:494
  297.2 1.7 collective-permute-start.9
  299.0 0.3 collective-permute-start.2
  299.3 1.7 collective-permute-start.8
  301.0 42.2 %collective-permute-done.9.refs_2_ = bf16[2,384,1280]{2,1,0:T(8,128)(2,1)S(1)} collective-permute-done((bf16[2,384,1280]{2,1,0:T(8,128)(2,1)}, bf16[2,384,1280]{2,1,0:T(8,128)(2,1)S(1)}, u32[]{:S(2)}, u32[]{:S(2)}) %collective-permute-start.9) | collective-permute-done | bytes 1966112 | tf_op jit(solution)/shard_map/ppermute | solution.py:549
  343.2 42.1 %collective-permute-done.2 = f32[384,1280]{1,0:T(8,128)S(1)} collective-permute-done((f32[384,1280]{1,0:T(8,128)}, f32[384,1280]{1,0:T(8,128)S(1)}, u32[]{:S(2)}, u32[]{:S(2)}) %collective-permute-start.2) | collective-permute-done | bytes 1966112 | tf_op jit(solution)/shard_map/ppermute | solution.py:549
  385.3 0.2 add_convert_fusion
  385.6 1.7 collective-permute-start.3
  387.3 18.3 %collective-permute-done.8.refs_1_ = bf16[1,384,1280]{2,1,0:T(8,128)(2,1)S(1)} collective-permute-done((bf16[1,384,1280]{2,1,0:T(8,128)(2,1)}, bf16[1,384,1280]{2,1,0:T(8,128)(2,1)S(1)}, u32[]{:S(2)}, u32[]{:S(2)}) %collective-permute-start.8) | collective-permute-done | bytes 983072 | tf_op jit(solution)/shard_map/ppermute | solution.py:549
  405.7 1.7 collective-permute-start.13
  407.3 1.4 collective-permute-start.4
  408.7 14.6 %collective-permute-done.3 = bf16[384,1280]{1,0:T(8,128)(2,1)} collective-permute-done((bf16[384,1280]{1,0:T(8,128)(2,1)S(1)}, bf16[384,1280]{1,0:T(8,128)(2,1)}, u32[]{:S(2)}, u32[]{:S(2)}) %collective-permute-start.3) | collective-permute-done | bytes 983072 | tf_op jit(solution)/shard_map/ppermute | solution.py:549
  423.3 1.8 collective-permute-start.5
  425.0 0.7 copy-done.17
  425.7 0.9 copy-done.14
  426.7 22.1 %dispatch_far.1 = (bf16[8,576,1280]{2,1,0:T(8,128)(2,1)}, bf16[8,576,1280]{2,1,0:T(8,128)(2,1)}) custom-call(s32[2]{0:T(128)} %pad_add_fusion.ids, bf16[1,384,1280]{2,1,0:T(8,128)(2,1)} %get-tuple-element.64.refs_0_, bf16[1,384,1280]{2,1,0:T(8,128)(2,1)} %copy-done.13, bf16[2,384,1280]{2,1,0:T(8,128)(2,1)} %copy-done.12, ...), custom_call_target="tpu_custom_call" | custom-call | flops 9059696640 | bytes 39321600 | tf_op jit(solution)/shard_map/dispatch_far/pallas_call | solution.py:247
  448.8 0.9 copy-done.7
  449.7 2.1 pad_maximum_fusion.near_ref
  451.9 0.0 collective-permute-start.6
  451.9 7.0 %collective-permute-done.5 = bf16[384,1280]{1,0:T(8,128)(2,1)} collective-permute-done((bf16[384,1280]{1,0:T(8,128)(2,1)}, bf16[384,1280]{1,0:T(8,128)(2,1)}, u32[]{:S(2)}, u32[]{:S(2)}) %collective-permute-start.5) | collective-permute-done | bytes 983072 | tf_op jit(solution)/shard_map/ppermute | solution.py:549
  458.9 91.0 %grads.1 = (bf16[8,640,896]{2,1,0:T(8,128)(2,1)}, bf16[8,640,896]{2,1,0:T(8,128)(2,1)}, bf16[8,448,1280]{2,1,0:T(8,128)(2,1)}) custom-call(s32[2]{0:T(128)} %pad_add_fusion.ids, bf16[8,576,1280]{2,1,0:T(8,128)(2,1)} %get-tuple-element.47.x_ref, bf16[8,576,1280]{2,1,0:T(8,128)(2,1)} %dispatch_dy.1.q_ref, bf16[8,576,1280]{2,1,0:T(8,128)(2,1)} %get-tuple-element.66.xp_ref, ...), custom_call_target="tpu_custom_call" | custom-call | flops 63417876480 | bytes 154533888 | tf_op jit(solution)/shard_map/grads/pallas_call | solution.py:376
  550.0 10.2 %finish.1 = (bf16[1280,896]{1,0:T(8,128)(2,1)}, bf16[1280,896]{1,0:T(8,128)(2,1)}, bf16[896,1280]{1,0:T(8,128)(2,1)}) custom-call(s32[2]{0:T(128)} %pad_add_fusion.ids, bf16[3,384,1280]{2,1,0:T(8,128)(2,1)} %copy-done, bf16[1,384,1280]{2,1,0:T(8,128)(2,1)} %bitcast.11.corner_ref, bf16[3,384,1280]{2,1,0:T(8,128)(2,1)} %collective-permute-done.6.other_near_ref, ...), custom_call_target="tpu_custom_call" | custom-call | flops 1000000000 | bytes 15728640 | tf_op jit(solution)/shard_map/finish/pallas_call | solution.py:530
  560.1 2.8 add_convert_fusion.2
  562.9 2.7 add_convert_fusion.1
  (49 shorter events, 0.2 us)
Async XLA Ops:
  7.2 140.2 %all-gather.5.cloned.1.call-start = ((), (), s32[]{:S(2)}) async-start(), calls=%async_computation.4 | async-start | bytes 8847360 | tf_op jit(solution)/shard_map/all_gather | solution.py:565
  9.3 67.9 %copy-start.4 = (bf16[1280,896]{1,0:T(8,128)(2,1)S(1)}, bf16[1280,896]{1,0:T(8,128)(2,1)}, u32[]{:S(2)}) copy-start(bf16[1280,896]{1,0:T(8,128)(2,1)} %param.17) | copy-start | bytes 6881284
  51.8 373.9 %all-gather.7.cloned.1.call-start = ((), (), s32[]{:S(2)}) async-start(), calls=%async_computation.5 | async-start | bytes 8847360 | tf_op jit(solution)/shard_map/all_gather | solution.py:566
  51.8 24.3 %collective-permute-start.12 = (bf16[384,1280]{1,0:T(8,128)(2,1)}, bf16[384,1280]{1,0:T(8,128)(2,1)S(1)}, u32[]{:S(2)}, u32[]{:S(2)}) collective-permute-start(bf16[384,1280]{1,0:T(8,128)(2,1)} %get-tuple-element.49), channel_id=1, source_target_pairs={{0,8},{8,0},{1,9},{9,1},{2,10},{10,2},{3,11},{11,3},{4,12},{12,4},... | collective-permute-start | bytes 2949128 | tf_op jit(solution)/shard_map/ppermute | solution.py:549
  76.1 0.9 copy-start.6
  77.1 483.1 %reduce-scatter.3.cloned.1.call-start = ((), (), s32[]{:S(2)}) async-start(), calls=%async_computation.2 | async-start | bytes 17694720 | tf_op jit(solution)/shard_map/reduce_scatter | solution.py:588
  77.2 3.0 copy-start.3
  78.5 19.4 %copy-start.2 = (bf16[1280,256]{1,0:T(8,128)(2,1)}, bf16[1280,256]{1,0:T(8,128)(2,1)S(1)}, u32[]{:S(2)}) copy-start(bf16[1280,256]{1,0:T(8,128)(2,1)S(1)} %pad_maximum_fusion.1.refs_8_.wa_ref) | copy-start | bytes 1966084
  78.5 68.8 %collective-permute-start = (bf16[1280,256]{1,0:T(8,128)(2,1)S(1)}, bf16[1280,256]{1,0:T(8,128)(2,1)S(1)}, u32[]{:S(2)}, u32[]{:S(2)}) collective-permute-start(bf16[1280,256]{1,0:T(8,128)(2,1)S(1)} %pad_maximum_fusion.1.refs_8_.wa_ref), channel_id=1, source_target_pairs={{0,8},{8,0},{1,9},{9,1},{2,10},{10,2},{3,11},{11,3},{4,12},{12,4},... | collective-permute-start | bytes 1966088 | tf_op jit(solution)/shard_map/ppermute | solution.py:549
  80.2 17.7 %copy-start.11 = (bf16[128,1280]{1,0:T(8,128)(2,1)}, bf16[128,1280]{1,0:T(8,128)(2,1)S(1)}, u32[]{:S(2)}) copy-start(bf16[128,1280]{1,0:T(8,128)(2,1)S(1)} %pad_dynamic-slice_fusion.refs_10_.w2_ref) | copy-start | bytes 983044
  80.2 67.1 %collective-permute-start.1 = (bf16[128,1280]{1,0:T(8,128)(2,1)S(1)}, bf16[128,1280]{1,0:T(8,128)(2,1)S(1)}, u32[]{:S(2)}, u32[]{:S(2)}) collective-permute-start(bf16[128,1280]{1,0:T(8,128)(2,1)S(1)} %pad_dynamic-slice_fusion.refs_10_.w2_ref), channel_id=1, source_target_pairs={{0,8},{8,0},{1,9},{9,1},{2,10},{10,2},{3,11},{11,3},{4,12},{12,4},... | collective-permute-start | bytes 983048 | tf_op jit(solution)/shard_map/ppermute | solution.py:549
  147.3 0.7 copy-start.15
  147.3 0.9 copy-start.10
  204.6 358.4 %reduce-scatter.5.cloned.1.call-start = ((), (), s32[]{:S(2)}) async-start(), calls=%async_computation.3 | async-start | bytes 17694720 | tf_op jit(solution)/shard_map/reduce_scatter | solution.py:591
  297.2 88.1 %copy-start.5 = (f32[384,1280]{1,0:T(8,128)S(1)}, f32[384,1280]{1,0:T(8,128)}, u32[]{:S(2)}) copy-start(f32[384,1280]{1,0:T(8,128)} %get-tuple-element.59) | copy-start | bytes 5898244
  297.2 108.4 %copy-start.16 = (f32[8,12,384]{2,1,0:T(8,128)S(1)}, f32[8,12,384]{2,1,0:T(8,128)}, u32[]{:S(2)}) copy-start(f32[8,12,384]{2,1,0:T(8,128)} %get-tuple-element.41.refs_6_.meta_ref) | copy-start | bytes 442372
  297.2 45.9 %collective-permute-start.9 = (bf16[2,384,1280]{2,1,0:T(8,128)(2,1)}, bf16[2,384,1280]{2,1,0:T(8,128)(2,1)S(1)}, u32[]{:S(2)}, u32[]{:S(2)}) collective-permute-start(bf16[2,384,1280]{2,1,0:T(8,128)(2,1)} %get-tuple-element.43.refs_2_), channel_id=1, source_target_pairs={{0,8},{8,0},{1,9},{9,1},{2,10},{10,2},{3,11},{11,3},{4,12},{12,4},... | collective-permute-start | bytes 5898248 | tf_op jit(solution)/shard_map/ppermute | solution.py:549
  299.0 86.4 %collective-permute-start.2 = (f32[384,1280]{1,0:T(8,128)}, f32[384,1280]{1,0:T(8,128)S(1)}, u32[]{:S(2)}, u32[]{:S(2)}) collective-permute-start(f32[384,1280]{1,0:T(8,128)} %get-tuple-element.60), channel_id=1, source_target_pairs={{0,8},{8,0},{1,9},{9,1},{2,10},{10,2},{3,11},{11,3},{4,12},{12,4},... | collective-permute-start | bytes 5898248 | tf_op jit(solution)/shard_map/ppermute | solution.py:549
  299.3 106.3 %collective-permute-start.8 = (bf16[1,384,1280]{2,1,0:T(8,128)(2,1)}, bf16[1,384,1280]{2,1,0:T(8,128)(2,1)S(1)}, u32[]{:S(2)}, u32[]{:S(2)}) collective-permute-start(bf16[1,384,1280]{2,1,0:T(8,128)(2,1)} %get-tuple-element.42.refs_1_), channel_id=1, source_target_pairs={{0,8},{8,0},{1,9},{9,1},{2,10},{10,2},{3,11},{11,3},{4,12},{12,4},... | collective-permute-start | bytes 2949128 | tf_op jit(solution)/shard_map/ppermute | solution.py:549
  343.2 80.1 %copy-start.12 = (bf16[2,384,1280]{2,1,0:T(8,128)(2,1)}, bf16[2,384,1280]{2,1,0:T(8,128)(2,1)S(1)}, u32[]{:S(2)}) copy-start(bf16[2,384,1280]{2,1,0:T(8,128)(2,1)S(1)} %collective-permute-done.9.refs_2_) | copy-start | bytes 5898244
  343.2 82.5 %collective-permute-start.11 = (bf16[2,384,1280]{2,1,0:T(8,128)(2,1)S(1)}, bf16[2,384,1280]{2,1,0:T(8,128)(2,1)}, u32[]{:S(2)}, u32[]{:S(2)}) collective-permute-start(bf16[2,384,1280]{2,1,0:T(8,128)(2,1)S(1)} %collective-permute-done.9.refs_2_), channel_id=1, source_target_pairs={{0,1},{1,0},{2,3},{3,2},{4,5},{5,4},{6,7},{7,6},{8,9},{9,8},{10,11... | collective-permute-start | bytes 5898248 | tf_op jit(solution)/shard_map/ppermute | solution.py:549
  385.6 63.2 %copy-start.1 = (bf16[384,1280]{1,0:T(8,128)(2,1)}, bf16[384,1280]{1,0:T(8,128)(2,1)S(1)}, u32[]{:S(2)}) copy-start(bf16[384,1280]{1,0:T(8,128)(2,1)S(1)} %add_convert_fusion) | copy-start | bytes 2949124
  385.6 37.7 %collective-permute-start.3 = (bf16[384,1280]{1,0:T(8,128)(2,1)S(1)}, bf16[384,1280]{1,0:T(8,128)(2,1)}, u32[]{:S(2)}, u32[]{:S(2)}) collective-permute-start(bf16[384,1280]{1,0:T(8,128)(2,1)S(1)} %add_convert_fusion), channel_id=1, source_target_pairs={{0,2},{1,3},{2,0},{3,1},{4,6},{5,7},{6,4},{7,5},{8,10},{9,11},{10,... | collective-permute-start | bytes 2949128 | tf_op jit(solution)/shard_map/ppermute | solution.py:549
  405.6 19.4 %copy-start.13 = (bf16[1,384,1280]{2,1,0:T(8,128)(2,1)}, bf16[1,384,1280]{2,1,0:T(8,128)(2,1)S(1)}, u32[]{:S(2)}) copy-start(bf16[1,384,1280]{2,1,0:T(8,128)(2,1)S(1)} %collective-permute-done.8.refs_1_) | copy-start | bytes 2949124
  405.6 19.4 %collective-permute-start.10 = (bf16[1,384,1280]{2,1,0:T(8,128)(2,1)S(1)}, bf16[1,384,1280]{2,1,0:T(8,128)(2,1)S(1)}, u32[]{:S(2)}, u32[]{:S(2)}) collective-permute-start(bf16[1,384,1280]{2,1,0:T(8,128)(2,1)S(1)} %collective-permute-done.8.refs_1_), channel_id=1, source_target_pairs={{0,1},{1,0},{2,3},{3,2},{4,5},{5,4},{6,7},{7,6},{8,9},{9,8},{10,11... | collective-permute-start | bytes 2949128 | tf_op jit(solution)/shard_map/ppermute | solution.py:549
  405.7 19.4 %collective-permute-start.13 = (f32[8,12,384]{2,1,0:T(8,128)S(1)}, f32[8,12,384]{2,1,0:T(8,128)S(1)}, u32[]{:S(2)}, u32[]{:S(2)}) collective-permute-start(f32[8,12,384]{2,1,0:T(8,128)S(1)} %copy-done.16), channel_id=1, source_target_pairs={{0,8},{8,0},{1,9},{9,1},{2,10},{10,2},{3,11},{11,3},{4,12},{12,4},... | collective-permute-start | bytes 442376 | tf_op jit(solution)/shard_map/ppermute | solution.py:549
  407.3 41.5 %collective-permute-start.4 = (bf16[384,1280]{1,0:T(8,128)(2,1)S(1)}, bf16[384,1280]{1,0:T(8,128)(2,1)S(1)}, u32[]{:S(2)}, u32[]{:S(2)}) collective-permute-start(bf16[384,1280]{1,0:T(8,128)(2,1)S(1)} %add_convert_fusion), channel_id=1, source_target_pairs={{0,4},{1,5},{2,6},{3,7},{4,0},{5,1},{6,2},{7,3},{8,12},{9,13},{10,... | collective-permute-start | bytes 2949128 | tf_op jit(solution)/shard_map/ppermute | solution.py:549
  423.3 35.6 %collective-permute-start.5 = (bf16[384,1280]{1,0:T(8,128)(2,1)}, bf16[384,1280]{1,0:T(8,128)(2,1)}, u32[]{:S(2)}, u32[]{:S(2)}) collective-permute-start(bf16[384,1280]{1,0:T(8,128)(2,1)} %collective-permute-done.3), channel_id=1, source_target_pairs={{0,4},{1,5},{2,6},{3,7},{4,0},{5,1},{6,2},{7,3},{8,12},{9,13},{10,... | collective-permute-start | bytes 2949128 | tf_op jit(solution)/shard_map/ppermute | solution.py:549
  425.0 0.7 copy-start.17
  425.7 0.9 copy-start.14
  448.8 0.9 copy-start.7
  451.9 98.1 %copy-start = (bf16[3,384,1280]{2,1,0:T(8,128)(2,1)}, bf16[3,384,1280]{2,1,0:T(8,128)(2,1)S(1)}, u32[]{:S(2)}) copy-start(bf16[3,384,1280]{2,1,0:T(8,128)(2,1)S(1)} %pad_maximum_fusion.near_ref) | copy-start | bytes 8847364
  451.9 98.1 %collective-permute-start.6 = (bf16[3,384,1280]{2,1,0:T(8,128)(2,1)S(1)}, bf16[3,384,1280]{2,1,0:T(8,128)(2,1)}, u32[]{:S(2)}, u32[]{:S(2)}) collective-permute-start(bf16[3,384,1280]{2,1,0:T(8,128)(2,1)S(1)} %pad_maximum_fusion.near_ref), channel_id=1, source_target_pairs={{0,1},{1,0},{2,3},{3,2},{4,5},{5,4},{6,7},{7,6},{8,9},{9,8},{10,11... | collective-permute-start | bytes 8847368 | tf_op jit(solution)/shard_map/ppermute | solution.py:549
  458.9 91.0 %collective-permute-start.7 = (bf16[384,1280]{1,0:T(8,128)(2,1)}, bf16[384,1280]{1,0:T(8,128)(2,1)}, u32[]{:S(2)}, u32[]{:S(2)}) collective-permute-start(bf16[384,1280]{1,0:T(8,128)(2,1)} %collective-permute-done.5), channel_id=1, source_target_pairs={{0,1},{1,0},{2,3},{3,2},{4,5},{5,4},{6,7},{7,6},{8,9},{9,8},{10,11... | collective-permute-start | bytes 2949128 | tf_op jit(solution)/shard_map/ppermute | solution.py:549
  549.9 10.2 %copy-start.8 = (bf16[384,1280]{1,0:T(8,128)(2,1)S(1)}, bf16[384,1280]{1,0:T(8,128)(2,1)}, u32[]{:S(2)}) copy-start(bf16[384,1280]{1,0:T(8,128)(2,1)} %x_ref.1) | copy-start | bytes 2949124
  560.1 2.8 copy-start.9
Sparse Core Ops, SparseCore 0:
  51.9 48.4 all-gather.4
  102.2 48.2 all-gather.6
  204.7 105.6 reduce-scatter.2
  313.7 117.8 reduce-scatter.4

commit v5 on v4

--- a/solution.py
+++ b/solution.py
@@ -164,14 +164,14 @@
     return step % 2
 
 
-def lay_rows(local, cap, got, out_ref):
-    for l in range(local):
-        out_ref[l] = got[l * cap:(l + 1) * cap].astype(BF16)
-
-
-def gate_rows(meta, ids, rows, top_k):
+def lay_rows(first, count, cap, got, out_ref):
+    for l in range(count):
+        out_ref[first + l] = got[l * cap:(l + 1) * cap].astype(BF16)
+
+
+def gate_rows(meta, ids, total, first, rows, top_k):
     tokens = meta.shape[1]
-    base = (ids[1] * rows).astype(F32)
+    base = (ids[1] * total + first).astype(F32)
     row_ids = lax.broadcasted_iota(jnp.int32, (rows, tokens), 0).astype(F32) + base
     gates = jnp.zeros((rows, tokens), F32)
     for j in range(top_k):
@@ -182,10 +182,15 @@
 def dispatch_x_kernel(local, cap, top_k, ids, *refs):
     *blocks, meta_ref, xd_ref, select_ref, gate_ref, buffer, sem = refs
     slot = stream(blocks, 1, buffer, sem)
-    gates, select = gate_rows(meta_ref[0], ids, local * cap, top_k)
-    select_ref[0] = select
-    gate_ref[0] = jnp.broadcast_to(jnp.sum(gates, axis=1, keepdims=True), gate_ref.shape[1:])
-    lay_rows(local, cap, dot(select, buffer[slot, 0]), xd_ref)
+    meta = meta_ref[0]
+    count = local // 2
+    rows = count * cap
+    for first in range(0, local, count):
+        gates, select = gate_rows(meta, ids, local * cap, first * cap, rows, top_k)
+        span = slice(first * cap, first * cap + rows)
+        select_ref[0, span] = select
+        gate_ref[0, span] = jnp.broadcast_to(jnp.sum(gates, axis=1, keepdims=True), (rows, gate_ref.shape[2]))
+        lay_rows(first, count, cap, dot(select, buffer[slot, 0]), xd_ref)
 
 
 def dispatch_x(ids, blocks, meta_all, local, cap, top_k):
@@ -211,7 +216,7 @@
 
 
 def dispatch_dy_kernel(local, cap, ids, dy_ref, select_ref, gate_ref, qd_ref):
-    lay_rows(local, cap, dot(select_ref[0], dy_ref[0]) * gate_ref[0][:, :1], qd_ref)
+    lay_rows(0, local, cap, dot(select_ref[0], dy_ref[0]) * gate_ref[0][:, :1], qd_ref)
 
 
 def dispatch_dy(ids, dy_all, select, gate, local, cap):
@@ -234,9 +239,12 @@
 def dispatch_far_kernel(local, cap, top_k, ids, *refs):
     *blocks, dy_ref, meta_ref, xd_ref, qd_ref, buffer, sem = refs
     slot = stream(blocks, 1, buffer, sem)
-    gates, select = gate_rows(meta_ref[0], ids, local * cap, top_k)
-    lay_rows(local, cap, dot(select, buffer[slot, 0]), xd_ref)
-    lay_rows(local, cap, dot(select, dy_ref[0]) * jnp.sum(gates, axis=1, keepdims=True), qd_ref)
+    meta = meta_ref[0]
+    count = local // 2
+    for first in range(0, local, count):
+        gates, select = gate_rows(meta, ids, local * cap, first * cap, count * cap, top_k)
+        lay_rows(first, count, cap, dot(select, buffer[slot, 0]), xd_ref)
+        lay_rows(first, count, cap, dot(select, dy_ref[0]) * jnp.sum(gates, axis=1, keepdims=True), qd_ref)
 
 
 def dispatch_far(ids, blocks, dy_all, meta_all, local, cap, top_k):

time: 574 us -> 574 us (level)
  no operation moved by 1% of the time
where the time goes in v5:
time: 574 us; the launch traced here: 573 us
  Pallas kernels  380 us (66%)
  waiting for transfers between devices  148 us (26%)
  between operations  14 us (2%)
  starting transfers between devices  13.9 us (2%)
  other arithmetic  10.6 us (2%)
  local copies, waits for them, and re-layouts  5.76 us (1%)
    ppermute x14, waiting for transfers between devices, move(): return lax.ppermute(value, axis, route)  148 us
    pallas_call x1, Pallas kernels, expert_grads(): pl.pallas_call(grads_kernel, grid_spec=pltpu.PrefetchScalarGridSpec(num_s...  91 us
    pallas_call x1, Pallas kernels, backward(): pl.pallas_call(functools.partial(backward_kernel, cap), grid=(local,), in...  57.1 us
    pallas_call x1, Pallas kernels, forward(): pl.pallas_call(functools.partial(forward_kernel, cap), grid=(local,), in_...  50.3 us
    pallas_call x1, Pallas kernels, gather_layer(): pl.pallas_call(functools.partial(gather_kernel, ep_size), in_specs=[anywh...  42.5 us
    pallas_call x1, Pallas kernels, combine_out(): pl.pallas_call(functools.partial(combine_out_kernel, top_k), grid_spec=pl...  33.3 us
    pallas_call x1, Pallas kernels, shared_expert(): pl.pallas_call(shared_kernel, grid_spec=pltpu.PrefetchScalarGridSpec(num_...  23 us
    pallas_call x1, Pallas kernels, dispatch_far(): pl.pallas_call(functools.partial(dispatch_far_kernel, local, cap, top_k),...  22 us
  transfers between devices with their start and end apart: 18, of which 6 were waited for; matrix products, arithmetic and copies ran while one was open for 1% of the time, Pallas kernels for 59%

profile of v5, /device:TPU:0, one launch (start us, length us, event | category | flops | bytes accessed | tf_op | source)
XLA Modules:
  0.0 572.7 jit_solution(12884707687203185144)
XLA Ops:
  7.2 0.0 all-gather.5.cloned.1.call-start
  7.2 0.7 convert_bitcast_fusion
  7.9 1.3 pad_maximum_fusion.2.meta_ref
  9.3 42.5 %gather.1 = (bf16[1,384,1280]{2,1,0:T(8,128)(2,1)}, bf16[2,384,1280]{2,1,0:T(8,128)(2,1)}, bf16[1,384,1280]{2,1,0:T(8,128)(2,1)}, bf16[1,384,1280]{2,1,0:T(8,128...) custom-call(bf16[384,1280]{1,0:T(8,128)(2,1)} %x_ref.1, ...), custom_call_target="tpu_custom_call" | custom-call | flops 30000001024 | bytes 31457280 | tf_op jit(solution)/shard_map/gather/pallas_call | solution.py:123
  51.8 0.0 all-gather.7.cloned.1.call-start
  51.8 1.6 collective-permute-start.12
  53.4 22.7 %collective-permute-done.12 = bf16[384,1280]{1,0:T(8,128)(2,1)S(1)} collective-permute-done((bf16[384,1280]{1,0:T(8,128)(2,1)}, bf16[384,1280]{1,0:T(8,128)(2,1)S(1)}, u32[]{:S(2)}, u32[]{:S(2)}) %collective-permute-start.12) | collective-permute-done | bytes 983072 | tf_op jit(solution)/shard_map/ppermute | solution.py:557
  76.1 0.9 copy-done.6
  77.1 0.0 reduce-scatter.3.cloned.1.call-start
  77.2 1.3 pad_dynamic-slice_fusion.1
  78.4 0.1 pad_maximum_fusion.1.refs_8_.wa_ref
  78.5 1.6 collective-permute-start
  80.1 0.1 pad_dynamic-slice_fusion.refs_10_.w2_ref
  80.2 0.5 collective-permute-start.1
  80.7 0.6 pad_add_fusion.ids
  81.3 15.6 %dispatch_x.1 = (bf16[8,576,1280]{2,1,0:T(8,128)(2,1)}, bf16[8,576,384]{2,1,0:T(8,128)(2,1)}, f32[8,576,128]{2,1,0:T(8,128)}) custom-call(s32[2]{0:T(128)} %pad_add_fusion.ids, bf16[1,384,1280]{2,1,0:T(8,128)(2,1)} %bitcast.22, bf16[1,384,1280]{2,1,0:T(8,128)(2,1)} %get-tuple-element.42.refs_1_, bf16[2,384,1280]{2,1,0:T(8,128)(2,1)} %get-tuple-element.43.refs_2_, ...), custom_call_target="tpu_custom_call" | custom-call | flops 4529848320 | bytes 19660800 | tf_op jit(solution)/shard_map/dispatch_x/pallas_call | solution.py:200
  96.9 50.3 %forward.1 = (bf16[8,576,1280]{2,1,0:T(8,128)(2,1)}, bf16[8,576,896]{2,1,0:T(8,128)(2,1)}, f32[8,576,896]{2,1,0:T(8,128)}, f32[8,576,896]{2,1,0:T(8,128)}) custom-call(bf16[8,576,1280]{2,1,0:T(8,128)(2,1)} %get-tuple-element.47.x_ref, bf16[8,1280,896]{2,1,0:T(8,128)(2,1)} %w1_ref.5, bf16[8,1280,896]{2,1,0:T(8,128)(2,1)} %w3_ref.5, bf16[8,896,1280]{2,1,0:T(8,128)(2,1)} %w2_ref.5), custom_call_target="tpu_custom_call" | custom-call | flops 31708938240 | bytes 119930880 | tf_op jit(solution)/shard_map/forward/pallas_call | solution.py:294
  147.3 0.7 copy-done.15
  148.0 0.2 copy-done.10
  148.2 23.0 %shared.1 = (bf16[8,384,256]{2,1,0:T(8,128)(2,1)}, bf16[8,384,512]{2,1,0:T(8,128)(2,1)}, f32[384,1280]{1,0:T(8,128)}, f32[384,1280]{1,0:T(8,128)}) custom-call(s32[2]{0:T(128)} %pad_add_fusion.ids, bf16[1,384,1280]{2,1,0:T(8,128)(2,1)} %bitcast.23, bf16[1,384,1280]{2,1,0:T(8,128)(2,1)} %get-tuple-element.42.refs_1_, ...), custom_call_target="tpu_custom_call" | custom-call | flops 9059696640 | bytes 15728640 | tf_op jit(solution)/shard_map/shared/pallas_call | solution.py:425
  171.2 33.3 %combine_out.1 = (f32[8,384,1280]{2,1,0:T(8,128)}, bf16[8,384,576]{2,1,0:T(8,128)(2,1)}) custom-call(s32[2]{0:T(128)} %pad_add_fusion.ids, f32[8,12,384]{2,1,0:T(8,128)} %get-tuple-element.41.refs_6_.meta_ref, bf16[8,576,1280]{2,1,0:T(8,128)(2,1)} %get-tuple-element.48.o_ref, bf16[8,384,256]{2,1,0:T(8,128)(2,1)} %get-tuple-element.50.h_ref, ...), custom_call_target="tpu_custom_call" | custom-call | flops 13589544960 | bytes 27525120 | tf_op jit(solution)/shard_map/combine_out/pallas_call | solution.py:477
  204.5 0.2 reduce-scatter.5.cloned.1.call-start
  204.8 15.6 %dispatch_dy.1.q_ref = bf16[8,576,1280]{2,1,0:T(8,128)(2,1)} custom-call(s32[2]{0:T(128)} %pad_add_fusion.ids, bf16[8,384,1280]{2,1,0:T(8,128)(2,1)} %bitcast.19, bf16[8,576,384]{2,1,0:T(8,128)(2,1)} %get-tuple-element.53.select_ref, f32[8,576,128]{2,1,0:T(8,128)} %get-tuple-element.54.gate_ref), custom_call_target="tpu_custom_call" | custom-call | flops 4529848320 | bytes 19660800 | tf_op jit(solution)/shard_map/dispatch_dy/pallas_call | solution.py:226
  220.4 57.1 %backward.1 = (bf16[8,576,1280]{2,1,0:T(8,128)(2,1)}, bf16[8,576,896]{2,1,0:T(8,128)(2,1)}, bf16[8,576,896]{2,1,0:T(8,128)(2,1)}) custom-call(bf16[8,576,1280]{2,1,0:T(8,128)(2,1)} %dispatch_dy.1.q_ref, f32[8,576,896]{2,1,0:T(8,128)} %get-tuple-element.55.a1_ref, f32[8,576,896]{2,1,0:T(8,128)} %get-tuple-element.56.a3_ref, bf16[8,1280,896]{2,1,0:T(8,128)(2,1)} %w1_ref.5, ...), custom_call_target="tpu_custom_call" | custom-call | flops 31708938240 | bytes 128188416 | tf_op jit(solution)/shard_map/backward/pallas_call | solution.py:329
  277.5 19.6 %combine_back.1 = f32[8,384,1280]{2,1,0:T(8,128)} custom-call(s32[2]{0:T(128)} %pad_add_fusion.ids, bf16[8,384,576]{2,1,0:T(8,128)(2,1)} %get-tuple-element.52.select_ref, bf16[8,576,1280]{2,1,0:T(8,128)(2,1)} %get-tuple-element.57.dr_ref, bf16[8,384,512]{2,1,0:T(8,128)(2,1)} %get-tuple-element.58.da_ref, bf16[1280,256]{1,0:T(8,128)(2,1)} %copy-done.2, ...), custom_call_target="tpu_custom_call" | custom-call | flops 8556380160 | bytes 27525120 | tf_op jit(solution)/shard_map/combine_back/pallas_call | solution.py:502
  297.1 1.8 collective-permute-start.9
  298.9 0.3 collective-permute-start.2
  299.2 1.7 collective-permute-start.8
  300.9 42.1 %collective-permute-done.9.refs_2_ = bf16[2,384,1280]{2,1,0:T(8,128)(2,1)S(1)} collective-permute-done((bf16[2,384,1280]{2,1,0:T(8,128)(2,1)}, bf16[2,384,1280]{2,1,0:T(8,128)(2,1)S(1)}, u32[]{:S(2)}, u32[]{:S(2)}) %collective-permute-start.9) | collective-permute-done | bytes 1966112 | tf_op jit(solution)/shard_map/ppermute | solution.py:557
  343.0 42.1 %collective-permute-done.2 = f32[384,1280]{1,0:T(8,128)S(1)} collective-permute-done((f32[384,1280]{1,0:T(8,128)}, f32[384,1280]{1,0:T(8,128)S(1)}, u32[]{:S(2)}, u32[]{:S(2)}) %collective-permute-start.2) | collective-permute-done | bytes 1966112 | tf_op jit(solution)/shard_map/ppermute | solution.py:557
  385.2 0.2 add_convert_fusion
  385.4 1.9 collective-permute-start.3
  387.3 18.0 %collective-permute-done.8.refs_1_ = bf16[1,384,1280]{2,1,0:T(8,128)(2,1)S(1)} collective-permute-done((bf16[1,384,1280]{2,1,0:T(8,128)(2,1)}, bf16[1,384,1280]{2,1,0:T(8,128)(2,1)S(1)}, u32[]{:S(2)}, u32[]{:S(2)}) %collective-permute-start.8) | collective-permute-done | bytes 983072 | tf_op jit(solution)/shard_map/ppermute | solution.py:557
  405.3 0.7 collective-permute-start.13
  406.0 1.6 collective-permute-start.4
  407.6 14.7 %collective-permute-done.3 = bf16[384,1280]{1,0:T(8,128)(2,1)} collective-permute-done((bf16[384,1280]{1,0:T(8,128)(2,1)S(1)}, bf16[384,1280]{1,0:T(8,128)(2,1)}, u32[]{:S(2)}, u32[]{:S(2)}) %collective-permute-start.3) | collective-permute-done | bytes 983072 | tf_op jit(solution)/shard_map/ppermute | solution.py:557
  422.3 1.9 collective-permute-start.5
  424.2 0.7 copy-done.17
  424.9 0.9 copy-done.14
  425.8 22.0 %dispatch_far.1 = (bf16[8,576,1280]{2,1,0:T(8,128)(2,1)}, bf16[8,576,1280]{2,1,0:T(8,128)(2,1)}) custom-call(s32[2]{0:T(128)} %pad_add_fusion.ids, bf16[1,384,1280]{2,1,0:T(8,128)(2,1)} %get-tuple-element.64.refs_0_, bf16[1,384,1280]{2,1,0:T(8,128)(2,1)} %copy-done.13, bf16[2,384,1280]{2,1,0:T(8,128)(2,1)} %copy-done.12, ...), custom_call_target="tpu_custom_call" | custom-call | flops 9059696640 | bytes 39321600 | tf_op jit(solution)/shard_map/dispatch_far/pallas_call | solution.py:255
  447.8 0.9 copy-done.7
  448.8 2.1 pad_maximum_fusion.near_ref
  450.9 0.0 collective-permute-start.6
  451.0 8.4 %collective-permute-done.5 = bf16[384,1280]{1,0:T(8,128)(2,1)} collective-permute-done((bf16[384,1280]{1,0:T(8,128)(2,1)}, bf16[384,1280]{1,0:T(8,128)(2,1)}, u32[]{:S(2)}, u32[]{:S(2)}) %collective-permute-start.5) | collective-permute-done | bytes 983072 | tf_op jit(solution)/shard_map/ppermute | solution.py:557
  459.4 91.0 %grads.1 = (bf16[8,640,896]{2,1,0:T(8,128)(2,1)}, bf16[8,640,896]{2,1,0:T(8,128)(2,1)}, bf16[8,448,1280]{2,1,0:T(8,128)(2,1)}) custom-call(s32[2]{0:T(128)} %pad_add_fusion.ids, bf16[8,576,1280]{2,1,0:T(8,128)(2,1)} %get-tuple-element.47.x_ref, bf16[8,576,1280]{2,1,0:T(8,128)(2,1)} %dispatch_dy.1.q_ref, bf16[8,576,1280]{2,1,0:T(8,128)(2,1)} %get-tuple-element.66.xp_ref, ...), custom_call_target="tpu_custom_call" | custom-call | flops 63417876480 | bytes 154533888 | tf_op jit(solution)/shard_map/grads/pallas_call | solution.py:384
  550.4 10.2 %finish.1 = (bf16[1280,896]{1,0:T(8,128)(2,1)}, bf16[1280,896]{1,0:T(8,128)(2,1)}, bf16[896,1280]{1,0:T(8,128)(2,1)}) custom-call(s32[2]{0:T(128)} %pad_add_fusion.ids, bf16[3,384,1280]{2,1,0:T(8,128)(2,1)} %copy-done, bf16[1,384,1280]{2,1,0:T(8,128)(2,1)} %bitcast.11.corner_ref, bf16[3,384,1280]{2,1,0:T(8,128)(2,1)} %collective-permute-done.6.other_near_ref, ...), custom_call_target="tpu_custom_call" | custom-call | flops 1000000000 | bytes 15728640 | tf_op jit(solution)/shard_map/finish/pallas_call | solution.py:538
  560.6 2.8 add_convert_fusion.2
  563.4 2.7 add_convert_fusion.1
  (49 shorter events, 0.2 us)
Async XLA Ops:
  7.2 140.1 %all-gather.5.cloned.1.call-start = ((), (), s32[]{:S(2)}) async-start(), calls=%async_computation.4 | async-start | bytes 8847360 | tf_op jit(solution)/shard_map/all_gather | solution.py:573
  9.3 67.9 %copy-start.4 = (bf16[1280,896]{1,0:T(8,128)(2,1)S(1)}, bf16[1280,896]{1,0:T(8,128)(2,1)}, u32[]{:S(2)}) copy-start(bf16[1280,896]{1,0:T(8,128)(2,1)} %param.17) | copy-start | bytes 6881284
  51.8 373.1 %all-gather.7.cloned.1.call-start = ((), (), s32[]{:S(2)}) async-start(), calls=%async_computation.5 | async-start | bytes 8847360 | tf_op jit(solution)/shard_map/all_gather | solution.py:574
  51.8 24.3 %collective-permute-start.12 = (bf16[384,1280]{1,0:T(8,128)(2,1)}, bf16[384,1280]{1,0:T(8,128)(2,1)S(1)}, u32[]{:S(2)}, u32[]{:S(2)}) collective-permute-start(bf16[384,1280]{1,0:T(8,128)(2,1)} %get-tuple-element.49), channel_id=1, source_target_pairs={{0,8},{8,0},{1,9},{9,1},{2,10},{10,2},{3,11},{11,3},{4,12},{12,4},... | collective-permute-start | bytes 2949128 | tf_op jit(solution)/shard_map/ppermute | solution.py:557
  76.1 0.9 copy-start.6
  77.1 483.6 %reduce-scatter.3.cloned.1.call-start = ((), (), s32[]{:S(2)}) async-start(), calls=%async_computation.2 | async-start | bytes 17694720 | tf_op jit(solution)/shard_map/reduce_scatter | solution.py:596
  77.2 3.0 copy-start.3
  78.5 18.4 %copy-start.2 = (bf16[1280,256]{1,0:T(8,128)(2,1)}, bf16[1280,256]{1,0:T(8,128)(2,1)S(1)}, u32[]{:S(2)}) copy-start(bf16[1280,256]{1,0:T(8,128)(2,1)S(1)} %pad_maximum_fusion.1.refs_8_.wa_ref) | copy-start | bytes 1966084
  78.5 68.7 %collective-permute-start = (bf16[1280,256]{1,0:T(8,128)(2,1)S(1)}, bf16[1280,256]{1,0:T(8,128)(2,1)S(1)}, u32[]{:S(2)}, u32[]{:S(2)}) collective-permute-start(bf16[1280,256]{1,0:T(8,128)(2,1)S(1)} %pad_maximum_fusion.1.refs_8_.wa_ref), channel_id=1, source_target_pairs={{0,8},{8,0},{1,9},{9,1},{2,10},{10,2},{3,11},{11,3},{4,12},{12,4},... | collective-permute-start | bytes 1966088 | tf_op jit(solution)/shard_map/ppermute | solution.py:557
  80.2 16.7 %copy-start.11 = (bf16[128,1280]{1,0:T(8,128)(2,1)}, bf16[128,1280]{1,0:T(8,128)(2,1)S(1)}, u32[]{:S(2)}) copy-start(bf16[128,1280]{1,0:T(8,128)(2,1)S(1)} %pad_dynamic-slice_fusion.refs_10_.w2_ref) | copy-start | bytes 983044
  80.2 67.0 %collective-permute-start.1 = (bf16[128,1280]{1,0:T(8,128)(2,1)S(1)}, bf16[128,1280]{1,0:T(8,128)(2,1)S(1)}, u32[]{:S(2)}, u32[]{:S(2)}) collective-permute-start(bf16[128,1280]{1,0:T(8,128)(2,1)S(1)} %pad_dynamic-slice_fusion.refs_10_.w2_ref), channel_id=1, source_target_pairs={{0,8},{8,0},{1,9},{9,1},{2,10},{10,2},{3,11},{11,3},{4,12},{12,4},... | collective-permute-start | bytes 983048 | tf_op jit(solution)/shard_map/ppermute | solution.py:557
  147.3 0.7 copy-start.15
  147.3 0.9 copy-start.10
  204.5 358.9 %reduce-scatter.5.cloned.1.call-start = ((), (), s32[]{:S(2)}) async-start(), calls=%async_computation.3 | async-start | bytes 17694720 | tf_op jit(solution)/shard_map/reduce_scatter | solution.py:599
  297.1 88.1 %copy-start.5 = (f32[384,1280]{1,0:T(8,128)S(1)}, f32[384,1280]{1,0:T(8,128)}, u32[]{:S(2)}) copy-start(f32[384,1280]{1,0:T(8,128)} %get-tuple-element.59) | copy-start | bytes 5898244
  297.1 108.2 %copy-start.16 = (f32[8,12,384]{2,1,0:T(8,128)S(1)}, f32[8,12,384]{2,1,0:T(8,128)}, u32[]{:S(2)}) copy-start(f32[8,12,384]{2,1,0:T(8,128)} %get-tuple-element.41.refs_6_.meta_ref) | copy-start | bytes 442372
  297.1 45.9 %collective-permute-start.9 = (bf16[2,384,1280]{2,1,0:T(8,128)(2,1)}, bf16[2,384,1280]{2,1,0:T(8,128)(2,1)S(1)}, u32[]{:S(2)}, u32[]{:S(2)}) collective-permute-start(bf16[2,384,1280]{2,1,0:T(8,128)(2,1)} %get-tuple-element.43.refs_2_), channel_id=1, source_target_pairs={{0,8},{8,0},{1,9},{9,1},{2,10},{10,2},{3,11},{11,3},{4,12},{12,4},... | collective-permute-start | bytes 5898248 | tf_op jit(solution)/shard_map/ppermute | solution.py:557
  298.9 86.3 %collective-permute-start.2 = (f32[384,1280]{1,0:T(8,128)}, f32[384,1280]{1,0:T(8,128)S(1)}, u32[]{:S(2)}, u32[]{:S(2)}) collective-permute-start(f32[384,1280]{1,0:T(8,128)} %get-tuple-element.60), channel_id=1, source_target_pairs={{0,8},{8,0},{1,9},{9,1},{2,10},{10,2},{3,11},{11,3},{4,12},{12,4},... | collective-permute-start | bytes 5898248 | tf_op jit(solution)/shard_map/ppermute | solution.py:557
  299.2 106.1 %collective-permute-start.8 = (bf16[1,384,1280]{2,1,0:T(8,128)(2,1)}, bf16[1,384,1280]{2,1,0:T(8,128)(2,1)S(1)}, u32[]{:S(2)}, u32[]{:S(2)}) collective-permute-start(bf16[1,384,1280]{2,1,0:T(8,128)(2,1)} %get-tuple-element.42.refs_1_), channel_id=1, source_target_pairs={{0,8},{8,0},{1,9},{9,1},{2,10},{10,2},{3,11},{11,3},{4,12},{12,4},... | collective-permute-start | bytes 2949128 | tf_op jit(solution)/shard_map/ppermute | solution.py:557
  343.0 79.3 %copy-start.12 = (bf16[2,384,1280]{2,1,0:T(8,128)(2,1)}, bf16[2,384,1280]{2,1,0:T(8,128)(2,1)S(1)}, u32[]{:S(2)}) copy-start(bf16[2,384,1280]{2,1,0:T(8,128)(2,1)S(1)} %collective-permute-done.9.refs_2_) | copy-start | bytes 5898244
  343.0 81.9 %collective-permute-start.11 = (bf16[2,384,1280]{2,1,0:T(8,128)(2,1)S(1)}, bf16[2,384,1280]{2,1,0:T(8,128)(2,1)}, u32[]{:S(2)}, u32[]{:S(2)}) collective-permute-start(bf16[2,384,1280]{2,1,0:T(8,128)(2,1)S(1)} %collective-permute-done.9.refs_2_), channel_id=1, source_target_pairs={{0,1},{1,0},{2,3},{3,2},{4,5},{5,4},{6,7},{7,6},{8,9},{9,8},{10,11... | collective-permute-start | bytes 5898248 | tf_op jit(solution)/shard_map/ppermute | solution.py:557
  385.4 62.4 %copy-start.1 = (bf16[384,1280]{1,0:T(8,128)(2,1)}, bf16[384,1280]{1,0:T(8,128)(2,1)S(1)}, u32[]{:S(2)}) copy-start(bf16[384,1280]{1,0:T(8,128)(2,1)S(1)} %add_convert_fusion) | copy-start | bytes 2949124
  385.4 36.9 %collective-permute-start.3 = (bf16[384,1280]{1,0:T(8,128)(2,1)S(1)}, bf16[384,1280]{1,0:T(8,128)(2,1)}, u32[]{:S(2)}, u32[]{:S(2)}) collective-permute-start(bf16[384,1280]{1,0:T(8,128)(2,1)S(1)} %add_convert_fusion), channel_id=1, source_target_pairs={{0,2},{1,3},{2,0},{3,1},{4,6},{5,7},{6,4},{7,5},{8,10},{9,11},{10,... | collective-permute-start | bytes 2949128 | tf_op jit(solution)/shard_map/ppermute | solution.py:557
  405.3 18.9 %copy-start.13 = (bf16[1,384,1280]{2,1,0:T(8,128)(2,1)}, bf16[1,384,1280]{2,1,0:T(8,128)(2,1)S(1)}, u32[]{:S(2)}) copy-start(bf16[1,384,1280]{2,1,0:T(8,128)(2,1)S(1)} %collective-permute-done.8.refs_1_) | copy-start | bytes 2949124
  405.3 18.9 %collective-permute-start.10 = (bf16[1,384,1280]{2,1,0:T(8,128)(2,1)S(1)}, bf16[1,384,1280]{2,1,0:T(8,128)(2,1)S(1)}, u32[]{:S(2)}, u32[]{:S(2)}) collective-permute-start(bf16[1,384,1280]{2,1,0:T(8,128)(2,1)S(1)} %collective-permute-done.8.refs_1_), channel_id=1, source_target_pairs={{0,1},{1,0},{2,3},{3,2},{4,5},{5,4},{6,7},{7,6},{8,9},{9,8},{10,11... | collective-permute-start | bytes 2949128 | tf_op jit(solution)/shard_map/ppermute | solution.py:557
  405.3 18.9 %collective-permute-start.13 = (f32[8,12,384]{2,1,0:T(8,128)S(1)}, f32[8,12,384]{2,1,0:T(8,128)S(1)}, u32[]{:S(2)}, u32[]{:S(2)}) collective-permute-start(f32[8,12,384]{2,1,0:T(8,128)S(1)} %copy-done.16), channel_id=1, source_target_pairs={{0,8},{8,0},{1,9},{9,1},{2,10},{10,2},{3,11},{11,3},{4,12},{12,4},... | collective-permute-start | bytes 442376 | tf_op jit(solution)/shard_map/ppermute | solution.py:557
  406.0 41.8 %collective-permute-start.4 = (bf16[384,1280]{1,0:T(8,128)(2,1)S(1)}, bf16[384,1280]{1,0:T(8,128)(2,1)S(1)}, u32[]{:S(2)}, u32[]{:S(2)}) collective-permute-start(bf16[384,1280]{1,0:T(8,128)(2,1)S(1)} %add_convert_fusion), channel_id=1, source_target_pairs={{0,4},{1,5},{2,6},{3,7},{4,0},{5,1},{6,2},{7,3},{8,12},{9,13},{10,... | collective-permute-start | bytes 2949128 | tf_op jit(solution)/shard_map/ppermute | solution.py:557
  422.3 37.0 %collective-permute-start.5 = (bf16[384,1280]{1,0:T(8,128)(2,1)}, bf16[384,1280]{1,0:T(8,128)(2,1)}, u32[]{:S(2)}, u32[]{:S(2)}) collective-permute-start(bf16[384,1280]{1,0:T(8,128)(2,1)} %collective-permute-done.3), channel_id=1, source_target_pairs={{0,4},{1,5},{2,6},{3,7},{4,0},{5,1},{6,2},{7,3},{8,12},{9,13},{10,... | collective-permute-start | bytes 2949128 | tf_op jit(solution)/shard_map/ppermute | solution.py:557
  424.2 0.7 copy-start.17
  424.9 0.9 copy-start.14
  447.8 0.9 copy-start.7
  450.9 99.5 %copy-start = (bf16[3,384,1280]{2,1,0:T(8,128)(2,1)}, bf16[3,384,1280]{2,1,0:T(8,128)(2,1)S(1)}, u32[]{:S(2)}) copy-start(bf16[3,384,1280]{2,1,0:T(8,128)(2,1)S(1)} %pad_maximum_fusion.near_ref) | copy-start | bytes 8847364
  450.9 99.5 %collective-permute-start.6 = (bf16[3,384,1280]{2,1,0:T(8,128)(2,1)S(1)}, bf16[3,384,1280]{2,1,0:T(8,128)(2,1)}, u32[]{:S(2)}, u32[]{:S(2)}) collective-permute-start(bf16[3,384,1280]{2,1,0:T(8,128)(2,1)S(1)} %pad_maximum_fusion.near_ref), channel_id=1, source_target_pairs={{0,1},{1,0},{2,3},{3,2},{4,5},{5,4},{6,7},{7,6},{8,9},{9,8},{10,11... | collective-permute-start | bytes 8847368 | tf_op jit(solution)/shard_map/ppermute | solution.py:557
  459.4 91.0 %collective-permute-start.7 = (bf16[384,1280]{1,0:T(8,128)(2,1)}, bf16[384,1280]{1,0:T(8,128)(2,1)}, u32[]{:S(2)}, u32[]{:S(2)}) collective-permute-start(bf16[384,1280]{1,0:T(8,128)(2,1)} %collective-permute-done.5), channel_id=1, source_target_pairs={{0,1},{1,0},{2,3},{3,2},{4,5},{5,4},{6,7},{7,6},{8,9},{9,8},{10,11... | collective-permute-start | bytes 2949128 | tf_op jit(solution)/shard_map/ppermute | solution.py:557
  550.4 10.2 %copy-start.8 = (bf16[384,1280]{1,0:T(8,128)(2,1)S(1)}, bf16[384,1280]{1,0:T(8,128)(2,1)}, u32[]{:S(2)}) copy-start(bf16[384,1280]{1,0:T(8,128)(2,1)} %x_ref.1) | copy-start | bytes 2949124
  560.6 2.8 copy-start.9
Sparse Core Ops, SparseCore 0:
  51.9 48.4 all-gather.4
  102.2 48.2 all-gather.6
  204.7 105.3 reduce-scatter.2
  313.4 117.8 reduce-scatter.4
